TPU v7x, 256 devices: a whole 4x4x8 slice. The times are simulated.
256 devices in a mesh: grp: 4 (over y), cp: 64 (over x, z, core).
Axes of the slice: x: 4, y: 4, z: 8, core: 2. Of those that a mesh axis runs over, the one named last changes fastest.
Arguments:
- queries: bfloat16 [131072, 2048], P(('grp', 'cp')), parts along dimension 0, may hold values from -6 to 6
- keys: bfloat16 [131072, 1024], P(('grp', 'cp')), parts along dimension 0, may hold values from -8 to 8
- values: bfloat16 [131072, 1024], P(('grp', 'cp')), parts along dimension 0, may hold values from -6 to 6
- doc_lengths: int32 [1024], P('grp'), parts along dimension 0, may hold values from 1 to 1024, 32768 in all
Outputs:
- attended: bfloat16 [131072, 2048], P(('grp', 'cp')), parts along dimension 0
There are 4 independent parts, one for each index of `grp`. A program takes and returns all parts, laid end to end along the dimension named above; each array names one. Nothing has to cross between parts.
Inputs may be any that keep to these rules, and one draw needn't show every extreme that they name: doc_lengths sums to 32768, and its largest entry is exactly 1024.
All inputs are finite; a program needn't handle non-finite values.
Results may differ from a plain program's by a relative error of at most 0.0031.
Values may be sent and summed in bfloat16 or wider, within the bound.
No kernel may reach another device: no remote copies, remote signals or barrier semaphores. Data moves between devices by JAX's collectives and lax.ppermute only.
A program may use at most 64 MiB of HBM per device.

v0:
```python
import jax
import jax.numpy as jnp
from jax import lax
from jax.sharding import PartitionSpec as P

HQ = 16
HK = 8
DH = 128
REACH = 2


query_scale = 144.0 ** (-0.5)


def shifted(block, axis, distance):
    devices = range(lax.axis_size(axis))
    route = [(i - distance, i) for i in devices if i - distance in devices]
    return lax.ppermute(block, axis, route)


def doc_index(positions, doc_ends):
    return jnp.sum((positions[:, None] >= doc_ends[None, :]).astype(jnp.int32), axis=1)


def on_device(queries, keys, values, doc_lengths):
    tok_rows = queries.shape[0]
    dev_index = lax.axis_index("cp")
    doc_ends = jnp.cumsum(doc_lengths)
    arrived = []
    passed = (keys, values)
    for offset in range(REACH):
        passed = shifted((passed[0], passed[1]), "cp", 1)
        arrived.append(passed)
    ordered = list(reversed(arrived)) + [(keys, values)]
    all_keys = jnp.concatenate([pair[0] for pair in ordered], axis=0)
    all_values = jnp.concatenate([pair[1] for pair in ordered], axis=0)
    first_row = dev_index * tok_rows
    query_pos = first_row + jnp.arange(tok_rows, dtype=jnp.int32)
    key_pos = first_row - REACH * tok_rows + jnp.arange(all_keys.shape[0], dtype=jnp.int32)
    same_doc = doc_index(query_pos, doc_ends)[:, None] == doc_index(key_pos, doc_ends)[None, :]
    visible = same_doc & (key_pos[None, :] <= query_pos[:, None]) & (key_pos[None, :] >= 0)
    groups = HQ // HK
    width = groups * DH

    def one_head(head, result):
        query_part = lax.dynamic_slice_in_dim(queries, head * width, width, 1).reshape(
            tok_rows, groups, DH
        )
        key_part = lax.dynamic_slice_in_dim(all_keys, head * DH, DH, 1)
        value_part = lax.dynamic_slice_in_dim(all_values, head * DH, DH, 1)
        scores = (
            jnp.einsum("tgd,wd->gtw", query_part, key_part, preferred_element_type=jnp.float32)
            * query_scale
        )
        scores = jnp.where(visible[None], scores, -jnp.inf)
        highest = jnp.max(scores, axis=-1, keepdims=True)
        weights = jnp.exp(scores - highest)
        totals = jnp.sum(weights, axis=-1)
        rounded = weights.astype(jnp.bfloat16)
        mixed = jnp.einsum("gtw,wd->tgd", rounded, value_part, preferred_element_type=jnp.float32)
        mixed = mixed / jnp.transpose(totals, (1, 0))[..., None]
        return lax.dynamic_update_slice_in_dim(
            result, mixed.reshape(tok_rows, width).astype(jnp.bfloat16), head * width, 1
        )

    return lax.fori_loop(0, HK, one_head, jnp.zeros_like(queries))


def solution(mesh):
    return jax.shard_map(
        on_device,
        mesh=mesh,
        in_specs=(P(("grp", "cp"), None), P(("grp", "cp"), None), P(("grp", "cp"), None), P("grp")),
        out_specs=P(("grp", "cp"), None),
        check_vma=False,
    )
```

profile of v0, /device:TPU:6, one launch (start us, length us, event | category | flops | bytes accessed | tf_op | source)
XLA Modules:
  0.0 136.8 jit_solution(16757669202044391408)
XLA Ops:
  0.0 1.5 %copy.17 = bf16[512,1024]{0,1:T(8,128)(2,1)S(1)} copy(bf16[512,1024]{1,0:T(8,128)(2,1)} %param.8) | data formatting | bytes 2097152 | tf_op args[2]
  1.5 1.9 %collective-permute-start = (bf16[512,1024]{0,1:T(8,128)(2,1)S(1)}, bf16[512,1024]{0,1:T(8,128)(2,1)S(1)}, u32[]{:S(2)}, u32[]{:S(2)}) collective-permute-start(bf16[512,1024]{0,1:T(8,128)(2,1)S(1)} %copy.17), channel_id=1, source_target_pairs={{0,1},{1,2},{2,3},{3,4},{4,5},{5,6},{6,7},{7,8},{8,9},{9,10},{10,1... | collective-permute-start | bytes 3145736 | tf_op jit(solution)/shard_map/ppermute | solution.py:18
  3.4 3.9 %collective-permute-start.2 = (bf16[512,1024]{1,0:T(8,128)(2,1)}, bf16[512,1024]{1,0:T(8,128)(2,1)S(1)}, u32[]{:S(2)}, u32[]{:S(2)}) collective-permute-start(bf16[512,1024]{1,0:T(8,128)(2,1)} %param.7), channel_id=1, source_target_pairs={{0,1},{1,2},{2,3},{3,4},{4,5},{5,6},{6,7},{7,8},{8,9},{9,10},{10,1... | collective-permute-start | bytes 3145736 | tf_op jit(solution)/shard_map/ppermute | solution.py:18
  7.4 14.1 %collective-permute-done = bf16[512,1024]{0,1:T(8,128)(2,1)S(1)} collective-permute-done((bf16[512,1024]{0,1:T(8,128)(2,1)S(1)}, bf16[512,1024]{0,1:T(8,128)(2,1)S(1)}, u32[]{:S(2)}, u32[]{:S(2)}) %collective-permute-start) | collective-permute-done | bytes 1048608 | tf_op jit(solution)/shard_map/ppermute | solution.py:18
  21.4 1.9 %collective-permute-start.1 = (bf16[512,1024]{0,1:T(8,128)(2,1)S(1)}, bf16[512,1024]{0,1:T(8,128)(2,1)}, u32[]{:S(2)}, u32[]{:S(2)}) collective-permute-start(bf16[512,1024]{0,1:T(8,128)(2,1)S(1)} %collective-permute-done), channel_id=1, source_target_pairs={{0,1},{1,2},{2,3},{3,4},{4,5},{5,6},{6,7},{7,8},{8,9},{9,10},{10,1... | collective-permute-start | bytes 3145736 | tf_op jit(solution)/shard_map/ppermute | solution.py:18
  23.4 9.3 %collective-permute-done.2 = bf16[512,1024]{1,0:T(8,128)(2,1)S(1)} collective-permute-done((bf16[512,1024]{1,0:T(8,128)(2,1)}, bf16[512,1024]{1,0:T(8,128)(2,1)S(1)}, u32[]{:S(2)}, u32[]{:S(2)}) %collective-permute-start.2) | collective-permute-done | bytes 1048608 | tf_op jit(solution)/shard_map/ppermute | solution.py:18
  32.7 1.9 %collective-permute-start.3 = (bf16[512,1024]{1,0:T(8,128)(2,1)S(1)}, bf16[512,1024]{1,0:T(8,128)(2,1)}, u32[]{:S(2)}, u32[]{:S(2)}) collective-permute-start(bf16[512,1024]{1,0:T(8,128)(2,1)S(1)} %collective-permute-done.2), channel_id=1, source_target_pairs={{0,1},{1,2},{2,3},{3,4},{4,5},{5,6},{6,7},{7,8},{8,9},{9,10},{10,1... | collective-permute-start | bytes 3145736 | tf_op jit(solution)/shard_map/ppermute | solution.py:18
  34.6 1.0 reduce-window.9
  35.9 0.2 convert_reduce_fusion.1
  36.1 0.5 convert_reduce_fusion
  36.6 7.4 %collective-permute-done.1 = bf16[512,1024]{0,1:T(8,128)(2,1)} collective-permute-done((bf16[512,1024]{0,1:T(8,128)(2,1)S(1)}, bf16[512,1024]{0,1:T(8,128)(2,1)}, u32[]{:S(2)}, u32[]{:S(2)}) %collective-permute-start.1) | collective-permute-done | bytes 1048608 | tf_op jit(solution)/shard_map/ppermute | solution.py:18
  44.0 2.8 %pad_maximum_fusion = bf16[1536,1024]{0,1:T(8,128)(2,1)} fusion(bf16[512,1024]{0,1:T(8,128)(2,1)S(1)} %copy.17, bf16[512,1024]{0,1:T(8,128)(2,1)S(1)} %collective-permute-done, bf16[512,1024]{0,1:T(8,128)(2,1)} %collective-permute-done.1), kind=kLoop, calls=%fused_computation.23 | loop fusion | flops 9437184 | bytes 6291456 | tf_op jit(solution)/shard_map/concatenate | solution.py:36
  46.8 8.4 %collective-permute-done.3 = bf16[512,1024]{1,0:T(8,128)(2,1)} collective-permute-done((bf16[512,1024]{1,0:T(8,128)(2,1)S(1)}, bf16[512,1024]{1,0:T(8,128)(2,1)}, u32[]{:S(2)}, u32[]{:S(2)}) %collective-permute-start.3) | collective-permute-done | bytes 1048608 | tf_op jit(solution)/shard_map/ppermute | solution.py:18
  55.3 2.9 %pad_maximum_fusion.1 = bf16[1536,1024]{1,0:T(8,128)(2,1)} fusion(bf16[512,1024]{1,0:T(8,128)(2,1)S(1)} %copy-done.1, bf16[512,1024]{1,0:T(8,128)(2,1)S(1)} %collective-permute-done.2, bf16[512,1024]{1,0:T(8,128)(2,1)} %collective-permute-done.3), kind=kLoop, calls=%fused_computation.24 | loop fusion | flops 9437184 | bytes 6291456 | tf_op jit(solution)/shard_map/concatenate | solution.py:35
  58.2 0.2 broadcast_in_dim.45.clone
  58.4 77.0 %while.14 = (s32[]{:T(128)}, bf16[512,2048]{1,0:T(8,128)(2,1)S(1)}, bf16[1536,1024]{0,1:T(8,128)(2,1)}, bf16[1536,1024]{1,0:T(8,128)(2,1)}, bf16[512,2048]{1,0:T...) while((s32[]{:T(128)}, bf16[512,2048]{1,0:T(8,128)(2,1)S(1)}, ...), condition=%wide.region_7.8_spmd.clone, body=%wide.region_4.0_spmd.clone.sunk | while | flops 826013696 | bytes 25466632 | solution.py:66
  58.4 1.0 constant_dynamic-slice_fusion.2
  59.4 0.1 copy.28
  59.6 1.5 %and_and_fusion.2 = pred[512,1536]{0,1:T(8,128)(4,1)S(1)} fusion(s32[512]{0:T(512)S(1)} %get-tuple-element.288, s32[512]{0:T(512)S(1)} %get-tuple-element.287, s32[1536]{0:T(1024)S(1)} %get-tuple-element.289, s32[1536]{0:T(1024)S(1)} %get-tuple-element.286, pred[1536]{0:T(1024)(128)(4,1)S(1)} %get-tuple-element.290), kind=kLoop, calls=%fused_computation.7.clone.1 | loop fusion | flops 3145728 | bytes 804352 | tf_op jit(solution)/shard_map/and | solution.py:41
  61.1 2.3 %fusion.36 = (f32[2,512]{1,0:T(2,128)S(1)}, f32[1536,512,2]{1,0,2:T(8,128)S(1)}) fusion(pred[512,1536]{0,1:T(8,128)(4,1)S(1)} %and_and_fusion.2, bf16[512,2,128]{0,2,1:T(8,128)(2,1)S(1)} %bitcast.57, bf16[1536,1024]{1,0:T(8,128)(2,1)} %get-tuple-element.284, s32[]{:T(128)S(6)} %select_n.50), kind=kOutput, calls=%fused_computation.5.clone.1 | convolution fusion | flops 407370752 | bytes 7737348 | tf_op jit(solution)/shard_map/while/body/eval_jaxpr/tgd,wd->gtw/dot_general | solution.py:52
  63.4 1.4 %fusion.37 = f32[2,512]{1,0:T(2,128)S(1)} fusion(f32[1536,512,2]{1,0,2:T(8,128)S(1)} %get-tuple-element.247, f32[2,512]{1,0:T(2,128)S(1)} %get-tuple-element.248, pred[512,1536]{0,1:T(8,128)(4,1)S(1)} %and_and_fusion.2), kind=kLoop, calls=%fused_computation.3.clone.1 | loop fusion | flops 6290432 | bytes 7086080 | tf_op jit(solution)/shard_map/while/body/eval_jaxpr/reduce_sum | solution.py:58
  64.9 3.0 %fusion.38 = bf16[512,2,128]{0,2,1:T(8,128)(2,1)S(1)} fusion(f32[1536,512,2]{1,0,2:T(8,128)S(1)} %get-tuple-element.247, f32[2,512]{1,0:T(2,128)S(1)} %get-tuple-element.248, pred[512,1536]{0,1:T(8,128)(4,1)S(1)} %and_and_fusion.2, bf16[1536,1024]{0,1:T(8,128)(2,1)} %get-tuple-element.283, s32[]{:T(128)S(6)} %select_n.50, f32[512,2]{0,1:T(2,128)S(1)} %bitcast.58), kind=kOutput, calls=%fused_computation.11.clone.1 | convolution fusion | flops 409206784 | bytes 7741444 | tf_op jit(solution)/shard_map/while/body/eval_jaxpr/gtw,wd->tgd/dot_general | solution.py:60
  68.1 1.0 constant_dynamic-slice_fusion.2
  69.0 0.1 copy.28
  69.2 1.5 %and_and_fusion.2 = pred[512,1536]{0,1:T(8,128)(4,1)S(1)} fusion(s32[512]{0:T(512)S(1)} %get-tuple-element.288, s32[512]{0:T(512)S(1)} %get-tuple-element.287, s32[1536]{0:T(1024)S(1)} %get-tuple-element.289, s32[1536]{0:T(1024)S(1)} %get-tuple-element.286, pred[1536]{0:T(1024)(128)(4,1)S(1)} %get-tuple-element.290), kind=kLoop, calls=%fused_computation.7.clone.1 | loop fusion | flops 3145728 | bytes 804352 | tf_op jit(solution)/shard_map/and | solution.py:41
  70.7 2.3 %fusion.36 = (f32[2,512]{1,0:T(2,128)S(1)}, f32[1536,512,2]{1,0,2:T(8,128)S(1)}) fusion(pred[512,1536]{0,1:T(8,128)(4,1)S(1)} %and_and_fusion.2, bf16[512,2,128]{0,2,1:T(8,128)(2,1)S(1)} %bitcast.57, bf16[1536,1024]{1,0:T(8,128)(2,1)} %get-tuple-element.284, s32[]{:T(128)S(6)} %select_n.50), kind=kOutput, calls=%fused_computation.5.clone.1 | convolution fusion | flops 407370752 | bytes 7737348 | tf_op jit(solution)/shard_map/while/body/eval_jaxpr/tgd,wd->gtw/dot_general | solution.py:52
  73.1 1.4 %fusion.37 = f32[2,512]{1,0:T(2,128)S(1)} fusion(f32[1536,512,2]{1,0,2:T(8,128)S(1)} %get-tuple-element.247, f32[2,512]{1,0:T(2,128)S(1)} %get-tuple-element.248, pred[512,1536]{0,1:T(8,128)(4,1)S(1)} %and_and_fusion.2), kind=kLoop, calls=%fused_computation.3.clone.1 | loop fusion | flops 6290432 | bytes 7086080 | tf_op jit(solution)/shard_map/while/body/eval_jaxpr/reduce_sum | solution.py:58
  74.5 3.0 %fusion.38 = bf16[512,2,128]{0,2,1:T(8,128)(2,1)S(1)} fusion(f32[1536,512,2]{1,0,2:T(8,128)S(1)} %get-tuple-element.247, f32[2,512]{1,0:T(2,128)S(1)} %get-tuple-element.248, pred[512,1536]{0,1:T(8,128)(4,1)S(1)} %and_and_fusion.2, bf16[1536,1024]{0,1:T(8,128)(2,1)} %get-tuple-element.283, s32[]{:T(128)S(6)} %select_n.50, f32[512,2]{0,1:T(2,128)S(1)} %bitcast.58), kind=kOutput, calls=%fused_computation.11.clone.1 | convolution fusion | flops 409206784 | bytes 7741444 | tf_op jit(solution)/shard_map/while/body/eval_jaxpr/gtw,wd->tgd/dot_general | solution.py:60
  77.7 1.0 constant_dynamic-slice_fusion.2
  78.7 0.1 copy.28
  78.8 1.5 %and_and_fusion.2 = pred[512,1536]{0,1:T(8,128)(4,1)S(1)} fusion(s32[512]{0:T(512)S(1)} %get-tuple-element.288, s32[512]{0:T(512)S(1)} %get-tuple-element.287, s32[1536]{0:T(1024)S(1)} %get-tuple-element.289, s32[1536]{0:T(1024)S(1)} %get-tuple-element.286, pred[1536]{0:T(1024)(128)(4,1)S(1)} %get-tuple-element.290), kind=kLoop, calls=%fused_computation.7.clone.1 | loop fusion | flops 3145728 | bytes 804352 | tf_op jit(solution)/shard_map/and | solution.py:41
  80.4 2.3 %fusion.36 = (f32[2,512]{1,0:T(2,128)S(1)}, f32[1536,512,2]{1,0,2:T(8,128)S(1)}) fusion(pred[512,1536]{0,1:T(8,128)(4,1)S(1)} %and_and_fusion.2, bf16[512,2,128]{0,2,1:T(8,128)(2,1)S(1)} %bitcast.57, bf16[1536,1024]{1,0:T(8,128)(2,1)} %get-tuple-element.284, s32[]{:T(128)S(6)} %select_n.50), kind=kOutput, calls=%fused_computation.5.clone.1 | convolution fusion | flops 407370752 | bytes 7737348 | tf_op jit(solution)/shard_map/while/body/eval_jaxpr/tgd,wd->gtw/dot_general | solution.py:52
  82.7 1.4 %fusion.37 = f32[2,512]{1,0:T(2,128)S(1)} fusion(f32[1536,512,2]{1,0,2:T(8,128)S(1)} %get-tuple-element.247, f32[2,512]{1,0:T(2,128)S(1)} %get-tuple-element.248, pred[512,1536]{0,1:T(8,128)(4,1)S(1)} %and_and_fusion.2), kind=kLoop, calls=%fused_computation.3.clone.1 | loop fusion | flops 6290432 | bytes 7086080 | tf_op jit(solution)/shard_map/while/body/eval_jaxpr/reduce_sum | solution.py:58
  84.1 3.0 %fusion.38 = bf16[512,2,128]{0,2,1:T(8,128)(2,1)S(1)} fusion(f32[1536,512,2]{1,0,2:T(8,128)S(1)} %get-tuple-element.247, f32[2,512]{1,0:T(2,128)S(1)} %get-tuple-element.248, pred[512,1536]{0,1:T(8,128)(4,1)S(1)} %and_and_fusion.2, bf16[1536,1024]{0,1:T(8,128)(2,1)} %get-tuple-element.283, s32[]{:T(128)S(6)} %select_n.50, f32[512,2]{0,1:T(2,128)S(1)} %bitcast.58), kind=kOutput, calls=%fused_computation.11.clone.1 | convolution fusion | flops 409206784 | bytes 7741444 | tf_op jit(solution)/shard_map/while/body/eval_jaxpr/gtw,wd->tgd/dot_general | solution.py:60
  87.3 1.0 constant_dynamic-slice_fusion.2
  88.3 0.1 copy.28
  88.4 1.5 %and_and_fusion.2 = pred[512,1536]{0,1:T(8,128)(4,1)S(1)} fusion(s32[512]{0:T(512)S(1)} %get-tuple-element.288, s32[512]{0:T(512)S(1)} %get-tuple-element.287, s32[1536]{0:T(1024)S(1)} %get-tuple-element.289, s32[1536]{0:T(1024)S(1)} %get-tuple-element.286, pred[1536]{0:T(1024)(128)(4,1)S(1)} %get-tuple-element.290), kind=kLoop, calls=%fused_computation.7.clone.1 | loop fusion | flops 3145728 | bytes 804352 | tf_op jit(solution)/shard_map/and | solution.py:41
  90.0 2.3 %fusion.36 = (f32[2,512]{1,0:T(2,128)S(1)}, f32[1536,512,2]{1,0,2:T(8,128)S(1)}) fusion(pred[512,1536]{0,1:T(8,128)(4,1)S(1)} %and_and_fusion.2, bf16[512,2,128]{0,2,1:T(8,128)(2,1)S(1)} %bitcast.57, bf16[1536,1024]{1,0:T(8,128)(2,1)} %get-tuple-element.284, s32[]{:T(128)S(6)} %select_n.50), kind=kOutput, calls=%fused_computation.5.clone.1 | convolution fusion | flops 407370752 | bytes 7737348 | tf_op jit(solution)/shard_map/while/body/eval_jaxpr/tgd,wd->gtw/dot_general | solution.py:52
  92.3 1.4 %fusion.37 = f32[2,512]{1,0:T(2,128)S(1)} fusion(f32[1536,512,2]{1,0,2:T(8,128)S(1)} %get-tuple-element.247, f32[2,512]{1,0:T(2,128)S(1)} %get-tuple-element.248, pred[512,1536]{0,1:T(8,128)(4,1)S(1)} %and_and_fusion.2), kind=kLoop, calls=%fused_computation.3.clone.1 | loop fusion | flops 6290432 | bytes 7086080 | tf_op jit(solution)/shard_map/while/body/eval_jaxpr/reduce_sum | solution.py:58
  93.8 3.0 %fusion.38 = bf16[512,2,128]{0,2,1:T(8,128)(2,1)S(1)} fusion(f32[1536,512,2]{1,0,2:T(8,128)S(1)} %get-tuple-element.247, f32[2,512]{1,0:T(2,128)S(1)} %get-tuple-element.248, pred[512,1536]{0,1:T(8,128)(4,1)S(1)} %and_and_fusion.2, bf16[1536,1024]{0,1:T(8,128)(2,1)} %get-tuple-element.283, s32[]{:T(128)S(6)} %select_n.50, f32[512,2]{0,1:T(2,128)S(1)} %bitcast.58), kind=kOutput, calls=%fused_computation.11.clone.1 | convolution fusion | flops 409206784 | bytes 7741444 | tf_op jit(solution)/shard_map/while/body/eval_jaxpr/gtw,wd->tgd/dot_general | solution.py:60
  96.9 1.0 constant_dynamic-slice_fusion.2
  97.9 0.1 copy.28
  98.1 1.5 %and_and_fusion.2 = pred[512,1536]{0,1:T(8,128)(4,1)S(1)} fusion(s32[512]{0:T(512)S(1)} %get-tuple-element.288, s32[512]{0:T(512)S(1)} %get-tuple-element.287, s32[1536]{0:T(1024)S(1)} %get-tuple-element.289, s32[1536]{0:T(1024)S(1)} %get-tuple-element.286, pred[1536]{0:T(1024)(128)(4,1)S(1)} %get-tuple-element.290), kind=kLoop, calls=%fused_computation.7.clone.1 | loop fusion | flops 3145728 | bytes 804352 | tf_op jit(solution)/shard_map/and | solution.py:41
  99.6 2.3 %fusion.36 = (f32[2,512]{1,0:T(2,128)S(1)}, f32[1536,512,2]{1,0,2:T(8,128)S(1)}) fusion(pred[512,1536]{0,1:T(8,128)(4,1)S(1)} %and_and_fusion.2, bf16[512,2,128]{0,2,1:T(8,128)(2,1)S(1)} %bitcast.57, bf16[1536,1024]{1,0:T(8,128)(2,1)} %get-tuple-element.284, s32[]{:T(128)S(6)} %select_n.50), kind=kOutput, calls=%fused_computation.5.clone.1 | convolution fusion | flops 407370752 | bytes 7737348 | tf_op jit(solution)/shard_map/while/body/eval_jaxpr/tgd,wd->gtw/dot_general | solution.py:52
  101.9 1.4 %fusion.37 = f32[2,512]{1,0:T(2,128)S(1)} fusion(f32[1536,512,2]{1,0,2:T(8,128)S(1)} %get-tuple-element.247, f32[2,512]{1,0:T(2,128)S(1)} %get-tuple-element.248, pred[512,1536]{0,1:T(8,128)(4,1)S(1)} %and_and_fusion.2), kind=kLoop, calls=%fused_computation.3.clone.1 | loop fusion | flops 6290432 | bytes 7086080 | tf_op jit(solution)/shard_map/while/body/eval_jaxpr/reduce_sum | solution.py:58
  103.4 3.0 %fusion.38 = bf16[512,2,128]{0,2,1:T(8,128)(2,1)S(1)} fusion(f32[1536,512,2]{1,0,2:T(8,128)S(1)} %get-tuple-element.247, f32[2,512]{1,0:T(2,128)S(1)} %get-tuple-element.248, pred[512,1536]{0,1:T(8,128)(4,1)S(1)} %and_and_fusion.2, bf16[1536,1024]{0,1:T(8,128)(2,1)} %get-tuple-element.283, s32[]{:T(128)S(6)} %select_n.50, f32[512,2]{0,1:T(2,128)S(1)} %bitcast.58), kind=kOutput, calls=%fused_computation.11.clone.1 | convolution fusion | flops 409206784 | bytes 7741444 | tf_op jit(solution)/shard_map/while/body/eval_jaxpr/gtw,wd->tgd/dot_general | solution.py:60
  106.6 1.0 constant_dynamic-slice_fusion.2
  107.5 0.1 copy.28
  107.7 1.5 %and_and_fusion.2 = pred[512,1536]{0,1:T(8,128)(4,1)S(1)} fusion(s32[512]{0:T(512)S(1)} %get-tuple-element.288, s32[512]{0:T(512)S(1)} %get-tuple-element.287, s32[1536]{0:T(1024)S(1)} %get-tuple-element.289, s32[1536]{0:T(1024)S(1)} %get-tuple-element.286, pred[1536]{0:T(1024)(128)(4,1)S(1)} %get-tuple-element.290), kind=kLoop, calls=%fused_computation.7.clone.1 | loop fusion | flops 3145728 | bytes 804352 | tf_op jit(solution)/shard_map/and | solution.py:41
  109.2 2.3 %fusion.36 = (f32[2,512]{1,0:T(2,128)S(1)}, f32[1536,512,2]{1,0,2:T(8,128)S(1)}) fusion(pred[512,1536]{0,1:T(8,128)(4,1)S(1)} %and_and_fusion.2, bf16[512,2,128]{0,2,1:T(8,128)(2,1)S(1)} %bitcast.57, bf16[1536,1024]{1,0:T(8,128)(2,1)} %get-tuple-element.284, s32[]{:T(128)S(6)} %select_n.50), kind=kOutput, calls=%fused_computation.5.clone.1 | convolution fusion | flops 407370752 | bytes 7737348 | tf_op jit(solution)/shard_map/while/body/eval_jaxpr/tgd,wd->gtw/dot_general | solution.py:52
  111.6 1.4 %fusion.37 = f32[2,512]{1,0:T(2,128)S(1)} fusion(f32[1536,512,2]{1,0,2:T(8,128)S(1)} %get-tuple-element.247, f32[2,512]{1,0:T(2,128)S(1)} %get-tuple-element.248, pred[512,1536]{0,1:T(8,128)(4,1)S(1)} %and_and_fusion.2), kind=kLoop, calls=%fused_computation.3.clone.1 | loop fusion | flops 6290432 | bytes 7086080 | tf_op jit(solution)/shard_map/while/body/eval_jaxpr/reduce_sum | solution.py:58
  113.0 3.0 %fusion.38 = bf16[512,2,128]{0,2,1:T(8,128)(2,1)S(1)} fusion(f32[1536,512,2]{1,0,2:T(8,128)S(1)} %get-tuple-element.247, f32[2,512]{1,0:T(2,128)S(1)} %get-tuple-element.248, pred[512,1536]{0,1:T(8,128)(4,1)S(1)} %and_and_fusion.2, bf16[1536,1024]{0,1:T(8,128)(2,1)} %get-tuple-element.283, s32[]{:T(128)S(6)} %select_n.50, f32[512,2]{0,1:T(2,128)S(1)} %bitcast.58), kind=kOutput, calls=%fused_computation.11.clone.1 | convolution fusion | flops 409206784 | bytes 7741444 | tf_op jit(solution)/shard_map/while/body/eval_jaxpr/gtw,wd->tgd/dot_general | solution.py:60
  116.2 1.0 constant_dynamic-slice_fusion.2
  117.2 0.1 copy.28
  117.3 1.5 %and_and_fusion.2 = pred[512,1536]{0,1:T(8,128)(4,1)S(1)} fusion(s32[512]{0:T(512)S(1)} %get-tuple-element.288, s32[512]{0:T(512)S(1)} %get-tuple-element.287, s32[1536]{0:T(1024)S(1)} %get-tuple-element.289, s32[1536]{0:T(1024)S(1)} %get-tuple-element.286, pred[1536]{0:T(1024)(128)(4,1)S(1)} %get-tuple-element.290), kind=kLoop, calls=%fused_computation.7.clone.1 | loop fusion | flops 3145728 | bytes 804352 | tf_op jit(solution)/shard_map/and | solution.py:41
  118.9 2.3 %fusion.36 = (f32[2,512]{1,0:T(2,128)S(1)}, f32[1536,512,2]{1,0,2:T(8,128)S(1)}) fusion(pred[512,1536]{0,1:T(8,128)(4,1)S(1)} %and_and_fusion.2, bf16[512,2,128]{0,2,1:T(8,128)(2,1)S(1)} %bitcast.57, bf16[1536,1024]{1,0:T(8,128)(2,1)} %get-tuple-element.284, s32[]{:T(128)S(6)} %select_n.50), kind=kOutput, calls=%fused_computation.5.clone.1 | convolution fusion | flops 407370752 | bytes 7737348 | tf_op jit(solution)/shard_map/while/body/eval_jaxpr/tgd,wd->gtw/dot_general | solution.py:52
  121.2 1.4 %fusion.37 = f32[2,512]{1,0:T(2,128)S(1)} fusion(f32[1536,512,2]{1,0,2:T(8,128)S(1)} %get-tuple-element.247, f32[2,512]{1,0:T(2,128)S(1)} %get-tuple-element.248, pred[512,1536]{0,1:T(8,128)(4,1)S(1)} %and_and_fusion.2), kind=kLoop, calls=%fused_computation.3.clone.1 | loop fusion | flops 6290432 | bytes 7086080 | tf_op jit(solution)/shard_map/while/body/eval_jaxpr/reduce_sum | solution.py:58
  122.6 3.0 %fusion.38 = bf16[512,2,128]{0,2,1:T(8,128)(2,1)S(1)} fusion(f32[1536,512,2]{1,0,2:T(8,128)S(1)} %get-tuple-element.247, f32[2,512]{1,0:T(2,128)S(1)} %get-tuple-element.248, pred[512,1536]{0,1:T(8,128)(4,1)S(1)} %and_and_fusion.2, bf16[1536,1024]{0,1:T(8,128)(2,1)} %get-tuple-element.283, s32[]{:T(128)S(6)} %select_n.50, f32[512,2]{0,1:T(2,128)S(1)} %bitcast.58), kind=kOutput, calls=%fused_computation.11.clone.1 | convolution fusion | flops 409206784 | bytes 7741444 | tf_op jit(solution)/shard_map/while/body/eval_jaxpr/gtw,wd->tgd/dot_general | solution.py:60
  125.8 1.0 constant_dynamic-slice_fusion.2
  126.9 1.5 %and_and_fusion.2 = pred[512,1536]{0,1:T(8,128)(4,1)S(1)} fusion(s32[512]{0:T(512)S(1)} %get-tuple-element.288, s32[512]{0:T(512)S(1)} %get-tuple-element.287, s32[1536]{0:T(1024)S(1)} %get-tuple-element.289, s32[1536]{0:T(1024)S(1)} %get-tuple-element.286, pred[1536]{0:T(1024)(128)(4,1)S(1)} %get-tuple-element.290), kind=kLoop, calls=%fused_computation.7.clone.1 | loop fusion | flops 3145728 | bytes 804352 | tf_op jit(solution)/shard_map/and | solution.py:41
  128.5 2.3 %fusion.36 = (f32[2,512]{1,0:T(2,128)S(1)}, f32[1536,512,2]{1,0,2:T(8,128)S(1)}) fusion(pred[512,1536]{0,1:T(8,128)(4,1)S(1)} %and_and_fusion.2, bf16[512,2,128]{0,2,1:T(8,128)(2,1)S(1)} %bitcast.57, bf16[1536,1024]{1,0:T(8,128)(2,1)} %get-tuple-element.284, s32[]{:T(128)S(6)} %select_n.50), kind=kOutput, calls=%fused_computation.5.clone.1 | convolution fusion | flops 407370752 | bytes 7737348 | tf_op jit(solution)/shard_map/while/body/eval_jaxpr/tgd,wd->gtw/dot_general | solution.py:52
  130.8 1.4 %fusion.37 = f32[2,512]{1,0:T(2,128)S(1)} fusion(f32[1536,512,2]{1,0,2:T(8,128)S(1)} %get-tuple-element.247, f32[2,512]{1,0:T(2,128)S(1)} %get-tuple-element.248, pred[512,1536]{0,1:T(8,128)(4,1)S(1)} %and_and_fusion.2), kind=kLoop, calls=%fused_computation.3.clone.1 | loop fusion | flops 6290432 | bytes 7086080 | tf_op jit(solution)/shard_map/while/body/eval_jaxpr/reduce_sum | solution.py:58
  132.3 3.0 %fusion.38 = bf16[512,2,128]{0,2,1:T(8,128)(2,1)S(1)} fusion(f32[1536,512,2]{1,0,2:T(8,128)S(1)} %get-tuple-element.247, f32[2,512]{1,0:T(2,128)S(1)} %get-tuple-element.248, pred[512,1536]{0,1:T(8,128)(4,1)S(1)} %and_and_fusion.2, bf16[1536,1024]{0,1:T(8,128)(2,1)} %get-tuple-element.283, s32[]{:T(128)S(6)} %select_n.50, f32[512,2]{0,1:T(2,128)S(1)} %bitcast.58), kind=kOutput, calls=%fused_computation.11.clone.1 | convolution fusion | flops 409206784 | bytes 7741444 | tf_op jit(solution)/shard_map/while/body/eval_jaxpr/gtw,wd->tgd/dot_general | solution.py:60
  135.4 1.3 copy-done
  (27 shorter events, 1.7 us)
Async XLA Ops:
  1.5 19.9 %collective-permute-start = (bf16[512,1024]{0,1:T(8,128)(2,1)S(1)}, bf16[512,1024]{0,1:T(8,128)(2,1)S(1)}, u32[]{:S(2)}, u32[]{:S(2)}) collective-permute-start(bf16[512,1024]{0,1:T(8,128)(2,1)S(1)} %copy.17), channel_id=1, source_target_pairs={{0,1},{1,2},{2,3},{3,4},{4,5},{5,6},{6,7},{7,8},{8,9},{9,10},{10,1... | collective-permute-start | bytes 3145736 | tf_op jit(solution)/shard_map/ppermute | solution.py:18
  3.4 29.3 %collective-permute-start.2 = (bf16[512,1024]{1,0:T(8,128)(2,1)}, bf16[512,1024]{1,0:T(8,128)(2,1)S(1)}, u32[]{:S(2)}, u32[]{:S(2)}) collective-permute-start(bf16[512,1024]{1,0:T(8,128)(2,1)} %param.7), channel_id=1, source_target_pairs={{0,1},{1,2},{2,3},{3,4},{4,5},{5,6},{6,7},{7,8},{8,9},{9,10},{10,1... | collective-permute-start | bytes 3145736 | tf_op jit(solution)/shard_map/ppermute | solution.py:18
  21.4 22.6 %collective-permute-start.1 = (bf16[512,1024]{0,1:T(8,128)(2,1)S(1)}, bf16[512,1024]{0,1:T(8,128)(2,1)}, u32[]{:S(2)}, u32[]{:S(2)}) collective-permute-start(bf16[512,1024]{0,1:T(8,128)(2,1)S(1)} %collective-permute-done), channel_id=1, source_target_pairs={{0,1},{1,2},{2,3},{3,4},{4,5},{5,6},{6,7},{7,8},{8,9},{9,10},{10,1... | collective-permute-start | bytes 3145736 | tf_op jit(solution)/shard_map/ppermute | solution.py:18
  32.7 22.6 %collective-permute-start.3 = (bf16[512,1024]{1,0:T(8,128)(2,1)S(1)}, bf16[512,1024]{1,0:T(8,128)(2,1)}, u32[]{:S(2)}, u32[]{:S(2)}) collective-permute-start(bf16[512,1024]{1,0:T(8,128)(2,1)S(1)} %collective-permute-done.2), channel_id=1, source_target_pairs={{0,1},{1,2},{2,3},{3,4},{4,5},{5,6},{6,7},{7,8},{8,9},{9,10},{10,1... | collective-permute-start | bytes 3145736 | tf_op jit(solution)/shard_map/ppermute | solution.py:18
  36.6 18.6 %copy-start.1 = (bf16[512,1024]{1,0:T(8,128)(2,1)S(1)}, bf16[512,1024]{1,0:T(8,128)(2,1)}, u32[]{:S(2)}) copy-start(bf16[512,1024]{1,0:T(8,128)(2,1)} %param.7) | copy-start | bytes 3145732
  135.4 1.3 copy-start
where the time goes:
time: 138 us; the launch traced here: 137 us
  matrix products  42.5 us (31%)
  waiting for transfers between devices  39.2 us (28%)
  other arithmetic  31.3 us (23%)
  local copies, waits for them, and re-layouts  13.4 us (10%)
  starting transfers between devices  9.67 us (7%)
    ppermute x4, waiting for transfers between devices, shifted(): return lax.ppermute(block, axis, route)  39.2 us
    dot_general x8, matrix products, one_head(): jnp.einsum('gtw,wd->tgd', rounded, value_part, preferred_element_type=jnp...  23.9 us
    dot_general x8, matrix products, one_head(): jnp.einsum('tgd,wd->gtw', query_part, key_part, preferred_element_type=jn...  18.6 us
    and x8, other arithmetic, on_device(): same_doc & (key_pos[None, :] <= query_pos[:, None])  12.2 us
    reduce_sum x8, other arithmetic, one_head(): totals = jnp.sum(weights, axis=-1)  11.5 us
    ppermute x4, starting transfers between devices, shifted(): return lax.ppermute(block, axis, route)  9.67 us
    dynamic_slice x16, local copies, waits for them, and re-layouts, one_head(): lax.dynamic_slice_in_dim(queries, head * width, width, 1)  8.91 us
    concatenate x1, other arithmetic, on_device(): all_keys = jnp.concatenate([pair[0] for pair in ordered], axis=0)  2.91 us
  transfers between devices with their start and end apart: 4, of which 4 were waited for; matrix products, arithmetic and copies ran while one was open for 4% of the time, Pallas kernels for 0%

commit v1 on v0

v1 whole, which is shorter than its diff:
```python
import functools
import math

import jax
import jax.numpy as jnp
from jax import lax
from jax.experimental import pallas as pl
from jax.experimental.pallas import tpu as pltpu
from jax.sharding import PartitionSpec as P


HQ = 16
HK = 8
DH = 128
GROUPS = HQ // HK
WIDTH = GROUPS * DH
BQ = 128
HIDDEN = -1e30
RATE = math.log2(math.e) * 144.0 ** -0.5
START_LANE = 2 * HQ
VMEM = 24 << 20
INTERPRET = False


def document_ends(lengths):
    docs = lengths.shape[1]
    sub = lax.broadcasted_iota(jnp.int32, (docs, docs), 0)
    lane = lax.broadcasted_iota(jnp.int32, (docs, docs), 1)
    rows = jnp.broadcast_to(lengths.astype(jnp.float32), (docs, docs))
    column = jnp.sum(jnp.where(sub == lane, rows, 0.0), axis=1, keepdims=True)
    return jnp.sum(jnp.where(sub <= lane, column, 0.0), axis=0, keepdims=True)


def lane_column(table, lane):
    return table[:, lane : lane + 1]


def head_pair(ref, head):
    both = ref[:, head * WIDTH : (head + 1) * WIDTH]
    return jnp.concatenate([both[:, :DH], both[:, DH:]], axis=0)


def block_attention(queries, keys, values, bias, highest=None):
    rows = bias.shape[0]
    scores = lax.dot_general(queries, keys, (((1,), (1,)), ((), ())), preferred_element_type=jnp.float32)
    scores = scores.reshape(GROUPS, rows, -1) + bias[None]
    top = jnp.max(scores, axis=-1, keepdims=True)
    if highest is not None:
        top = jnp.maximum(top, highest)
    weights = jnp.exp2((scores - top) * RATE)
    totals = jnp.sum(weights, axis=-1, keepdims=True)
    rounded = weights.astype(jnp.bfloat16).reshape(GROUPS * rows, -1)
    mixed = lax.dot_general(rounded, values, (((1,), (0,)), ((), ())), preferred_element_type=jnp.float32)
    return mixed.reshape(GROUPS, rows, DH), top, totals


def own_kernel(first_ref, len_ref, q_ref, k_ref, v_ref, acc_ref, state_ref, ends_ref):
    block = pl.program_id(0)

    @pl.when(block == 0)
    def _():
        ends_ref[...] = document_ends(len_ref[...])

    ends = ends_ref[...]
    keys = k_ref.shape[0]
    first = first_ref[0].astype(jnp.float32)
    at = (block * BQ).astype(jnp.float32)
    row = lax.broadcasted_iota(jnp.int32, (BQ, 1), 0).astype(jnp.float32) + at
    start = jnp.max(jnp.where(ends <= row + first, ends, 0.0), axis=1, keepdims=True)
    col = lax.broadcasted_iota(jnp.int32, (BQ, keys), 1).astype(jnp.float32)
    bias = jnp.where((col >= start - first) & (col <= row), 0.0, HIDDEN)
    lane = lax.broadcasted_iota(jnp.int32, (BQ, 128), 1)
    state = jnp.broadcast_to(start, (BQ, 128))
    for head in range(HK):
        mixed, top, totals = block_attention(
            head_pair(q_ref, head), k_ref[:, head * DH : (head + 1) * DH], v_ref[:, head * DH : (head + 1) * DH], bias
        )
        for g in range(GROUPS):
            h = head * GROUPS + g
            acc_ref[:, h * DH : (h + 1) * DH] = mixed[g]
            state = jnp.where(lane == h, top[g], state)
            state = jnp.where(lane == HQ + h, totals[g], state)
    state_ref[...] = state


def more_kernel(last, base_ref, q_ref, k_ref, v_ref, acc_ref, state_ref, out_ref, *out_state):
    keys = k_ref.shape[0]
    base = base_ref[0].astype(jnp.float32)
    state = state_ref[...]
    start = lane_column(state, START_LANE)
    needed = jnp.min(start) < base + keys

    @pl.when(jnp.logical_not(needed))
    def _():
        for h in range(HQ):
            part = acc_ref[:, h * DH : (h + 1) * DH]
            if last:
                part = (part * (1.0 / lane_column(state, HQ + h))).astype(out_ref.dtype)
            out_ref[:, h * DH : (h + 1) * DH] = part
        if not last:
            out_state[0][...] = state

    @pl.when(needed)
    def _():
        col = lax.broadcasted_iota(jnp.int32, (BQ, keys), 1).astype(jnp.float32)
        bias = jnp.where(col >= start - base, 0.0, HIDDEN)
        lane = lax.broadcasted_iota(jnp.int32, (BQ, 128), 1)
        new = state
        for head in range(HK):
            heads = [head * GROUPS + g for g in range(GROUPS)]
            before = jnp.stack([lane_column(state, h) for h in heads])
            mixed, top, totals = block_attention(
                head_pair(q_ref, head), k_ref[:, head * DH : (head + 1) * DH], v_ref[:, head * DH : (head + 1) * DH], bias, before
            )
            keep = jnp.exp2((before - top) * RATE)
            for g, h in enumerate(heads):
                total = totals[g] + keep[g] * lane_column(state, HQ + h)
                part = mixed[g] + keep[g] * acc_ref[:, h * DH : (h + 1) * DH]
                if last:
                    part = (part * (1.0 / total)).astype(out_ref.dtype)
                else:
                    new = jnp.where(lane == h, top[g], new)
                    new = jnp.where(lane == HQ + h, total, new)
                out_ref[:, h * DH : (h + 1) * DH] = part
        if not last:
            out_state[0][...] = new


def whole():
    return pl.BlockSpec(memory_space=pltpu.VMEM)


def rows_of(width):
    return pl.BlockSpec((BQ, width), lambda i: (i, 0))


SMEM = pl.BlockSpec(memory_space=pltpu.SMEM)


def cost(rows, keys):
    flops = 4 * rows * keys * HQ * DH
    return pl.CostEstimate(flops=flops, bytes_accessed=rows * HQ * DH * 8, transcendentals=rows * keys * HQ)


def own_stage(first, lengths, queries, keys, values):
    rows = queries.shape[0]
    return pl.pallas_call(
        own_kernel,
        grid=(rows // BQ,),
        in_specs=[SMEM, whole(), rows_of(HQ * DH), whole(), whole()],
        out_specs=[rows_of(HQ * DH), rows_of(128)],
        out_shape=[jax.ShapeDtypeStruct((rows, HQ * DH), jnp.float32), jax.ShapeDtypeStruct((rows, 128), jnp.float32)],
        scratch_shapes=[pltpu.VMEM(lengths.shape, jnp.float32)],
        cost_estimate=cost(rows, keys.shape[0]),
        compiler_params=pltpu.CompilerParams(vmem_limit_bytes=VMEM),
        name="own_shard",
        interpret=INTERPRET,
    )(first, lengths, queries, keys, values)


def more_stage(base, queries, keys, values, acc, state, last):
    rows = queries.shape[0]
    out_specs = [rows_of(HQ * DH)] + ([] if last else [rows_of(128)])
    out_shape = [jax.ShapeDtypeStruct((rows, HQ * DH), jnp.bfloat16 if last else jnp.float32)]
    if not last:
        out_shape.append(jax.ShapeDtypeStruct((rows, 128), jnp.float32))
    return pl.pallas_call(
        functools.partial(more_kernel, last),
        grid=(rows // BQ,),
        in_specs=[SMEM, rows_of(HQ * DH), whole(), whole(), rows_of(HQ * DH), rows_of(128)],
        out_specs=out_specs,
        out_shape=out_shape,
        cost_estimate=cost(rows, keys.shape[0]),
        compiler_params=pltpu.CompilerParams(vmem_limit_bytes=VMEM),
        name="last_shard" if last else "next_shard",
        interpret=INTERPRET,
    )(base, queries, keys, values, acc, state)


def on_device(queries, keys, values, doc_lengths):
    rows = queries.shape[0]
    count = lax.axis_size("cp")
    first = lax.axis_index("cp").astype(jnp.int32) * rows
    onward = [(i, i + 1) for i in range(count - 1)]
    one_k = lax.ppermute(keys, "cp", onward)
    one_v = lax.ppermute(values, "cp", onward)
    two_k = lax.ppermute(one_k, "cp", onward)
    two_v = lax.ppermute(one_v, "cp", onward)
    lengths = doc_lengths.reshape(1, -1)
    acc, state = own_stage(first.reshape(1), lengths, queries, keys, values)
    acc, state = more_stage((first - rows).reshape(1), queries, one_k, one_v, acc, state, False)
    (out,) = more_stage((first - 2 * rows).reshape(1), queries, two_k, two_v, acc, state, True)
    return out


def solution(mesh):
    return jax.shard_map(
        on_device,
        mesh=mesh,
        in_specs=(P(("grp", "cp"), None), P(("grp", "cp"), None), P(("grp", "cp"), None), P("grp")),
        out_specs=P(("grp", "cp"), None),
        check_vma=False,
    )
```

time: 138 us -> 79.6 us (0.58)
  the two profiles are of different devices: /device:TPU:6 before, /device:TPU:20 now
where the time goes in v1:
time: 79.6 us; the launch traced here: 79.3 us
  Pallas kernels  41.5 us (52%)
  waiting for transfers between devices  23.3 us (29%)
  starting transfers between devices  9.66 us (12%)
  local copies, waits for them, and re-layouts  4.71 us (6%)
    pallas_call x2, Pallas kernels, more_stage(): pl.pallas_call(functools.partial(more_kernel, last), grid=(rows // BQ,),...  30.7 us
    ppermute x1, waiting for transfers between devices, on_device(): one_k = lax.ppermute(keys, 'cp', onward)  14 us
    pallas_call x1, Pallas kernels, own_stage(): pl.pallas_call(own_kernel, grid=(rows // BQ,), in_specs=[SMEM, whole(), r...  10.8 us
    ppermute x1, waiting for transfers between devices, on_device(): one_v = lax.ppermute(values, 'cp', onward)  9.32 us
    unnamed x10, local copies, waits for them, and re-layouts  4.71 us
    ppermute x1, starting transfers between devices, on_device(): one_v = lax.ppermute(values, 'cp', onward)  3.93 us
    ppermute x1, starting transfers between devices, on_device(): two_v = lax.ppermute(one_v, 'cp', onward)  1.91 us
    ppermute x1, starting transfers between devices, on_device(): two_k = lax.ppermute(one_k, 'cp', onward)  1.91 us
  transfers between devices with their start and end apart: 4, of which 2 were waited for; matrix products, arithmetic and copies ran while one was open for 0% of the time, Pallas kernels for 32%

profile of v1, /device:TPU:20, one launch (start us, length us, event | category | flops | bytes accessed | tf_op | source)
XLA Modules:
  0.0 79.3 jit_solution(13556104704132005863)
XLA Ops:
  0.0 1.9 %collective-permute-start = (bf16[512,1024]{1,0:T(8,128)(2,1)}, bf16[512,1024]{1,0:T(8,128)(2,1)S(1)}, u32[]{:S(2)}, u32[]{:S(2)}) collective-permute-start(bf16[512,1024]{1,0:T(8,128)(2,1)} %k_ref.1), channel_id=1, source_target_pairs={{0,1},{1,2},{2,3},{3,4},{4,5},{5,6},{6,7},{7,8},{8,9},{9,10},{10,1... | collective-permute-start | bytes 3145736 | tf_op jit(solution)/shard_map/ppermute | solution.py:185
  1.9 3.9 %collective-permute-start.2 = (bf16[512,1024]{1,0:T(8,128)(2,1)}, bf16[512,1024]{1,0:T(8,128)(2,1)S(1)}, u32[]{:S(2)}, u32[]{:S(2)}) collective-permute-start(bf16[512,1024]{1,0:T(8,128)(2,1)} %v_ref.1), channel_id=1, source_target_pairs={{0,1},{1,2},{2,3},{3,4},{4,5},{5,6},{6,7},{7,8},{8,9},{9,10},{10,1... | collective-permute-start | bytes 3145736 | tf_op jit(solution)/shard_map/ppermute | solution.py:186
  5.9 14.0 %collective-permute-done.k_ref = bf16[512,1024]{1,0:T(8,128)(2,1)S(1)} collective-permute-done((bf16[512,1024]{1,0:T(8,128)(2,1)}, bf16[512,1024]{1,0:T(8,128)(2,1)S(1)}, u32[]{:S(2)}, u32[]{:S(2)}) %collective-permute-start) | collective-permute-done | bytes 1048608 | tf_op jit(solution)/shard_map/ppermute | solution.py:185
  19.9 1.9 %collective-permute-start.1 = (bf16[512,1024]{1,0:T(8,128)(2,1)S(1)}, bf16[512,1024]{1,0:T(8,128)(2,1)S(1)}, u32[]{:S(2)}, u32[]{:S(2)}) collective-permute-start(bf16[512,1024]{1,0:T(8,128)(2,1)S(1)} %collective-permute-done.k_ref), channel_id=1, source_target_pairs={{0,1},{1,2},{2,3},{3,4},{4,5},{5,6},{6,7},{7,8},{8,9},{9,10},{10,1... | collective-permute-start | bytes 3145736 | tf_op jit(solution)/shard_map/ppermute | solution.py:187
  21.8 9.3 %collective-permute-done.2.v_ref = bf16[512,1024]{1,0:T(8,128)(2,1)S(1)} collective-permute-done((bf16[512,1024]{1,0:T(8,128)(2,1)}, bf16[512,1024]{1,0:T(8,128)(2,1)S(1)}, u32[]{:S(2)}, u32[]{:S(2)}) %collective-permute-start.2) | collective-permute-done | bytes 1048608 | tf_op jit(solution)/shard_map/ppermute | solution.py:186
  31.1 1.9 %collective-permute-start.3 = (bf16[512,1024]{1,0:T(8,128)(2,1)S(1)}, bf16[512,1024]{1,0:T(8,128)(2,1)}, u32[]{:S(2)}, u32[]{:S(2)}) collective-permute-start(bf16[512,1024]{1,0:T(8,128)(2,1)S(1)} %collective-permute-done.2.v_ref), channel_id=1, source_target_pairs={{0,1},{1,2},{2,3},{3,4},{4,5},{5,6},{6,7},{7,8},{8,9},{9,10},{10,1... | collective-permute-start | bytes 3145736 | tf_op jit(solution)/shard_map/ppermute | solution.py:188
  33.0 0.0 copy-start
  33.0 1.6 %copy-done = bf16[512,2048]{1,0:T(8,128)(2,1)S(1)} copy-done((bf16[512,2048]{1,0:T(8,128)(2,1)S(1)}, bf16[512,2048]{1,0:T(8,128)(2,1)}, u32[]{:S(2)}) %copy-start) | copy-done | bytes 2097176
  34.6 0.0 copy-start.2
  34.6 1.2 %copy-done.2 = bf16[512,1024]{1,0:T(8,128)(2,1)S(1)} copy-done((bf16[512,1024]{1,0:T(8,128)(2,1)S(1)}, bf16[512,1024]{1,0:T(8,128)(2,1)}, u32[]{:S(2)}) %copy-start.2) | copy-done | bytes 1048600
  35.8 0.0 copy-start.3
  35.8 1.2 %copy-done.3 = bf16[512,1024]{1,0:T(8,128)(2,1)S(1)} copy-done((bf16[512,1024]{1,0:T(8,128)(2,1)S(1)}, bf16[512,1024]{1,0:T(8,128)(2,1)}, u32[]{:S(2)}) %copy-start.3) | copy-done | bytes 1048600
  37.1 0.0 copy-start.4
  37.1 0.7 copy-done.4
  37.7 0.0 copy-start.1
  37.7 10.8 %own_shard.1 = (f32[512,2048]{1,0:T(8,128)S(1)}, f32[512,128]{1,0:T(8,128)S(1)}) custom-call(s32[1]{0:T(128)} %bitcast.2.first_ref, s32[1,256]{1,0:T(1,128)S(1)} %bitcast.4, bf16[512,2048]{1,0:T(8,128)(2,1)S(1)} %copy-done, bf16[512,1024]{1,0:T(8,128)(2,1)S(1)} %copy-done.2, bf16[512,1024]{1,0:T(8,128)(2,1)S(1)} %copy-done.3), custom_call_target="tpu_custom_call" | custom-call | flops 2147483648 | bytes 8388608 | tf_op jit(solution)/shard_map/own_shard/pallas_call | solution.py:147
  48.6 0.0 copy-done.1
  48.6 14.2 %next_shard.1 = (f32[512,2048]{1,0:T(8,128)S(1)}, f32[512,128]{1,0:T(8,128)S(1)}) custom-call(s32[1]{0:T(128)} %bitcast.1.base_ref, bf16[512,2048]{1,0:T(8,128)(2,1)S(1)} %copy-done.1, bf16[512,1024]{1,0:T(8,128)(2,1)S(1)} %collective-permute-done.k_ref, bf16[512,1024]{1,0:T(8,128)(2,1)S(1)} %collective-permute-done.2.v_ref, ...), custom_call_target="tpu_custom_call" | custom-call | flops 2147483648 | bytes 8388608 | tf_op jit(solution)/shard_map/next_shard/pallas_call | solution.py:167
  62.8 0.0 collective-permute-done.1.k_ref
  62.8 0.0 collective-permute-done.3.v_ref
  62.8 16.4 %last_shard.1 = bf16[512,2048]{1,0:T(8,128)(2,1)} custom-call(s32[1]{0:T(128)} %bitcast.base_ref, bf16[512,2048]{1,0:T(8,128)(2,1)S(1)} %copy-done.1, bf16[512,1024]{1,0:T(8,128)(2,1)S(1)} %collective-permute-done.1.k_ref, bf16[512,1024]{1,0:T(8,128)(2,1)} %collective-permute-done.3.v_ref, f32[512,2048]{1,0:T(8,128)S(1)} %get-tuple-element.11.acc_ref, ...), custom_call_target="tpu_custom_call" | custom-call | flops 2147483648 | bytes 8388608 | tf_op jit(solution)/shard_map/last_shard/pallas_call | solution.py:167
Async XLA Ops:
  0.0 19.8 %collective-permute-start = (bf16[512,1024]{1,0:T(8,128)(2,1)}, bf16[512,1024]{1,0:T(8,128)(2,1)S(1)}, u32[]{:S(2)}, u32[]{:S(2)}) collective-permute-start(bf16[512,1024]{1,0:T(8,128)(2,1)} %k_ref.1), channel_id=1, source_target_pairs={{0,1},{1,2},{2,3},{3,4},{4,5},{5,6},{6,7},{7,8},{8,9},{9,10},{10,1... | collective-permute-start | bytes 3145736 | tf_op jit(solution)/shard_map/ppermute | solution.py:185
  1.9 29.2 %collective-permute-start.2 = (bf16[512,1024]{1,0:T(8,128)(2,1)}, bf16[512,1024]{1,0:T(8,128)(2,1)S(1)}, u32[]{:S(2)}, u32[]{:S(2)}) collective-permute-start(bf16[512,1024]{1,0:T(8,128)(2,1)} %v_ref.1), channel_id=1, source_target_pairs={{0,1},{1,2},{2,3},{3,4},{4,5},{5,6},{6,7},{7,8},{8,9},{9,10},{10,1... | collective-permute-start | bytes 3145736 | tf_op jit(solution)/shard_map/ppermute | solution.py:186
  19.9 43.0 %collective-permute-start.1 = (bf16[512,1024]{1,0:T(8,128)(2,1)S(1)}, bf16[512,1024]{1,0:T(8,128)(2,1)S(1)}, u32[]{:S(2)}, u32[]{:S(2)}) collective-permute-start(bf16[512,1024]{1,0:T(8,128)(2,1)S(1)} %collective-permute-done.k_ref), channel_id=1, source_target_pairs={{0,1},{1,2},{2,3},{3,4},{4,5},{5,6},{6,7},{7,8},{8,9},{9,10},{10,1... | collective-permute-start | bytes 3145736 | tf_op jit(solution)/shard_map/ppermute | solution.py:187
  31.1 31.7 %collective-permute-start.3 = (bf16[512,1024]{1,0:T(8,128)(2,1)S(1)}, bf16[512,1024]{1,0:T(8,128)(2,1)}, u32[]{:S(2)}, u32[]{:S(2)}) collective-permute-start(bf16[512,1024]{1,0:T(8,128)(2,1)S(1)} %collective-permute-done.2.v_ref), channel_id=1, source_target_pairs={{0,1},{1,2},{2,3},{3,4},{4,5},{5,6},{6,7},{7,8},{8,9},{9,10},{10,1... | collective-permute-start | bytes 3145736 | tf_op jit(solution)/shard_map/ppermute | solution.py:188
  33.0 1.6 %copy-start = (bf16[512,2048]{1,0:T(8,128)(2,1)S(1)}, bf16[512,2048]{1,0:T(8,128)(2,1)}, u32[]{:S(2)}) copy-start(bf16[512,2048]{1,0:T(8,128)(2,1)} %q_ref.5) | copy-start | bytes 6291460
  34.6 1.2 %copy-start.2 = (bf16[512,1024]{1,0:T(8,128)(2,1)S(1)}, bf16[512,1024]{1,0:T(8,128)(2,1)}, u32[]{:S(2)}) copy-start(bf16[512,1024]{1,0:T(8,128)(2,1)} %k_ref.1) | copy-start | bytes 3145732
  35.8 1.2 %copy-start.3 = (bf16[512,1024]{1,0:T(8,128)(2,1)S(1)}, bf16[512,1024]{1,0:T(8,128)(2,1)}, u32[]{:S(2)}) copy-start(bf16[512,1024]{1,0:T(8,128)(2,1)} %v_ref.1) | copy-start | bytes 3145732
  37.1 0.7 copy-start.4
  37.7 10.8 %copy-start.1 = (bf16[512,2048]{1,0:T(8,128)(2,1)S(1)}, bf16[512,2048]{1,0:T(8,128)(2,1)}, u32[]{:S(2)}) copy-start(bf16[512,2048]{1,0:T(8,128)(2,1)} %q_ref.5) | copy-start | bytes 6291460

commit v2 on v1

v2 whole, which is shorter than its diff:
```python
import math

import jax
import jax.numpy as jnp
from jax import lax
from jax.experimental import pallas as pl
from jax.experimental.pallas import tpu as pltpu
from jax.sharding import PartitionSpec as P


HQ = 16
HK = 8
DH = 128
GROUPS = HQ // HK
WIDTH = GROUPS * DH
KV = HK * DH
BQ = 128
HIDDEN = -1e30
RATE = math.log2(math.e) * 144.0 ** -0.5
START = 2 * HQ
PARTS = 3
VMEM = 24 << 20
INTERPRET = False

SLOT = 256


def document_ends(lengths):
    docs = lengths.shape[1]
    sub = lax.broadcasted_iota(jnp.int32, (docs, docs), 0)
    lane = lax.broadcasted_iota(jnp.int32, (docs, docs), 1)
    rows = jnp.broadcast_to(lengths.astype(jnp.float32), (docs, docs))
    column = jnp.sum(jnp.where(sub == lane, rows, 0.0), axis=1, keepdims=True)
    return jnp.sum(jnp.where(sub <= lane, column, 0.0), axis=0, keepdims=True)


def float_iota(shape, axis):
    return lax.broadcasted_iota(jnp.int32, shape, axis).astype(jnp.float32)


def attend(pair, keys, values, bias, before, emit):
    rows = bias.shape[0]

    def score(head):
        return lax.dot_general(pair(head), keys(head), (((1,), (1,)), ((), ())), preferred_element_type=jnp.float32)

    ahead = score(0)
    for head in range(HK):
        scores = ahead
        if head + 1 < HK:
            ahead = score(head + 1)
        scores = scores.reshape(GROUPS, rows, -1) + bias[None]
        top = jnp.max(scores, axis=-1, keepdims=True)
        if before is not None:
            top = jnp.maximum(top, before(head))
        weights = jnp.exp2((scores - top) * RATE)
        rounded = weights.astype(jnp.bfloat16).reshape(GROUPS * rows, -1)
        value = values(head)
        value = jnp.concatenate([value, jnp.ones_like(value)], axis=1)
        mixed = lax.dot_general(rounded, value, (((1,), (0,)), ((), ())), preferred_element_type=jnp.float32)
        mixed = mixed.reshape(GROUPS, rows, 2 * DH)
        for g in range(GROUPS):
            emit(head, g, mixed[g, :, :DH], mixed[g, :, DH:], top[g])


def heads_of(ref, rows=slice(None), at=0):
    return lambda head: ref[rows, at + head * DH : at + (head + 1) * DH]


def pairs_of(ref, rows=slice(None)):
    def pair(head):
        both = ref[rows, head * WIDTH : (head + 1) * WIDTH]
        return jnp.concatenate([both[:, :DH], both[:, DH:]], axis=0)

    return pair


def own_kernel(first_ref, len_ref, q_ref, k_ref, v_ref, acc_ref, state_ref, ends_ref):
    block = pl.program_id(0)

    @pl.when(block == 0)
    def _():
        ends_ref[...] = document_ends(len_ref[...])

    ends = ends_ref[...]
    keys = k_ref.shape[0]
    first = first_ref[0].astype(jnp.float32)
    row = float_iota((BQ, 1), 0) + (block * BQ).astype(jnp.float32)
    start = jnp.max(jnp.where(ends <= row + first, ends, 0.0), axis=1, keepdims=True)
    col = float_iota((BQ, keys), 1)
    bias = jnp.where((col >= start - first) & (col <= row), 0.0, HIDDEN)
    lane = lax.broadcasted_iota(jnp.int32, (BQ, 128), 1)
    state = [jnp.broadcast_to(start, (BQ, 128))]

    def emit(head, g, mixed, total, top):
        h = head * GROUPS + g
        acc_ref[:, h * DH : (h + 1) * DH] = mixed
        state[0] = jnp.where(lane == HQ + h, total, jnp.where(lane == h, top, state[0]))

    attend(pairs_of(q_ref), heads_of(k_ref), heads_of(v_ref), bias, None, emit)
    state_ref[...] = state[0]


def back_kernel(first_ref, len_ref, q_ref, k_ref, v_ref, slot_ref):
    first = first_ref[0]
    here = first.astype(jnp.float32)
    keys = k_ref.shape[0]
    block = pl.program_id(0)

    @pl.when((first // keys) % 2 == 0)
    def _():
        ends = document_ends(len_ref[...])
        edge = here + 2 * keys
        start = jnp.max(jnp.where(ends <= edge, ends, 0.0))
        right = jnp.min(jnp.where(ends > edge, ends, edge + edge)) - edge
        by_keys = here + keys - start <= SLOT

        @pl.when(by_keys)
        def _():
            rows = pl.ds(keys - SLOT + block * BQ, BQ)
            slot_ref[:, :KV] = k_ref[rows, :]
            slot_ref[:, KV : 2 * KV] = v_ref[rows, :]
            slot_ref[:, 2 * KV :] = jnp.zeros((BQ, 128), jnp.bfloat16)

        @pl.when(jnp.logical_not(by_keys))
        def _():
            row = float_iota((BQ, 1), 0) + (block * BQ).astype(jnp.float32)
            col = float_iota((BQ, keys), 1)
            bias = jnp.where((col >= start - here) & (row < right), 0.0, HIDDEN)
            lane = lax.broadcasted_iota(jnp.int32, (BQ, 128), 1)
            level = [jnp.zeros((BQ, 128), jnp.float32)]

            def emit(head, g, mixed, total, top):
                h = head * GROUPS + g
                slot_ref[:, h * DH : (h + 1) * DH] = (mixed * (1.0 / total)).astype(jnp.bfloat16)
                level[0] = jnp.where(lane % HQ == h, top * RATE + jnp.log2(total), level[0])

            attend(pairs_of(q_ref), heads_of(k_ref), heads_of(v_ref), bias, None, emit)
            rest = level[0]
            tail = jnp.zeros((BQ, 128), jnp.float32)
            for part in range(PARTS):
                piece = rest.astype(jnp.bfloat16).astype(jnp.float32)
                tail = jnp.where(lane // HQ == part, piece, tail)
                rest = rest - piece
            slot_ref[:, 2 * KV :] = tail.astype(jnp.bfloat16)


def column(state, lane):
    return state[:, lane : lane + 1]


def old_tops(state):
    return lambda head: jnp.stack([column(state, head * GROUPS + g) for g in range(GROUPS)])


def next_kernel(first_ref, q_ref, k_ref, v_ref, acc_ref, state_ref, out_ref, new_acc_ref, new_state_ref):
    keys = k_ref.shape[0]
    first = first_ref[0].astype(jnp.float32)
    base = first - keys
    state = state_ref[...]
    start = column(state, START)
    lowest = jnp.min(start)

    @pl.when(lowest >= first)
    def _():
        for h in range(HQ):
            cols = slice(h * DH, (h + 1) * DH)
            out_ref[:, cols] = (acc_ref[:, cols] * (1.0 / column(state, HQ + h))).astype(out_ref.dtype)
        new_state_ref[...] = state

    @pl.when(lowest < first)
    def _():
        bias = jnp.where(float_iota((BQ, keys), 1) >= start - base, 0.0, HIDDEN)
        lane = lax.broadcasted_iota(jnp.int32, (BQ, 128), 1)
        new = [state]

        def emit(head, g, mixed, total, top):
            h = head * GROUPS + g
            cols = slice(h * DH, (h + 1) * DH)
            keep = jnp.exp2((column(state, h) - top) * RATE)
            total = total + keep * column(state, HQ + h)
            mixed = mixed + keep * acc_ref[:, cols]
            new_acc_ref[:, cols] = mixed
            new[0] = jnp.where(lane == HQ + h, total, jnp.where(lane == h, top, new[0]))
            out_ref[:, cols] = (mixed * (1.0 / total)).astype(out_ref.dtype)

        attend(pairs_of(q_ref), heads_of(k_ref), heads_of(v_ref), bias, old_tops(state), emit)
        new_state_ref[...] = new[0]


def last_kernel(first_ref, q_ref, slot_ref, k_ref, v_ref, acc_ref, state_ref, prior_ref, out_ref, rows_ref, sem):
    keys = k_ref.shape[0]
    first = first_ref[0].astype(jnp.float32)
    odd = (first_ref[0] // keys) % 2 == 1
    base = first - keys
    blocks = q_ref.shape[0] // BQ
    by_keys = base - jnp.min(state_ref[:8, START : START + 1]) <= SLOT

    def reaches(block):
        return jnp.min(state_ref[pl.ds(block * BQ, 8), START : START + 1]) < base

    def copy(block):
        rows = pl.ds(pl.multiple_of(block * BQ, BQ), BQ)
        return pltpu.make_async_copy(rows_ref.at[rows, :], out_ref.at[rows, :], sem.at[block])

    def merge(block, get_keys, get_values, count, origin):
        rows = pl.ds(pl.multiple_of(block * BQ, BQ), BQ)
        state = state_ref[rows, :]
        start = column(state, START)
        bias = jnp.where(float_iota((BQ, count), 1) >= start - origin, 0.0, HIDDEN)

        def emit(head, g, mixed, total, top):
            h = head * GROUPS + g
            cols = slice(h * DH, (h + 1) * DH)
            keep = jnp.exp2((column(state, h) - top) * RATE)
            total = total + keep * column(state, HQ + h)
            mixed = mixed + keep * acc_ref[rows, cols]
            rows_ref[rows, cols] = (mixed * (1.0 / total)).astype(rows_ref.dtype)

        attend(pairs_of(q_ref, rows), get_keys, get_values, bias, old_tops(state), emit)

    def combine(block):
        rows = pl.ds(pl.multiple_of(block * BQ, BQ), BQ)
        state = state_ref[rows, :]
        tail = slot_ref[rows, 2 * KV :].astype(jnp.float32)
        for h in range(HQ):
            cols = slice(h * DH, (h + 1) * DH)
            there = sum(column(tail, part * HQ + h) for part in reversed(range(PARTS)))
            here = column(state, h) * RATE
            top = jnp.maximum(here, there)
            keep, take = jnp.exp2(here - top), jnp.exp2(there - top)
            scale = 1.0 / (keep * column(state, HQ + h) + take)
            mixed = acc_ref[rows, cols] * (keep * scale) + slot_ref[rows, cols].astype(jnp.float32) * (take * scale)
            rows_ref[rows, cols] = mixed.astype(rows_ref.dtype)

    @pl.loop(0, blocks)
    def _(block):
        needed = reaches(block)

        @pl.when(needed & odd)
        def _():
            merge(block, heads_of(k_ref), heads_of(v_ref), keys, base - keys)

        @pl.when(needed & jnp.logical_not(odd) & by_keys)
        def _():
            merge(block, heads_of(slot_ref), heads_of(slot_ref, at=KV), SLOT, base - SLOT)

        @pl.when(needed & jnp.logical_not(odd) & jnp.logical_not(by_keys) & (block * BQ < SLOT))
        def _():
            combine(block)

        @pl.when(needed)
        def _():
            copy(block).start()

    @pl.loop(0, blocks)
    def _(block):
        @pl.when(reaches(block))
        def _():
            copy(block).wait()


def rows_of(width):
    return pl.BlockSpec((BQ, width), lambda i: (i, 0))


SMEM = pl.BlockSpec(memory_space=pltpu.SMEM)
WHOLE = pl.BlockSpec(memory_space=pltpu.VMEM)
WIDE = HQ * DH


def cost(rows, keys):
    return pl.CostEstimate(
        flops=4 * rows * keys * WIDE, bytes_accessed=rows * WIDE * 8, transcendentals=rows * keys * HQ
    )


PARAMS = pltpu.CompilerParams(vmem_limit_bytes=VMEM)


def f32(*shape):
    return jax.ShapeDtypeStruct(shape, jnp.float32)


def bf16(*shape):
    return jax.ShapeDtypeStruct(shape, jnp.bfloat16)


def own_stage(first, lengths, queries, keys, values):
    rows = queries.shape[0]
    return pl.pallas_call(
        own_kernel,
        grid=(rows // BQ,),
        in_specs=[SMEM, WHOLE, rows_of(WIDE), WHOLE, WHOLE],
        out_specs=[rows_of(WIDE), rows_of(128)],
        out_shape=[f32(rows, WIDE), f32(rows, 128)],
        scratch_shapes=[pltpu.VMEM(lengths.shape, jnp.float32)],
        cost_estimate=cost(rows, keys.shape[0]),
        compiler_params=PARAMS,
        name="own_shard",
        interpret=INTERPRET,
    )(first, lengths, queries, keys, values)


def back_stage(first, lengths, queries, keys, values):
    return pl.pallas_call(
        back_kernel,
        grid=(SLOT // BQ,),
        in_specs=[SMEM, WHOLE, rows_of(WIDE), WHOLE, WHOLE],
        out_specs=rows_of(2 * KV + 128),
        out_shape=bf16(SLOT, 2 * KV + 128),
        cost_estimate=cost(SLOT, keys.shape[0]),
        compiler_params=PARAMS,
        name="back_shard",
        interpret=INTERPRET,
    )(first, lengths, queries, keys, values)


def next_stage(first, queries, keys, values, acc, state):
    rows = queries.shape[0]
    return pl.pallas_call(
        next_kernel,
        grid=(rows // BQ,),
        in_specs=[SMEM, rows_of(WIDE), WHOLE, WHOLE, rows_of(WIDE), rows_of(128)],
        out_specs=[rows_of(WIDE), rows_of(WIDE), rows_of(128)],
        out_shape=[bf16(rows, WIDE), f32(rows, WIDE), f32(rows, 128)],
        cost_estimate=cost(rows, keys.shape[0]),
        compiler_params=PARAMS,
        name="next_shard",
        interpret=INTERPRET,
    )(first, queries, keys, values, acc, state)


def last_stage(first, queries, slot, keys, values, acc, state, prior):
    rows = queries.shape[0]
    return pl.pallas_call(
        last_kernel,
        in_specs=[SMEM, WHOLE, WHOLE, WHOLE, WHOLE, WHOLE, WHOLE, pl.BlockSpec(memory_space=pl.ANY)],
        out_specs=pl.BlockSpec(memory_space=pl.ANY),
        out_shape=bf16(rows, WIDE),
        scratch_shapes=[pltpu.VMEM((rows, WIDE), jnp.bfloat16), pltpu.SemaphoreType.DMA((rows // BQ,))],
        input_output_aliases={7: 0},
        cost_estimate=cost(rows, SLOT),
        compiler_params=PARAMS,
        name="last_shard",
        interpret=INTERPRET,
    )(first, queries, slot, keys, values, acc, state, prior)


def on_device(queries, keys, values, doc_lengths):
    count = lax.axis_size("cp")
    first = (lax.axis_index("cp").astype(jnp.int32) * queries.shape[0]).reshape(1)
    lengths = doc_lengths.reshape(1, -1)
    evens = range(0, count, 2)

    def hop(array, pairs):
        return lax.ppermute(array, "cp", pairs)

    onward = [(i, i + 1) for i in range(count - 1)]
    one_k = hop(keys, onward)
    one_v = hop(values, onward)
    guests = hop(queries[:SLOT], [(i, i - 2) for i in evens if i])
    acc, state = own_stage(first, lengths, queries, keys, values)
    slot = back_stage(first, lengths, guests, keys, values)
    slot = hop(slot, [(i, i + 2) for i in evens if i + 2 < count])
    across = [(i, i + 1) for i in evens]
    two_k = hop(one_k, across)
    two_v = hop(one_v, across)
    out, acc, state_next = next_stage(first, queries, one_k, one_v, acc, state)
    out = last_stage(first, queries, slot, two_k, two_v, acc, state_next, out)
    return out


def solution(mesh):
    return jax.shard_map(
        on_device,
        mesh=mesh,
        in_specs=(P(("grp", "cp"), None), P(("grp", "cp"), None), P(("grp", "cp"), None), P("grp")),
        out_specs=P(("grp", "cp"), None),
        check_vma=False,
    )
```

time: 79.6 us -> 81.9 us (1.029)
  starting transfers between devices: 9.66 us -> 16.4 us
  Pallas kernels: 41.5 us -> 34.9 us
  waiting for transfers between devices: 23.3 us -> 27.6 us
  local copies, waits for them, and re-layouts: 4.71 us -> 2.47 us
    ppermute x4 -> x6, starting transfers between devices: 9.66 us -> 16.4 us  [hop(): return lax.ppermute(array, 'cp', pairs)]
    pallas_call x3 -> x4, Pallas kernels: 41.5 us -> 34.9 us  [the longest x1 14.7 us: next_stage(): pl.pallas_call(next_kernel, grid=(rows // BQ,), in_specs=[SMEM, rows_of(W...]
    unnamed x10 -> x8, local copies, waits for them, and re-layouts: 4.71 us -> 0.01 us
    ppermute x4 -> x6, waiting for transfers between devices: 23.3 us -> 27.6 us  [hop(): return lax.ppermute(array, 'cp', pairs)]
    slice x0 -> x1, local copies, waits for them, and re-layouts: none -> 2.45 us  [on_device(): guests = hop(queries[:SLOT], [(i, i - 2) for i in evens if i])]
  transfers between devices with their start and end apart: 4 -> 6, of which waited for: 2 -> 3; matrix products, arithmetic and copies ran while one was open for 0% -> 0% of each run, Pallas kernels for 32% -> 28%
where the time goes in v2:
time: 81.9 us; the launch traced here: 81.6 us
  Pallas kernels  34.9 us (43%)
  waiting for transfers between devices  27.6 us (34%)
  starting transfers between devices  16.4 us (20%)
  local copies, waits for them, and re-layouts  2.47 us (3%)
    ppermute x6, waiting for transfers between devices, hop(): return lax.ppermute(array, 'cp', pairs)  27.6 us
    ppermute x6, starting transfers between devices, hop(): return lax.ppermute(array, 'cp', pairs)  16.4 us
    pallas_call x1, Pallas kernels, next_stage(): pl.pallas_call(next_kernel, grid=(rows // BQ,), in_specs=[SMEM, rows_of(W...  14.7 us
    pallas_call x1, Pallas kernels, last_stage(): pl.pallas_call(last_kernel, in_specs=[SMEM, WHOLE, WHOLE, WHOLE, WHOLE, W...  12 us
    pallas_call x1, Pallas kernels, own_stage(): pl.pallas_call(own_kernel, grid=(rows // BQ,), in_specs=[SMEM, WHOLE, row...  6.4 us
    slice x1, local copies, waits for them, and re-layouts, on_device(): guests = hop(queries[:SLOT], [(i, i - 2) for i in evens if i])  2.45 us
    pallas_call x1, Pallas kernels, back_stage(): pl.pallas_call(back_kernel, grid=(SLOT // BQ,), in_specs=[SMEM, WHOLE, ro...  1.79 us
  transfers between devices with their start and end apart: 6, of which 3 were waited for; matrix products, arithmetic and copies ran while one was open for 0% of the time, Pallas kernels for 28%

profile of v2, /device:TPU:20, one launch (start us, length us, event | category | flops | bytes accessed | tf_op | source)
XLA Modules:
  0.0 81.6 jit_solution(8606918463933038511)
XLA Ops:
  0.0 0.0 copy-start.1
  0.0 0.0 copy-start.2
  0.0 0.0 copy-start.3
  0.0 2.5 %slice.3 = bf16[256,2048]{1,0:T(8,128)(2,1)} slice(bf16[512,2048]{1,0:T(8,128)(2,1)} %q_ref.5), slice={[0:256], [0:2048]} | slice | bytes 2097152 | tf_op jit(solution)/shard_map/slice | solution.py:362
  2.5 7.7 %collective-permute-start = (bf16[256,2048]{1,0:T(8,128)(2,1)}, bf16[256,2048]{1,0:T(8,128)(2,1)}, u32[]{:S(2)}, u32[]{:S(2)}) collective-permute-start(bf16[256,2048]{1,0:T(8,128)(2,1)} %slice.3), channel_id=1, source_target_pairs={{2,0},{4,2},{6,4},{8,6},{10,8},{12,10},{14,12},{16,14},{18,16},{20... | collective-permute-start | bytes 3145736 | tf_op jit(solution)/shard_map/ppermute | solution.py:357
  10.2 0.0 copy-done.1
  10.2 1.9 %collective-permute-start.2 = (bf16[512,1024]{1,0:T(8,128)(2,1)S(1)}, bf16[512,1024]{1,0:T(8,128)(2,1)S(1)}, u32[]{:S(2)}, u32[]{:S(2)}) collective-permute-start(bf16[512,1024]{1,0:T(8,128)(2,1)S(1)} %copy-done.1), channel_id=1, source_target_pairs={{0,1},{1,2},{2,3},{3,4},{4,5},{5,6},{6,7},{7,8},{8,9},{9,10},{10,1... | collective-permute-start | bytes 3145736 | tf_op jit(solution)/shard_map/ppermute | solution.py:357
  12.1 0.0 copy-done.2
  12.1 1.9 %collective-permute-start.4 = (bf16[512,1024]{1,0:T(8,128)(2,1)S(1)}, bf16[512,1024]{1,0:T(8,128)(2,1)}, u32[]{:S(2)}, u32[]{:S(2)}) collective-permute-start(bf16[512,1024]{1,0:T(8,128)(2,1)S(1)} %copy-done.2), channel_id=1, source_target_pairs={{0,1},{1,2},{2,3},{3,4},{4,5},{5,6},{6,7},{7,8},{8,9},{9,10},{10,1... | collective-permute-start | bytes 3145736 | tf_op jit(solution)/shard_map/ppermute | solution.py:357
  14.1 8.7 %collective-permute-done.q_ref = bf16[256,2048]{1,0:T(8,128)(2,1)} collective-permute-done((bf16[256,2048]{1,0:T(8,128)(2,1)}, bf16[256,2048]{1,0:T(8,128)(2,1)}, u32[]{:S(2)}, u32[]{:S(2)}) %collective-permute-start) | collective-permute-done | bytes 1048608 | tf_op jit(solution)/shard_map/ppermute | solution.py:357
  22.8 0.0 copy-done.3
  22.8 0.0 copy-start
  22.8 1.8 %back_shard.1 = bf16[256,2176]{1,0:T(8,128)(2,1)S(1)} custom-call(s32[1]{0:T(128)} %bitcast.first_ref, s32[1,256]{1,0:T(1,128)S(1)} %bitcast.2, bf16[256,2048]{1,0:T(8,128)(2,1)} %collective-permute-done.q_ref, bf16[512,1024]{1,0:T(8,128)(2,1)S(1)} %copy-done.1, bf16[512,1024]{1,0:T(8,128)(2,1)S(1)} %copy-done.2), custom_call_target="tpu_custom_call" | custom-call | flops 1073741824 | bytes 4194304 | tf_op jit(solution)/shard_map/back_shard/pallas_call | solution.py:306
  24.6 1.9 %collective-permute-start.1 = (bf16[256,2176]{1,0:T(8,128)(2,1)S(1)}, bf16[256,2176]{1,0:T(8,128)(2,1)S(1)}, u32[]{:S(2)}, u32[]{:S(2)}) collective-permute-start(bf16[256,2176]{1,0:T(8,128)(2,1)S(1)} %back_shard.1), channel_id=1, source_target_pairs={{0,2},{2,4},{4,6},{6,8},{8,10},{10,12},{12,14},{14,16},{16,18},{18... | collective-permute-start | bytes 3342344 | tf_op jit(solution)/shard_map/ppermute | solution.py:357
  26.5 1.9 %collective-permute-done.2.k_ref = bf16[512,1024]{1,0:T(8,128)(2,1)S(1)} collective-permute-done((bf16[512,1024]{1,0:T(8,128)(2,1)S(1)}, bf16[512,1024]{1,0:T(8,128)(2,1)S(1)}, u32[]{:S(2)}, u32[]{:S(2)}) %collective-permute-start.2) | collective-permute-done | bytes 1048608 | tf_op jit(solution)/shard_map/ppermute | solution.py:357
  28.4 1.3 %collective-permute-start.3 = (bf16[512,1024]{1,0:T(8,128)(2,1)S(1)}, bf16[512,1024]{1,0:T(8,128)(2,1)S(1)}, u32[]{:S(2)}, u32[]{:S(2)}) collective-permute-start(bf16[512,1024]{1,0:T(8,128)(2,1)S(1)} %collective-permute-done.2.k_ref), channel_id=1, source_target_pairs={{0,1},{2,3},{4,5},{6,7},{8,9},{10,11},{12,13},{14,15},{16,17},{18,... | collective-permute-start | bytes 3145736 | tf_op jit(solution)/shard_map/ppermute | solution.py:357
  29.8 17.0 %collective-permute-done.4.v_ref = bf16[512,1024]{1,0:T(8,128)(2,1)} collective-permute-done((bf16[512,1024]{1,0:T(8,128)(2,1)S(1)}, bf16[512,1024]{1,0:T(8,128)(2,1)}, u32[]{:S(2)}, u32[]{:S(2)}) %collective-permute-start.4) | collective-permute-done | bytes 1048608 | tf_op jit(solution)/shard_map/ppermute | solution.py:357
  46.8 1.5 %collective-permute-start.5 = (bf16[512,1024]{1,0:T(8,128)(2,1)}, bf16[512,1024]{1,0:T(8,128)(2,1)S(1)}, u32[]{:S(2)}, u32[]{:S(2)}) collective-permute-start(bf16[512,1024]{1,0:T(8,128)(2,1)} %collective-permute-done.4.v_ref), channel_id=1, source_target_pairs={{0,1},{2,3},{4,5},{6,7},{8,9},{10,11},{12,13},{14,15},{16,17},{18,... | collective-permute-start | bytes 3145736 | tf_op jit(solution)/shard_map/ppermute | solution.py:357
  48.3 0.0 copy-done
  48.3 6.4 %own_shard.1 = (f32[512,2048]{1,0:T(8,128)S(1)}, f32[512,128]{1,0:T(8,128)S(1)}) custom-call(s32[1]{0:T(128)} %bitcast.first_ref, s32[1,256]{1,0:T(1,128)S(1)} %bitcast.3, bf16[512,2048]{1,0:T(8,128)(2,1)S(1)} %copy-done, bf16[512,1024]{1,0:T(8,128)(2,1)S(1)} %copy-done.1, bf16[512,1024]{1,0:T(8,128)(2,1)S(1)} %copy-done.2), custom_call_target="tpu_custom_call" | custom-call | flops 2147483648 | bytes 8388608 | tf_op jit(solution)/shard_map/own_shard/pallas_call | solution.py:291
  54.8 14.7 %next_shard.1 = (bf16[512,2048]{1,0:T(8,128)(2,1)}, f32[512,2048]{1,0:T(8,128)S(1)}, f32[512,128]{1,0:T(8,128)S(1)}) custom-call(s32[1]{0:T(128)} %bitcast.first_ref, bf16[512,2048]{1,0:T(8,128)(2,1)S(1)} %copy-done, bf16[512,1024]{1,0:T(8,128)(2,1)S(1)} %collective-permute-done.2.k_ref, bf16[512,1024]{1,0:T(8,128)(2,1)} %collective-permute-done.4.v_ref, ...), custom_call_target="tpu_custom_call" | custom-call | flops 2147483648 | bytes 8388608 | tf_op jit(solution)/shard_map/next_shard/pallas_call | solution.py:321
  69.5 0.0 collective-permute-done.3.k_ref
  69.5 0.0 collective-permute-done.5.v_ref
  69.5 0.0 collective-permute-done.1.slot_ref
  69.5 12.0 %last_shard.1 = bf16[512,2048]{1,0:T(8,128)(2,1)} custom-call(s32[1]{0:T(128)} %bitcast.first_ref, bf16[512,2048]{1,0:T(8,128)(2,1)S(1)} %copy-done, bf16[256,2176]{1,0:T(8,128)(2,1)S(1)} %collective-permute-done.1.slot_ref, bf16[512,1024]{1,0:T(8,128)(2,1)S(1)} %collective-permute-done.3.k_ref, ...), custom_call_target="tpu_custom_call", output_to_operand_aliasing={{}: (7, {})} | custom-call | flops 1073741824 | bytes 8388608 | tf_op jit(solution)/shard_map/last_shard/pallas_call | solution.py:336
Async XLA Ops:
  0.0 10.2 %copy-start.1 = (bf16[512,1024]{1,0:T(8,128)(2,1)S(1)}, bf16[512,1024]{1,0:T(8,128)(2,1)}, u32[]{:S(2)}) copy-start(bf16[512,1024]{1,0:T(8,128)(2,1)} %k_ref.3) | copy-start | bytes 3145732
  0.0 12.1 %copy-start.2 = (bf16[512,1024]{1,0:T(8,128)(2,1)S(1)}, bf16[512,1024]{1,0:T(8,128)(2,1)}, u32[]{:S(2)}) copy-start(bf16[512,1024]{1,0:T(8,128)(2,1)} %v_ref.3) | copy-start | bytes 3145732
  0.0 22.8 %copy-start.3 = (s32[256]{0:T(256)S(1)}, s32[256]{0:T(256)}, u32[]{:S(2)}) copy-start(s32[256]{0:T(256)} %param.7) | copy-start | bytes 3076
  2.5 20.3 %collective-permute-start = (bf16[256,2048]{1,0:T(8,128)(2,1)}, bf16[256,2048]{1,0:T(8,128)(2,1)}, u32[]{:S(2)}, u32[]{:S(2)}) collective-permute-start(bf16[256,2048]{1,0:T(8,128)(2,1)} %slice.3), channel_id=1, source_target_pairs={{2,0},{4,2},{6,4},{8,6},{10,8},{12,10},{14,12},{16,14},{18,16},{20... | collective-permute-start | bytes 3145736 | tf_op jit(solution)/shard_map/ppermute | solution.py:357
  10.2 18.2 %collective-permute-start.2 = (bf16[512,1024]{1,0:T(8,128)(2,1)S(1)}, bf16[512,1024]{1,0:T(8,128)(2,1)S(1)}, u32[]{:S(2)}, u32[]{:S(2)}) collective-permute-start(bf16[512,1024]{1,0:T(8,128)(2,1)S(1)} %copy-done.1), channel_id=1, source_target_pairs={{0,1},{1,2},{2,3},{3,4},{4,5},{5,6},{6,7},{7,8},{8,9},{9,10},{10,1... | collective-permute-start | bytes 3145736 | tf_op jit(solution)/shard_map/ppermute | solution.py:357
  12.1 34.7 %collective-permute-start.4 = (bf16[512,1024]{1,0:T(8,128)(2,1)S(1)}, bf16[512,1024]{1,0:T(8,128)(2,1)}, u32[]{:S(2)}, u32[]{:S(2)}) collective-permute-start(bf16[512,1024]{1,0:T(8,128)(2,1)S(1)} %copy-done.2), channel_id=1, source_target_pairs={{0,1},{1,2},{2,3},{3,4},{4,5},{5,6},{6,7},{7,8},{8,9},{9,10},{10,1... | collective-permute-start | bytes 3145736 | tf_op jit(solution)/shard_map/ppermute | solution.py:357
  22.8 25.5 %copy-start = (bf16[512,2048]{1,0:T(8,128)(2,1)S(1)}, bf16[512,2048]{1,0:T(8,128)(2,1)}, u32[]{:S(2)}) copy-start(bf16[512,2048]{1,0:T(8,128)(2,1)} %q_ref.5) | copy-start | bytes 6291460
  24.6 44.8 %collective-permute-start.1 = (bf16[256,2176]{1,0:T(8,128)(2,1)S(1)}, bf16[256,2176]{1,0:T(8,128)(2,1)S(1)}, u32[]{:S(2)}, u32[]{:S(2)}) collective-permute-start(bf16[256,2176]{1,0:T(8,128)(2,1)S(1)} %back_shard.1), channel_id=1, source_target_pairs={{0,2},{2,4},{4,6},{6,8},{8,10},{10,12},{12,14},{14,16},{16,18},{18... | collective-permute-start | bytes 3342344 | tf_op jit(solution)/shard_map/ppermute | solution.py:357
  28.4 41.0 %collective-permute-start.3 = (bf16[512,1024]{1,0:T(8,128)(2,1)S(1)}, bf16[512,1024]{1,0:T(8,128)(2,1)S(1)}, u32[]{:S(2)}, u32[]{:S(2)}) collective-permute-start(bf16[512,1024]{1,0:T(8,128)(2,1)S(1)} %collective-permute-done.2.k_ref), channel_id=1, source_target_pairs={{0,1},{2,3},{4,5},{6,7},{8,9},{10,11},{12,13},{14,15},{16,17},{18,... | collective-permute-start | bytes 3145736 | tf_op jit(solution)/shard_map/ppermute | solution.py:357
  46.8 22.7 %collective-permute-start.5 = (bf16[512,1024]{1,0:T(8,128)(2,1)}, bf16[512,1024]{1,0:T(8,128)(2,1)S(1)}, u32[]{:S(2)}, u32[]{:S(2)}) collective-permute-start(bf16[512,1024]{1,0:T(8,128)(2,1)} %collective-permute-done.4.v_ref), channel_id=1, source_target_pairs={{0,1},{2,3},{4,5},{6,7},{8,9},{10,11},{12,13},{14,15},{16,17},{18,... | collective-permute-start | bytes 3145736 | tf_op jit(solution)/shard_map/ppermute | solution.py:357

commit v3 on v2

--- a/solution.py
+++ b/solution.py
@@ -38,7 +38,7 @@
     return lax.broadcasted_iota(jnp.int32, shape, axis).astype(jnp.float32)
 
 
-def attend(pair, keys, values, bias, before, emit):
+def attend(pair, keys, values, bias, emit):
     rows = bias.shape[0]
 
     def score(head):
@@ -51,8 +51,6 @@
             ahead = score(head + 1)
         scores = scores.reshape(GROUPS, rows, -1) + bias[None]
         top = jnp.max(scores, axis=-1, keepdims=True)
-        if before is not None:
-            top = jnp.maximum(top, before(head))
         weights = jnp.exp2((scores - top) * RATE)
         rounded = weights.astype(jnp.bfloat16).reshape(GROUPS * rows, -1)
         value = values(head)
@@ -97,7 +95,7 @@
         acc_ref[:, h * DH : (h + 1) * DH] = mixed
         state[0] = jnp.where(lane == HQ + h, total, jnp.where(lane == h, top, state[0]))
 
-    attend(pairs_of(q_ref), heads_of(k_ref), heads_of(v_ref), bias, None, emit)
+    attend(pairs_of(q_ref), heads_of(k_ref), heads_of(v_ref), bias, emit)
     state_ref[...] = state[0]
 
 
@@ -135,7 +133,7 @@
                 slot_ref[:, h * DH : (h + 1) * DH] = (mixed * (1.0 / total)).astype(jnp.bfloat16)
                 level[0] = jnp.where(lane % HQ == h, top * RATE + jnp.log2(total), level[0])
 
-            attend(pairs_of(q_ref), heads_of(k_ref), heads_of(v_ref), bias, None, emit)
+            attend(pairs_of(q_ref), heads_of(k_ref), heads_of(v_ref), bias, emit)
             rest = level[0]
             tail = jnp.zeros((BQ, 128), jnp.float32)
             for part in range(PARTS):
@@ -149,11 +147,36 @@
     return state[:, lane : lane + 1]
 
 
-def old_tops(state):
-    return lambda head: jnp.stack([column(state, head * GROUPS + g) for g in range(GROUPS)])
-
-
-def next_kernel(first_ref, q_ref, k_ref, v_ref, acc_ref, state_ref, out_ref, new_acc_ref, new_state_ref):
+def heads_lanes(state, group):
+    return pltpu.roll(state, 128 - group * HQ, 1) if group else state
+
+
+def collect(fresh_ref):
+    rows = fresh_ref.shape[0]
+    lane = lax.broadcasted_iota(jnp.int32, (rows, 128), 1)
+    held = [jnp.zeros((rows, 128), jnp.float32)]
+
+    def emit(head, g, mixed, total, top):
+        h = head * GROUPS + g
+        fresh_ref[:, h * DH : (h + 1) * DH] = mixed
+        held[0] = jnp.where(lane == HQ + h, total, jnp.where(lane == h, top, held[0]))
+
+    return emit, held
+
+
+def joined(state, fresh, normalised):
+    top = jnp.maximum(state, fresh)
+    keep = jnp.exp2((state - top) * RATE)
+    take = jnp.exp2((fresh - top) * RATE)
+    before = keep * heads_lanes(state, 1)
+    total = before + take * heads_lanes(fresh, 1)
+    scale = 1.0 / total
+    return (before if normalised else keep) * scale, take * scale, top, total
+
+
+def next_kernel(
+    first_ref, q_ref, k_ref, v_ref, acc_ref, state_ref, out_ref, new_acc_ref, new_state_ref, fresh_ref
+):
     keys = k_ref.shape[0]
     first = first_ref[0].astype(jnp.float32)
     base = first - keys
@@ -163,89 +186,93 @@
 
     @pl.when(lowest >= first)
     def _():
+        scale = 1.0 / heads_lanes(state, 1)
         for h in range(HQ):
             cols = slice(h * DH, (h + 1) * DH)
-            out_ref[:, cols] = (acc_ref[:, cols] * (1.0 / column(state, HQ + h))).astype(out_ref.dtype)
+            out_ref[:, cols] = (acc_ref[:, cols] * column(scale, h)).astype(out_ref.dtype)
         new_state_ref[...] = state
 
     @pl.when(lowest < first)
     def _():
         bias = jnp.where(float_iota((BQ, keys), 1) >= start - base, 0.0, HIDDEN)
+        emit, held = collect(fresh_ref)
+        attend(pairs_of(q_ref), heads_of(k_ref), heads_of(v_ref), bias, emit)
+        keep, take, top, total = joined(state, held[0], False)
         lane = lax.broadcasted_iota(jnp.int32, (BQ, 128), 1)
-        new = [state]
-
-        def emit(head, g, mixed, total, top):
-            h = head * GROUPS + g
+        totals = pltpu.roll(total, HQ, 1)
+        new_state_ref[...] = jnp.where(lane < HQ, top, jnp.where(lane < 2 * HQ, totals, state))
+        for h in range(HQ):
             cols = slice(h * DH, (h + 1) * DH)
-            keep = jnp.exp2((column(state, h) - top) * RATE)
-            total = total + keep * column(state, HQ + h)
-            mixed = mixed + keep * acc_ref[:, cols]
+            mixed = acc_ref[:, cols] * column(keep, h) + fresh_ref[:, cols] * column(take, h)
             new_acc_ref[:, cols] = mixed
-            new[0] = jnp.where(lane == HQ + h, total, jnp.where(lane == h, top, new[0]))
-            out_ref[:, cols] = (mixed * (1.0 / total)).astype(out_ref.dtype)
-
-        attend(pairs_of(q_ref), heads_of(k_ref), heads_of(v_ref), bias, old_tops(state), emit)
-        new_state_ref[...] = new[0]
-
-
-def last_kernel(first_ref, q_ref, slot_ref, k_ref, v_ref, acc_ref, state_ref, prior_ref, out_ref, rows_ref, sem):
+            out_ref[:, cols] = mixed.astype(out_ref.dtype)
+
+
+def last_kernel(
+    first_ref, q_ref, slot_ref, k_ref, v_ref, acc_ref, state_ref, prior_ref, out_ref, rows_ref, fresh_ref, sem
+):
     keys = k_ref.shape[0]
     first = first_ref[0].astype(jnp.float32)
     odd = (first_ref[0] // keys) % 2 == 1
+    even = jnp.logical_not(odd)
     base = first - keys
     blocks = q_ref.shape[0] // BQ
     by_keys = base - jnp.min(state_ref[:8, START : START + 1]) <= SLOT
 
-    def reaches(block):
-        return jnp.min(state_ref[pl.ds(block * BQ, 8), START : START + 1]) < base
+    def earliest(block):
+        return jnp.min(state_ref[pl.ds(block * BQ, 8), START : START + 1])
 
     def copy(block):
         rows = pl.ds(pl.multiple_of(block * BQ, BQ), BQ)
         return pltpu.make_async_copy(rows_ref.at[rows, :], out_ref.at[rows, :], sem.at[block])
 
+    def write(rows, keep, take, added_ref, added_rows):
+        for h in range(HQ):
+            cols = slice(h * DH, (h + 1) * DH)
+            mixed = acc_ref[rows, cols] * column(keep, h) + added_ref[added_rows, cols].astype(jnp.float32) * column(take, h)
+            rows_ref[rows, cols] = mixed.astype(rows_ref.dtype)
+
     def merge(block, get_keys, get_values, count, origin):
         rows = pl.ds(pl.multiple_of(block * BQ, BQ), BQ)
         state = state_ref[rows, :]
-        start = column(state, START)
-        bias = jnp.where(float_iota((BQ, count), 1) >= start - origin, 0.0, HIDDEN)
-
-        def emit(head, g, mixed, total, top):
-            h = head * GROUPS + g
-            cols = slice(h * DH, (h + 1) * DH)
-            keep = jnp.exp2((column(state, h) - top) * RATE)
-            total = total + keep * column(state, HQ + h)
-            mixed = mixed + keep * acc_ref[rows, cols]
-            rows_ref[rows, cols] = (mixed * (1.0 / total)).astype(rows_ref.dtype)
-
-        attend(pairs_of(q_ref, rows), get_keys, get_values, bias, old_tops(state), emit)
+        bias = jnp.where(float_iota((BQ, count), 1) >= column(state, START) - origin, 0.0, HIDDEN)
+        emit, held = collect(fresh_ref)
+        attend(pairs_of(q_ref, rows), get_keys, get_values, bias, emit)
+        keep, take, _, _ = joined(state, held[0], True)
+        write(rows, keep, take, fresh_ref, slice(None))
 
     def combine(block):
         rows = pl.ds(pl.multiple_of(block * BQ, BQ), BQ)
         state = state_ref[rows, :]
-        tail = slot_ref[rows, 2 * KV :].astype(jnp.float32)
-        for h in range(HQ):
-            cols = slice(h * DH, (h + 1) * DH)
-            there = sum(column(tail, part * HQ + h) for part in reversed(range(PARTS)))
-            here = column(state, h) * RATE
-            top = jnp.maximum(here, there)
-            keep, take = jnp.exp2(here - top), jnp.exp2(there - top)
-            scale = 1.0 / (keep * column(state, HQ + h) + take)
-            mixed = acc_ref[rows, cols] * (keep * scale) + slot_ref[rows, cols].astype(jnp.float32) * (take * scale)
-            rows_ref[rows, cols] = mixed.astype(rows_ref.dtype)
+        parts = slot_ref[rows, 2 * KV :].astype(jnp.float32)
+        there = sum(heads_lanes(parts, part) for part in reversed(range(PARTS)))
+        here = state * RATE
+        top = jnp.maximum(here, there)
+        before = jnp.exp2(here - top) * heads_lanes(state, 1)
+        take = jnp.exp2(there - top)
+        scale = 1.0 / (before + take)
+        write(rows, before * scale, take * scale, slot_ref, rows)
 
     @pl.loop(0, blocks)
     def _(block):
-        needed = reaches(block)
-
-        @pl.when(needed & odd)
+        start = earliest(block)
+        needed = start < base
+        far = start < base - SLOT
+
+        @pl.when(odd & far)
         def _():
             merge(block, heads_of(k_ref), heads_of(v_ref), keys, base - keys)
 
-        @pl.when(needed & jnp.logical_not(odd) & by_keys)
+        @pl.when(odd & needed & jnp.logical_not(far))
+        def _():
+            near = slice(keys - SLOT, keys)
+            merge(block, heads_of(k_ref, near), heads_of(v_ref, near), SLOT, base - SLOT)
+
+        @pl.when(even & needed & by_keys)
         def _():
             merge(block, heads_of(slot_ref), heads_of(slot_ref, at=KV), SLOT, base - SLOT)
 
-        @pl.when(needed & jnp.logical_not(odd) & jnp.logical_not(by_keys) & (block * BQ < SLOT))
+        @pl.when(even & needed & jnp.logical_not(by_keys) & (block * BQ < SLOT))
         def _():
             combine(block)
 
@@ -255,7 +282,7 @@
 
     @pl.loop(0, blocks)
     def _(block):
-        @pl.when(reaches(block))
+        @pl.when(earliest(block) < base)
         def _():
             copy(block).wait()
 
@@ -302,6 +329,24 @@
     )(first, lengths, queries, keys, values)
 
 
+def copy_kernel(in_ref, out_ref):
+    out_ref[...] = in_ref[...]
+
+
+def leading_rows(array, rows):
+    block = pl.BlockSpec((rows, array.shape[1]), lambda i: (0, 0))
+    return pl.pallas_call(
+        copy_kernel,
+        grid=(1,),
+        in_specs=[block],
+        out_specs=block,
+        out_shape=jax.ShapeDtypeStruct((rows, array.shape[1]), array.dtype),
+        compiler_params=PARAMS,
+        name="leading_rows",
+        interpret=INTERPRET,
+    )(array)
+
+
 def back_stage(first, lengths, queries, keys, values):
     return pl.pallas_call(
         back_kernel,
@@ -324,6 +369,7 @@
         in_specs=[SMEM, rows_of(WIDE), WHOLE, WHOLE, rows_of(WIDE), rows_of(128)],
         out_specs=[rows_of(WIDE), rows_of(WIDE), rows_of(128)],
         out_shape=[bf16(rows, WIDE), f32(rows, WIDE), f32(rows, 128)],
+        scratch_shapes=[pltpu.VMEM((BQ, WIDE), jnp.float32)],
         cost_estimate=cost(rows, keys.shape[0]),
         compiler_params=PARAMS,
         name="next_shard",
@@ -338,7 +384,11 @@
         in_specs=[SMEM, WHOLE, WHOLE, WHOLE, WHOLE, WHOLE, WHOLE, pl.BlockSpec(memory_space=pl.ANY)],
         out_specs=pl.BlockSpec(memory_space=pl.ANY),
         out_shape=bf16(rows, WIDE),
-        scratch_shapes=[pltpu.VMEM((rows, WIDE), jnp.bfloat16), pltpu.SemaphoreType.DMA((rows // BQ,))],
+        scratch_shapes=[
+            pltpu.VMEM((rows, WIDE), jnp.bfloat16),
+            pltpu.VMEM((BQ, WIDE), jnp.float32),
+            pltpu.SemaphoreType.DMA((rows // BQ,)),
+        ],
         input_output_aliases={7: 0},
         cost_estimate=cost(rows, SLOT),
         compiler_params=PARAMS,
@@ -359,7 +409,7 @@
     onward = [(i, i + 1) for i in range(count - 1)]
     one_k = hop(keys, onward)
     one_v = hop(values, onward)
-    guests = hop(queries[:SLOT], [(i, i - 2) for i in evens if i])
+    guests = hop(leading_rows(queries, SLOT), [(i, i - 2) for i in evens if i])
     acc, state = own_stage(first, lengths, queries, keys, values)
     slot = back_stage(first, lengths, guests, keys, values)
     slot = hop(slot, [(i, i + 2) for i in evens if i + 2 < count])

time: 81.9 us -> 75.2 us (0.918)
  Pallas kernels: 34.9 us -> 29.1 us
  local copies, waits for them, and re-layouts: 2.47 us -> 1.61 us
    pallas_call x1, Pallas kernels: 12 us -> 7.93 us  [last_stage(): pl.pallas_call(last_kernel, in_specs=[SMEM, WHOLE, WHOLE, WHOLE, WHOLE, W...]
    pallas_call x1, Pallas kernels: 14.7 us -> 11.9 us  [next_stage(): pl.pallas_call(next_kernel, grid=(rows // BQ,), in_specs=[SMEM, rows_of(W...]
    slice x1 -> x0, local copies, waits for them, and re-layouts: 2.45 us -> none  [on_device(): guests = hop(queries[:SLOT], [(i, i - 2) for i in evens if i])]
    unnamed x8 -> x10, local copies, waits for them, and re-layouts: 0.01 us -> 1.61 us
    pallas_call x0 -> x1, Pallas kernels: none -> 1.04 us  [leading_rows(): pl.pallas_call(copy_kernel, grid=(1,), in_specs=[block], out_specs=block,...]
  transfers between devices with their start and end apart: 6 -> 6, of which waited for: 3 -> 3; matrix products, arithmetic and copies ran while one was open for 0% -> 0% of each run, Pallas kernels for 28% -> 27%
where the time goes in v3:
time: 75.2 us; the launch traced here: 75 us
  Pallas kernels  29.1 us (39%)
  waiting for transfers between devices  27.6 us (37%)
  starting transfers between devices  16.4 us (22%)
  local copies, waits for them, and re-layouts  1.61 us (2%)
    ppermute x6, waiting for transfers between devices, hop(): return lax.ppermute(array, 'cp', pairs)  27.6 us
    ppermute x6, starting transfers between devices, hop(): return lax.ppermute(array, 'cp', pairs)  16.4 us
    pallas_call x1, Pallas kernels, next_stage(): pl.pallas_call(next_kernel, grid=(rows // BQ,), in_specs=[SMEM, rows_of(W...  11.9 us
    pallas_call x1, Pallas kernels, last_stage(): pl.pallas_call(last_kernel, in_specs=[SMEM, WHOLE, WHOLE, WHOLE, WHOLE, W...  7.93 us
    pallas_call x1, Pallas kernels, own_stage(): pl.pallas_call(own_kernel, grid=(rows // BQ,), in_specs=[SMEM, WHOLE, row...  6.41 us
    pallas_call x1, Pallas kernels, back_stage(): pl.pallas_call(back_kernel, grid=(SLOT // BQ,), in_specs=[SMEM, WHOLE, ro...  1.79 us
    unnamed x10, local copies, waits for them, and re-layouts  1.61 us
  transfers between devices with their start and end apart: 6, of which 3 were waited for; matrix products, arithmetic and copies ran while one was open for 0% of the time, Pallas kernels for 27%

profile of v3, /device:TPU:20, one launch (start us, length us, event | category | flops | bytes accessed | tf_op | source)
XLA Modules:
  0.0 75.0 jit_solution(1084248869680613487)
XLA Ops:
  0.0 0.0 copy-start
  0.0 1.6 %copy-done = bf16[512,2048]{1,0:T(8,128)(2,1)S(1)} copy-done((bf16[512,2048]{1,0:T(8,128)(2,1)S(1)}, bf16[512,2048]{1,0:T(8,128)(2,1)}, u32[]{:S(2)}) %copy-start) | copy-done | bytes 2097176
  1.6 0.0 copy-start.2
  1.6 0.0 copy-start.3
  1.6 0.0 copy-start.4
  1.6 1.0 %leading_rows.1 = bf16[256,2048]{1,0:T(8,128)(2,1)} custom-call(bf16[512,2048]{1,0:T(8,128)(2,1)S(1)} %copy-done), custom_call_target="tpu_custom_call" | custom-call | tf_op jit(solution)/shard_map/leading_rows/pallas_call | solution.py:338
  2.6 7.7 %collective-permute-start = (bf16[256,2048]{1,0:T(8,128)(2,1)}, bf16[256,2048]{1,0:T(8,128)(2,1)}, u32[]{:S(2)}, u32[]{:S(2)}) collective-permute-start(bf16[256,2048]{1,0:T(8,128)(2,1)} %leading_rows.1), channel_id=1, source_target_pairs={{2,0},{4,2},{6,4},{8,6},{10,8},{12,10},{14,12},{16,14},{18,16},{20... | collective-permute-start | bytes 3145736 | tf_op jit(solution)/shard_map/ppermute | solution.py:407
  10.4 0.0 copy-done.2
  10.4 1.9 %collective-permute-start.2 = (bf16[512,1024]{1,0:T(8,128)(2,1)S(1)}, bf16[512,1024]{1,0:T(8,128)(2,1)S(1)}, u32[]{:S(2)}, u32[]{:S(2)}) collective-permute-start(bf16[512,1024]{1,0:T(8,128)(2,1)S(1)} %copy-done.2), channel_id=1, source_target_pairs={{0,1},{1,2},{2,3},{3,4},{4,5},{5,6},{6,7},{7,8},{8,9},{9,10},{10,1... | collective-permute-start | bytes 3145736 | tf_op jit(solution)/shard_map/ppermute | solution.py:407
  12.3 0.0 copy-done.3
  12.3 1.9 %collective-permute-start.4 = (bf16[512,1024]{1,0:T(8,128)(2,1)S(1)}, bf16[512,1024]{1,0:T(8,128)(2,1)}, u32[]{:S(2)}, u32[]{:S(2)}) collective-permute-start(bf16[512,1024]{1,0:T(8,128)(2,1)S(1)} %copy-done.3), channel_id=1, source_target_pairs={{0,1},{1,2},{2,3},{3,4},{4,5},{5,6},{6,7},{7,8},{8,9},{9,10},{10,1... | collective-permute-start | bytes 3145736 | tf_op jit(solution)/shard_map/ppermute | solution.py:407
  14.3 8.7 %collective-permute-done.q_ref = bf16[256,2048]{1,0:T(8,128)(2,1)} collective-permute-done((bf16[256,2048]{1,0:T(8,128)(2,1)}, bf16[256,2048]{1,0:T(8,128)(2,1)}, u32[]{:S(2)}, u32[]{:S(2)}) %collective-permute-start) | collective-permute-done | bytes 1048608 | tf_op jit(solution)/shard_map/ppermute | solution.py:407
  23.0 0.0 copy-done.4
  23.0 0.0 copy-start.1
  23.0 1.8 %back_shard.1 = bf16[256,2176]{1,0:T(8,128)(2,1)S(1)} custom-call(s32[1]{0:T(128)} %bitcast.first_ref, s32[1,256]{1,0:T(1,128)S(1)} %bitcast.2, bf16[256,2048]{1,0:T(8,128)(2,1)} %collective-permute-done.q_ref, bf16[512,1024]{1,0:T(8,128)(2,1)S(1)} %copy-done.2, bf16[512,1024]{1,0:T(8,128)(2,1)S(1)} %copy-done.3), custom_call_target="tpu_custom_call" | custom-call | flops 1073741824 | bytes 4194304 | tf_op jit(solution)/shard_map/back_shard/pallas_call | solution.py:351
  24.8 1.9 %collective-permute-start.1 = (bf16[256,2176]{1,0:T(8,128)(2,1)S(1)}, bf16[256,2176]{1,0:T(8,128)(2,1)S(1)}, u32[]{:S(2)}, u32[]{:S(2)}) collective-permute-start(bf16[256,2176]{1,0:T(8,128)(2,1)S(1)} %back_shard.1), channel_id=1, source_target_pairs={{0,2},{2,4},{4,6},{6,8},{8,10},{10,12},{12,14},{14,16},{16,18},{18... | collective-permute-start | bytes 3342344 | tf_op jit(solution)/shard_map/ppermute | solution.py:407
  26.7 1.9 %collective-permute-done.2.k_ref = bf16[512,1024]{1,0:T(8,128)(2,1)S(1)} collective-permute-done((bf16[512,1024]{1,0:T(8,128)(2,1)S(1)}, bf16[512,1024]{1,0:T(8,128)(2,1)S(1)}, u32[]{:S(2)}, u32[]{:S(2)}) %collective-permute-start.2) | collective-permute-done | bytes 1048608 | tf_op jit(solution)/shard_map/ppermute | solution.py:407
  28.6 1.3 %collective-permute-start.3 = (bf16[512,1024]{1,0:T(8,128)(2,1)S(1)}, bf16[512,1024]{1,0:T(8,128)(2,1)S(1)}, u32[]{:S(2)}, u32[]{:S(2)}) collective-permute-start(bf16[512,1024]{1,0:T(8,128)(2,1)S(1)} %collective-permute-done.2.k_ref), channel_id=1, source_target_pairs={{0,1},{2,3},{4,5},{6,7},{8,9},{10,11},{12,13},{14,15},{16,17},{18,... | collective-permute-start | bytes 3145736 | tf_op jit(solution)/shard_map/ppermute | solution.py:407
  30.0 17.0 %collective-permute-done.4.v_ref = bf16[512,1024]{1,0:T(8,128)(2,1)} collective-permute-done((bf16[512,1024]{1,0:T(8,128)(2,1)S(1)}, bf16[512,1024]{1,0:T(8,128)(2,1)}, u32[]{:S(2)}, u32[]{:S(2)}) %collective-permute-start.4) | collective-permute-done | bytes 1048608 | tf_op jit(solution)/shard_map/ppermute | solution.py:407
  47.0 1.5 %collective-permute-start.5 = (bf16[512,1024]{1,0:T(8,128)(2,1)}, bf16[512,1024]{1,0:T(8,128)(2,1)S(1)}, u32[]{:S(2)}, u32[]{:S(2)}) collective-permute-start(bf16[512,1024]{1,0:T(8,128)(2,1)} %collective-permute-done.4.v_ref), channel_id=1, source_target_pairs={{0,1},{2,3},{4,5},{6,7},{8,9},{10,11},{12,13},{14,15},{16,17},{18,... | collective-permute-start | bytes 3145736 | tf_op jit(solution)/shard_map/ppermute | solution.py:407
  48.5 0.0 copy-done.1
  48.5 6.4 %own_shard.1 = (f32[512,2048]{1,0:T(8,128)S(1)}, f32[512,128]{1,0:T(8,128)S(1)}) custom-call(s32[1]{0:T(128)} %bitcast.first_ref, s32[1,256]{1,0:T(1,128)S(1)} %bitcast.3, bf16[512,2048]{1,0:T(8,128)(2,1)S(1)} %copy-done.1, bf16[512,1024]{1,0:T(8,128)(2,1)S(1)} %copy-done.2, bf16[512,1024]{1,0:T(8,128)(2,1)S(1)} %copy-done.3), custom_call_target="tpu_custom_call" | custom-call | flops 2147483648 | bytes 8388608 | tf_op jit(solution)/shard_map/own_shard/pallas_call | solution.py:318
  54.9 11.9 %next_shard.1 = (bf16[512,2048]{1,0:T(8,128)(2,1)}, f32[512,2048]{1,0:T(8,128)S(1)}, f32[512,128]{1,0:T(8,128)S(1)}) custom-call(s32[1]{0:T(128)} %bitcast.first_ref, bf16[512,2048]{1,0:T(8,128)(2,1)S(1)} %copy-done.1, bf16[512,1024]{1,0:T(8,128)(2,1)S(1)} %collective-permute-done.2.k_ref, bf16[512,1024]{1,0:T(8,128)(2,1)} %collective-permute-done.4.v_ref, ...), custom_call_target="tpu_custom_call" | custom-call | flops 2147483648 | bytes 8388608 | tf_op jit(solution)/shard_map/next_shard/pallas_call | solution.py:366
  66.8 0.0 collective-permute-done.3.k_ref
  66.9 0.0 collective-permute-done.5.v_ref
  66.9 0.0 collective-permute-done.1.slot_ref
  66.9 7.9 %last_shard.1 = bf16[512,2048]{1,0:T(8,128)(2,1)} custom-call(s32[1]{0:T(128)} %bitcast.first_ref, bf16[512,2048]{1,0:T(8,128)(2,1)S(1)} %copy-done.1, bf16[256,2176]{1,0:T(8,128)(2,1)S(1)} %collective-permute-done.1.slot_ref, bf16[512,1024]{1,0:T(8,128)(2,1)S(1)} %collective-permute-done.3.k_ref, ...), custom_call_target="tpu_custom_call", output_to_operand_aliasing={{}: (7, {})} | custom-call | flops 1073741824 | bytes 8388608 | tf_op jit(solution)/shard_map/last_shard/pallas_call | solution.py:382
Async XLA Ops:
  0.0 1.6 %copy-start = (bf16[512,2048]{1,0:T(8,128)(2,1)S(1)}, bf16[512,2048]{1,0:T(8,128)(2,1)}, u32[]{:S(2)}) copy-start(bf16[512,2048]{1,0:T(8,128)(2,1)} %q_ref.5) | copy-start | bytes 6291460
  1.6 8.8 %copy-start.2 = (bf16[512,1024]{1,0:T(8,128)(2,1)S(1)}, bf16[512,1024]{1,0:T(8,128)(2,1)}, u32[]{:S(2)}) copy-start(bf16[512,1024]{1,0:T(8,128)(2,1)} %k_ref.3) | copy-start | bytes 3145732
  1.6 10.7 %copy-start.3 = (bf16[512,1024]{1,0:T(8,128)(2,1)S(1)}, bf16[512,1024]{1,0:T(8,128)(2,1)}, u32[]{:S(2)}) copy-start(bf16[512,1024]{1,0:T(8,128)(2,1)} %v_ref.3) | copy-start | bytes 3145732
  1.6 21.4 %copy-start.4 = (s32[256]{0:T(256)S(1)}, s32[256]{0:T(256)}, u32[]{:S(2)}) copy-start(s32[256]{0:T(256)} %param.7) | copy-start | bytes 3076
  2.6 20.3 %collective-permute-start = (bf16[256,2048]{1,0:T(8,128)(2,1)}, bf16[256,2048]{1,0:T(8,128)(2,1)}, u32[]{:S(2)}, u32[]{:S(2)}) collective-permute-start(bf16[256,2048]{1,0:T(8,128)(2,1)} %leading_rows.1), channel_id=1, source_target_pairs={{2,0},{4,2},{6,4},{8,6},{10,8},{12,10},{14,12},{16,14},{18,16},{20... | collective-permute-start | bytes 3145736 | tf_op jit(solution)/shard_map/ppermute | solution.py:407
  10.4 18.2 %collective-permute-start.2 = (bf16[512,1024]{1,0:T(8,128)(2,1)S(1)}, bf16[512,1024]{1,0:T(8,128)(2,1)S(1)}, u32[]{:S(2)}, u32[]{:S(2)}) collective-permute-start(bf16[512,1024]{1,0:T(8,128)(2,1)S(1)} %copy-done.2), channel_id=1, source_target_pairs={{0,1},{1,2},{2,3},{3,4},{4,5},{5,6},{6,7},{7,8},{8,9},{9,10},{10,1... | collective-permute-start | bytes 3145736 | tf_op jit(solution)/shard_map/ppermute | solution.py:407
  12.3 34.7 %collective-permute-start.4 = (bf16[512,1024]{1,0:T(8,128)(2,1)S(1)}, bf16[512,1024]{1,0:T(8,128)(2,1)}, u32[]{:S(2)}, u32[]{:S(2)}) collective-permute-start(bf16[512,1024]{1,0:T(8,128)(2,1)S(1)} %copy-done.3), channel_id=1, source_target_pairs={{0,1},{1,2},{2,3},{3,4},{4,5},{5,6},{6,7},{7,8},{8,9},{9,10},{10,1... | collective-permute-start | bytes 3145736 | tf_op jit(solution)/shard_map/ppermute | solution.py:407
  23.0 25.5 %copy-start.1 = (bf16[512,2048]{1,0:T(8,128)(2,1)S(1)}, bf16[512,2048]{1,0:T(8,128)(2,1)}, u32[]{:S(2)}) copy-start(bf16[512,2048]{1,0:T(8,128)(2,1)} %q_ref.5) | copy-start | bytes 6291460
  24.8 42.1 %collective-permute-start.1 = (bf16[256,2176]{1,0:T(8,128)(2,1)S(1)}, bf16[256,2176]{1,0:T(8,128)(2,1)S(1)}, u32[]{:S(2)}, u32[]{:S(2)}) collective-permute-start(bf16[256,2176]{1,0:T(8,128)(2,1)S(1)} %back_shard.1), channel_id=1, source_target_pairs={{0,2},{2,4},{4,6},{6,8},{8,10},{10,12},{12,14},{14,16},{16,18},{18... | collective-permute-start | bytes 3342344 | tf_op jit(solution)/shard_map/ppermute | solution.py:407
  28.6 38.2 %collective-permute-start.3 = (bf16[512,1024]{1,0:T(8,128)(2,1)S(1)}, bf16[512,1024]{1,0:T(8,128)(2,1)S(1)}, u32[]{:S(2)}, u32[]{:S(2)}) collective-permute-start(bf16[512,1024]{1,0:T(8,128)(2,1)S(1)} %collective-permute-done.2.k_ref), channel_id=1, source_target_pairs={{0,1},{2,3},{4,5},{6,7},{8,9},{10,11},{12,13},{14,15},{16,17},{18,... | collective-permute-start | bytes 3145736 | tf_op jit(solution)/shard_map/ppermute | solution.py:407
  47.0 19.9 %collective-permute-start.5 = (bf16[512,1024]{1,0:T(8,128)(2,1)}, bf16[512,1024]{1,0:T(8,128)(2,1)S(1)}, u32[]{:S(2)}, u32[]{:S(2)}) collective-permute-start(bf16[512,1024]{1,0:T(8,128)(2,1)} %collective-permute-done.4.v_ref), channel_id=1, source_target_pairs={{0,1},{2,3},{4,5},{6,7},{8,9},{10,11},{12,13},{14,15},{16,17},{18,... | collective-permute-start | bytes 3145736 | tf_op jit(solution)/shard_map/ppermute | solution.py:407

commit v4 on v3

--- a/solution.py
+++ b/solution.py
@@ -73,6 +73,31 @@
     return pair
 
 
+def in_parts(table):
+    rest = jnp.where(lax.broadcasted_iota(jnp.int32, table.shape, 1) < HQ, table, 0.0)
+    parts = jnp.zeros_like(table)
+    for part in range(PARTS):
+        piece = rest.astype(jnp.bfloat16).astype(jnp.float32)
+        parts = parts + (pltpu.roll(piece, part * HQ, 1) if part else piece)
+        rest = rest - piece
+    return parts.astype(jnp.bfloat16)
+
+
+def spreader():
+    sub = lax.broadcasted_iota(jnp.int32, (128, HQ * DH), 0)
+    lane = lax.broadcasted_iota(jnp.int32, (128, HQ * DH), 1)
+    return jnp.where((sub < PARTS * HQ) & (sub % HQ == lane // DH), 1.0, 0.0).astype(jnp.bfloat16)
+
+
+def mix(keep, kept, take, taken, spread_ref, write):
+    rows = keep.shape[0]
+    table = jnp.concatenate([in_parts(keep), in_parts(take)], axis=0)
+    for head in range(HK):
+        cols = slice(head * WIDTH, (head + 1) * WIDTH)
+        factors = jnp.dot(table, spread_ref[:, cols], preferred_element_type=jnp.float32)
+        write(cols, factors[:rows] * kept(cols) + factors[rows:] * taken(cols).astype(jnp.float32))
+
+
 def own_kernel(first_ref, len_ref, q_ref, k_ref, v_ref, acc_ref, state_ref, ends_ref):
     block = pl.program_id(0)
 
@@ -92,7 +117,7 @@
 
     def emit(head, g, mixed, total, top):
         h = head * GROUPS + g
-        acc_ref[:, h * DH : (h + 1) * DH] = mixed
+        acc_ref[:, h * DH : (h + 1) * DH] = mixed * (1.0 / total)
         state[0] = jnp.where(lane == HQ + h, total, jnp.where(lane == h, top, state[0]))
 
     attend(pairs_of(q_ref), heads_of(k_ref), heads_of(v_ref), bias, emit)
@@ -131,16 +156,10 @@
             def emit(head, g, mixed, total, top):
                 h = head * GROUPS + g
                 slot_ref[:, h * DH : (h + 1) * DH] = (mixed * (1.0 / total)).astype(jnp.bfloat16)
-                level[0] = jnp.where(lane % HQ == h, top * RATE + jnp.log2(total), level[0])
+                level[0] = jnp.where(lane == h, top * RATE + jnp.log2(total), level[0])
 
             attend(pairs_of(q_ref), heads_of(k_ref), heads_of(v_ref), bias, emit)
-            rest = level[0]
-            tail = jnp.zeros((BQ, 128), jnp.float32)
-            for part in range(PARTS):
-                piece = rest.astype(jnp.bfloat16).astype(jnp.float32)
-                tail = jnp.where(lane // HQ == part, piece, tail)
-                rest = rest - piece
-            slot_ref[:, 2 * KV :] = tail.astype(jnp.bfloat16)
+            slot_ref[:, 2 * KV :] = in_parts(level[0])
 
 
 def column(state, lane):
@@ -164,18 +183,17 @@
     return emit, held
 
 
-def joined(state, fresh, normalised):
+def joined(state, fresh):
     top = jnp.maximum(state, fresh)
-    keep = jnp.exp2((state - top) * RATE)
+    before = jnp.exp2((state - top) * RATE) * heads_lanes(state, 1)
     take = jnp.exp2((fresh - top) * RATE)
-    before = keep * heads_lanes(state, 1)
     total = before + take * heads_lanes(fresh, 1)
     scale = 1.0 / total
-    return (before if normalised else keep) * scale, take * scale, top, total
+    return before * scale, take * scale, top, total
 
 
 def next_kernel(
-    first_ref, q_ref, k_ref, v_ref, acc_ref, state_ref, out_ref, new_acc_ref, new_state_ref, fresh_ref
+    first_ref, q_ref, k_ref, v_ref, acc_ref, state_ref, out_ref, new_acc_ref, new_state_ref, fresh_ref, spread_ref
 ):
     keys = k_ref.shape[0]
     first = first_ref[0].astype(jnp.float32)
@@ -186,30 +204,33 @@
 
     @pl.when(lowest >= first)
     def _():
-        scale = 1.0 / heads_lanes(state, 1)
-        for h in range(HQ):
-            cols = slice(h * DH, (h + 1) * DH)
-            out_ref[:, cols] = (acc_ref[:, cols] * column(scale, h)).astype(out_ref.dtype)
+        out_ref[...] = acc_ref[...].astype(out_ref.dtype)
         new_state_ref[...] = state
+
+    @pl.when((lowest < first) & (pl.program_id(0) == 0))
+    def _():
+        spread_ref[...] = spreader()
 
     @pl.when(lowest < first)
     def _():
         bias = jnp.where(float_iota((BQ, keys), 1) >= start - base, 0.0, HIDDEN)
         emit, held = collect(fresh_ref)
         attend(pairs_of(q_ref), heads_of(k_ref), heads_of(v_ref), bias, emit)
-        keep, take, top, total = joined(state, held[0], False)
+        keep, take, top, total = joined(state, held[0])
         lane = lax.broadcasted_iota(jnp.int32, (BQ, 128), 1)
         totals = pltpu.roll(total, HQ, 1)
         new_state_ref[...] = jnp.where(lane < HQ, top, jnp.where(lane < 2 * HQ, totals, state))
-        for h in range(HQ):
-            cols = slice(h * DH, (h + 1) * DH)
-            mixed = acc_ref[:, cols] * column(keep, h) + fresh_ref[:, cols] * column(take, h)
+
+        def write(cols, mixed):
             new_acc_ref[:, cols] = mixed
             out_ref[:, cols] = mixed.astype(out_ref.dtype)
 
+        mix(keep, lambda cols: acc_ref[:, cols], take, lambda cols: fresh_ref[:, cols], spread_ref, write)
+
 
 def last_kernel(
-    first_ref, q_ref, slot_ref, k_ref, v_ref, acc_ref, state_ref, prior_ref, out_ref, rows_ref, fresh_ref, sem
+    first_ref, q_ref, slot_ref, k_ref, v_ref, acc_ref, state_ref, prior_ref, out_ref, rows_ref, fresh_ref,
+    spread_ref, sem,
 ):
     keys = k_ref.shape[0]
     first = first_ref[0].astype(jnp.float32)
@@ -226,11 +247,11 @@
         rows = pl.ds(pl.multiple_of(block * BQ, BQ), BQ)
         return pltpu.make_async_copy(rows_ref.at[rows, :], out_ref.at[rows, :], sem.at[block])
 
-    def write(rows, keep, take, added_ref, added_rows):
-        for h in range(HQ):
-            cols = slice(h * DH, (h + 1) * DH)
-            mixed = acc_ref[rows, cols] * column(keep, h) + added_ref[added_rows, cols].astype(jnp.float32) * column(take, h)
+    def write(rows, keep, take, added):
+        def put(cols, mixed):
             rows_ref[rows, cols] = mixed.astype(rows_ref.dtype)
+
+        mix(keep, lambda cols: acc_ref[rows, cols], take, added, spread_ref, put)
 
     def merge(block, get_keys, get_values, count, origin):
         rows = pl.ds(pl.multiple_of(block * BQ, BQ), BQ)
@@ -238,8 +259,8 @@
         bias = jnp.where(float_iota((BQ, count), 1) >= column(state, START) - origin, 0.0, HIDDEN)
         emit, held = collect(fresh_ref)
         attend(pairs_of(q_ref, rows), get_keys, get_values, bias, emit)
-        keep, take, _, _ = joined(state, held[0], True)
-        write(rows, keep, take, fresh_ref, slice(None))
+        keep, take, _, _ = joined(state, held[0])
+        write(rows, keep, take, lambda cols: fresh_ref[:, cols])
 
     def combine(block):
         rows = pl.ds(pl.multiple_of(block * BQ, BQ), BQ)
@@ -251,7 +272,11 @@
         before = jnp.exp2(here - top) * heads_lanes(state, 1)
         take = jnp.exp2(there - top)
         scale = 1.0 / (before + take)
-        write(rows, before * scale, take * scale, slot_ref, rows)
+        write(rows, before * scale, take * scale, lambda cols: slot_ref[rows, cols])
+
+    @pl.when(earliest(0) < base)
+    def _():
+        spread_ref[...] = spreader()
 
     @pl.loop(0, blocks)
     def _(block):
@@ -369,7 +394,7 @@
         in_specs=[SMEM, rows_of(WIDE), WHOLE, WHOLE, rows_of(WIDE), rows_of(128)],
         out_specs=[rows_of(WIDE), rows_of(WIDE), rows_of(128)],
         out_shape=[bf16(rows, WIDE), f32(rows, WIDE), f32(rows, 128)],
-        scratch_shapes=[pltpu.VMEM((BQ, WIDE), jnp.float32)],
+        scratch_shapes=[pltpu.VMEM((BQ, WIDE), jnp.float32), pltpu.VMEM((128, WIDE), jnp.bfloat16)],
         cost_estimate=cost(rows, keys.shape[0]),
         compiler_params=PARAMS,
         name="next_shard",
@@ -387,6 +412,7 @@
         scratch_shapes=[
             pltpu.VMEM((rows, WIDE), jnp.bfloat16),
             pltpu.VMEM((BQ, WIDE), jnp.float32),
+            pltpu.VMEM((128, WIDE), jnp.bfloat16),
             pltpu.SemaphoreType.DMA((rows // BQ,)),
         ],
         input_output_aliases={7: 0},

time: 75.2 us -> 73.6 us (0.979)
  Pallas kernels: 29.1 us -> 27.8 us
    pallas_call x1, Pallas kernels: 11.9 us -> 11.2 us  [next_stage(): pl.pallas_call(next_kernel, grid=(rows // BQ,), in_specs=[SMEM, rows_of(W...]
where the time goes in v4:
time: 73.6 us; the launch traced here: 73.3 us
  Pallas kernels  27.8 us (38%)
  waiting for transfers between devices  27.6 us (38%)
  starting transfers between devices  16.2 us (22%)
  local copies, waits for them, and re-layouts  1.61 us (2%)
    ppermute x6, waiting for transfers between devices, hop(): return lax.ppermute(array, 'cp', pairs)  27.6 us
    ppermute x6, starting transfers between devices, hop(): return lax.ppermute(array, 'cp', pairs)  16.2 us
    pallas_call x1, Pallas kernels, next_stage(): pl.pallas_call(next_kernel, grid=(rows // BQ,), in_specs=[SMEM, rows_of(W...  11.2 us
    pallas_call x1, Pallas kernels, last_stage(): pl.pallas_call(last_kernel, in_specs=[SMEM, WHOLE, WHOLE, WHOLE, WHOLE, W...  7.18 us
    pallas_call x1, Pallas kernels, own_stage(): pl.pallas_call(own_kernel, grid=(rows // BQ,), in_specs=[SMEM, WHOLE, row...  6.59 us
    pallas_call x1, Pallas kernels, back_stage(): pl.pallas_call(back_kernel, grid=(SLOT // BQ,), in_specs=[SMEM, WHOLE, ro...  1.79 us
    unnamed x10, local copies, waits for them, and re-layouts  1.61 us
  transfers between devices with their start and end apart: 6, of which 3 were waited for; matrix products, arithmetic and copies ran while one was open for 0% of the time, Pallas kernels for 27%

profile of v4, /device:TPU:20, one launch (start us, length us, event | category | flops | bytes accessed | tf_op | source)
XLA Modules:
  0.0 73.3 jit_solution(11833141498811030738)
XLA Ops:
  0.0 0.0 copy-start
  0.0 1.6 %copy-done = bf16[512,2048]{1,0:T(8,128)(2,1)S(1)} copy-done((bf16[512,2048]{1,0:T(8,128)(2,1)S(1)}, bf16[512,2048]{1,0:T(8,128)(2,1)}, u32[]{:S(2)}) %copy-start) | copy-done | bytes 2097176
  1.6 0.0 copy-start.2
  1.6 0.0 copy-start.3
  1.6 0.0 copy-start.4
  1.6 1.0 %leading_rows.1 = bf16[256,2048]{1,0:T(8,128)(2,1)} custom-call(bf16[512,2048]{1,0:T(8,128)(2,1)S(1)} %copy-done), custom_call_target="tpu_custom_call" | custom-call | tf_op jit(solution)/shard_map/leading_rows/pallas_call | solution.py:363
  2.6 7.7 %collective-permute-start = (bf16[256,2048]{1,0:T(8,128)(2,1)}, bf16[256,2048]{1,0:T(8,128)(2,1)}, u32[]{:S(2)}, u32[]{:S(2)}) collective-permute-start(bf16[256,2048]{1,0:T(8,128)(2,1)} %leading_rows.1), channel_id=1, source_target_pairs={{2,0},{4,2},{6,4},{8,6},{10,8},{12,10},{14,12},{16,14},{18,16},{20... | collective-permute-start | bytes 3145736 | tf_op jit(solution)/shard_map/ppermute | solution.py:433
  10.4 0.0 copy-done.2
  10.4 1.9 %collective-permute-start.2 = (bf16[512,1024]{1,0:T(8,128)(2,1)S(1)}, bf16[512,1024]{1,0:T(8,128)(2,1)S(1)}, u32[]{:S(2)}, u32[]{:S(2)}) collective-permute-start(bf16[512,1024]{1,0:T(8,128)(2,1)S(1)} %copy-done.2), channel_id=1, source_target_pairs={{0,1},{1,2},{2,3},{3,4},{4,5},{5,6},{6,7},{7,8},{8,9},{9,10},{10,1... | collective-permute-start | bytes 3145736 | tf_op jit(solution)/shard_map/ppermute | solution.py:433
  12.3 0.0 copy-done.3
  12.3 1.9 %collective-permute-start.4 = (bf16[512,1024]{1,0:T(8,128)(2,1)S(1)}, bf16[512,1024]{1,0:T(8,128)(2,1)}, u32[]{:S(2)}, u32[]{:S(2)}) collective-permute-start(bf16[512,1024]{1,0:T(8,128)(2,1)S(1)} %copy-done.3), channel_id=1, source_target_pairs={{0,1},{1,2},{2,3},{3,4},{4,5},{5,6},{6,7},{7,8},{8,9},{9,10},{10,1... | collective-permute-start | bytes 3145736 | tf_op jit(solution)/shard_map/ppermute | solution.py:433
  14.3 8.7 %collective-permute-done.q_ref = bf16[256,2048]{1,0:T(8,128)(2,1)} collective-permute-done((bf16[256,2048]{1,0:T(8,128)(2,1)}, bf16[256,2048]{1,0:T(8,128)(2,1)}, u32[]{:S(2)}, u32[]{:S(2)}) %collective-permute-start) | collective-permute-done | bytes 1048608 | tf_op jit(solution)/shard_map/ppermute | solution.py:433
  23.0 0.0 copy-done.4
  23.0 0.0 copy-start.1
  23.0 1.8 %back_shard.1 = bf16[256,2176]{1,0:T(8,128)(2,1)S(1)} custom-call(s32[1]{0:T(128)} %bitcast.first_ref, s32[1,256]{1,0:T(1,128)S(1)} %bitcast.2, bf16[256,2048]{1,0:T(8,128)(2,1)} %collective-permute-done.q_ref, bf16[512,1024]{1,0:T(8,128)(2,1)S(1)} %copy-done.2, bf16[512,1024]{1,0:T(8,128)(2,1)S(1)} %copy-done.3), custom_call_target="tpu_custom_call" | custom-call | flops 1073741824 | bytes 4194304 | tf_op jit(solution)/shard_map/back_shard/pallas_call | solution.py:376
  24.8 1.9 %collective-permute-start.1 = (bf16[256,2176]{1,0:T(8,128)(2,1)S(1)}, bf16[256,2176]{1,0:T(8,128)(2,1)S(1)}, u32[]{:S(2)}, u32[]{:S(2)}) collective-permute-start(bf16[256,2176]{1,0:T(8,128)(2,1)S(1)} %back_shard.1), channel_id=1, source_target_pairs={{0,2},{2,4},{4,6},{6,8},{8,10},{10,12},{12,14},{14,16},{16,18},{18... | collective-permute-start | bytes 3342344 | tf_op jit(solution)/shard_map/ppermute | solution.py:433
  26.7 1.9 %collective-permute-done.2.k_ref = bf16[512,1024]{1,0:T(8,128)(2,1)S(1)} collective-permute-done((bf16[512,1024]{1,0:T(8,128)(2,1)S(1)}, bf16[512,1024]{1,0:T(8,128)(2,1)S(1)}, u32[]{:S(2)}, u32[]{:S(2)}) %collective-permute-start.2) | collective-permute-done | bytes 1048608 | tf_op jit(solution)/shard_map/ppermute | solution.py:433
  28.6 1.3 %collective-permute-start.3 = (bf16[512,1024]{1,0:T(8,128)(2,1)S(1)}, bf16[512,1024]{1,0:T(8,128)(2,1)S(1)}, u32[]{:S(2)}, u32[]{:S(2)}) collective-permute-start(bf16[512,1024]{1,0:T(8,128)(2,1)S(1)} %collective-permute-done.2.k_ref), channel_id=1, source_target_pairs={{0,1},{2,3},{4,5},{6,7},{8,9},{10,11},{12,13},{14,15},{16,17},{18,... | collective-permute-start | bytes 3145736 | tf_op jit(solution)/shard_map/ppermute | solution.py:433
  30.0 17.0 %collective-permute-done.4.v_ref = bf16[512,1024]{1,0:T(8,128)(2,1)} collective-permute-done((bf16[512,1024]{1,0:T(8,128)(2,1)S(1)}, bf16[512,1024]{1,0:T(8,128)(2,1)}, u32[]{:S(2)}, u32[]{:S(2)}) %collective-permute-start.4) | collective-permute-done | bytes 1048608 | tf_op jit(solution)/shard_map/ppermute | solution.py:433
  47.0 1.3 %collective-permute-start.5 = (bf16[512,1024]{1,0:T(8,128)(2,1)}, bf16[512,1024]{1,0:T(8,128)(2,1)S(1)}, u32[]{:S(2)}, u32[]{:S(2)}) collective-permute-start(bf16[512,1024]{1,0:T(8,128)(2,1)} %collective-permute-done.4.v_ref), channel_id=1, source_target_pairs={{0,1},{2,3},{4,5},{6,7},{8,9},{10,11},{12,13},{14,15},{16,17},{18,... | collective-permute-start | bytes 3145736 | tf_op jit(solution)/shard_map/ppermute | solution.py:433
  48.3 0.0 copy-done.1
  48.3 6.6 %own_shard.1 = (f32[512,2048]{1,0:T(8,128)S(1)}, f32[512,128]{1,0:T(8,128)S(1)}) custom-call(s32[1]{0:T(128)} %bitcast.first_ref, s32[1,256]{1,0:T(1,128)S(1)} %bitcast.3, bf16[512,2048]{1,0:T(8,128)(2,1)S(1)} %copy-done.1, bf16[512,1024]{1,0:T(8,128)(2,1)S(1)} %copy-done.2, bf16[512,1024]{1,0:T(8,128)(2,1)S(1)} %copy-done.3), custom_call_target="tpu_custom_call" | custom-call | flops 2147483648 | bytes 8388608 | tf_op jit(solution)/shard_map/own_shard/pallas_call | solution.py:343
  54.9 11.2 %next_shard.1 = (bf16[512,2048]{1,0:T(8,128)(2,1)}, f32[512,2048]{1,0:T(8,128)S(1)}, f32[512,128]{1,0:T(8,128)S(1)}) custom-call(s32[1]{0:T(128)} %bitcast.first_ref, bf16[512,2048]{1,0:T(8,128)(2,1)S(1)} %copy-done.1, bf16[512,1024]{1,0:T(8,128)(2,1)S(1)} %collective-permute-done.2.k_ref, bf16[512,1024]{1,0:T(8,128)(2,1)} %collective-permute-done.4.v_ref, ...), custom_call_target="tpu_custom_call" | custom-call | flops 2147483648 | bytes 8388608 | tf_op jit(solution)/shard_map/next_shard/pallas_call | solution.py:391
  66.1 0.0 collective-permute-done.3.k_ref
  66.1 0.0 collective-permute-done.5.v_ref
  66.1 0.0 collective-permute-done.1.slot_ref
  66.1 7.2 %last_shard.1 = bf16[512,2048]{1,0:T(8,128)(2,1)} custom-call(s32[1]{0:T(128)} %bitcast.first_ref, bf16[512,2048]{1,0:T(8,128)(2,1)S(1)} %copy-done.1, bf16[256,2176]{1,0:T(8,128)(2,1)S(1)} %collective-permute-done.1.slot_ref, bf16[512,1024]{1,0:T(8,128)(2,1)S(1)} %collective-permute-done.3.k_ref, ...), custom_call_target="tpu_custom_call", output_to_operand_aliasing={{}: (7, {})} | custom-call | flops 1073741824 | bytes 8388608 | tf_op jit(solution)/shard_map/last_shard/pallas_call | solution.py:407
Async XLA Ops:
  0.0 1.6 %copy-start = (bf16[512,2048]{1,0:T(8,128)(2,1)S(1)}, bf16[512,2048]{1,0:T(8,128)(2,1)}, u32[]{:S(2)}) copy-start(bf16[512,2048]{1,0:T(8,128)(2,1)} %q_ref.5) | copy-start | bytes 6291460
  1.6 8.8 %copy-start.2 = (bf16[512,1024]{1,0:T(8,128)(2,1)S(1)}, bf16[512,1024]{1,0:T(8,128)(2,1)}, u32[]{:S(2)}) copy-start(bf16[512,1024]{1,0:T(8,128)(2,1)} %k_ref.3) | copy-start | bytes 3145732
  1.6 10.7 %copy-start.3 = (bf16[512,1024]{1,0:T(8,128)(2,1)S(1)}, bf16[512,1024]{1,0:T(8,128)(2,1)}, u32[]{:S(2)}) copy-start(bf16[512,1024]{1,0:T(8,128)(2,1)} %v_ref.3) | copy-start | bytes 3145732
  1.6 21.4 %copy-start.4 = (s32[256]{0:T(256)S(1)}, s32[256]{0:T(256)}, u32[]{:S(2)}) copy-start(s32[256]{0:T(256)} %param.7) | copy-start | bytes 3076
  2.6 20.3 %collective-permute-start = (bf16[256,2048]{1,0:T(8,128)(2,1)}, bf16[256,2048]{1,0:T(8,128)(2,1)}, u32[]{:S(2)}, u32[]{:S(2)}) collective-permute-start(bf16[256,2048]{1,0:T(8,128)(2,1)} %leading_rows.1), channel_id=1, source_target_pairs={{2,0},{4,2},{6,4},{8,6},{10,8},{12,10},{14,12},{16,14},{18,16},{20... | collective-permute-start | bytes 3145736 | tf_op jit(solution)/shard_map/ppermute | solution.py:433
  10.4 18.2 %collective-permute-start.2 = (bf16[512,1024]{1,0:T(8,128)(2,1)S(1)}, bf16[512,1024]{1,0:T(8,128)(2,1)S(1)}, u32[]{:S(2)}, u32[]{:S(2)}) collective-permute-start(bf16[512,1024]{1,0:T(8,128)(2,1)S(1)} %copy-done.2), channel_id=1, source_target_pairs={{0,1},{1,2},{2,3},{3,4},{4,5},{5,6},{6,7},{7,8},{8,9},{9,10},{10,1... | collective-permute-start | bytes 3145736 | tf_op jit(solution)/shard_map/ppermute | solution.py:433
  12.3 34.7 %collective-permute-start.4 = (bf16[512,1024]{1,0:T(8,128)(2,1)S(1)}, bf16[512,1024]{1,0:T(8,128)(2,1)}, u32[]{:S(2)}, u32[]{:S(2)}) collective-permute-start(bf16[512,1024]{1,0:T(8,128)(2,1)S(1)} %copy-done.3), channel_id=1, source_target_pairs={{0,1},{1,2},{2,3},{3,4},{4,5},{5,6},{6,7},{7,8},{8,9},{9,10},{10,1... | collective-permute-start | bytes 3145736 | tf_op jit(solution)/shard_map/ppermute | solution.py:433
  23.0 25.3 %copy-start.1 = (bf16[512,2048]{1,0:T(8,128)(2,1)S(1)}, bf16[512,2048]{1,0:T(8,128)(2,1)}, u32[]{:S(2)}) copy-start(bf16[512,2048]{1,0:T(8,128)(2,1)} %q_ref.5) | copy-start | bytes 6291460
  24.8 41.3 %collective-permute-start.1 = (bf16[256,2176]{1,0:T(8,128)(2,1)S(1)}, bf16[256,2176]{1,0:T(8,128)(2,1)S(1)}, u32[]{:S(2)}, u32[]{:S(2)}) collective-permute-start(bf16[256,2176]{1,0:T(8,128)(2,1)S(1)} %back_shard.1), channel_id=1, source_target_pairs={{0,2},{2,4},{4,6},{6,8},{8,10},{10,12},{12,14},{14,16},{16,18},{18... | collective-permute-start | bytes 3342344 | tf_op jit(solution)/shard_map/ppermute | solution.py:433
  28.6 37.5 %collective-permute-start.3 = (bf16[512,1024]{1,0:T(8,128)(2,1)S(1)}, bf16[512,1024]{1,0:T(8,128)(2,1)S(1)}, u32[]{:S(2)}, u32[]{:S(2)}) collective-permute-start(bf16[512,1024]{1,0:T(8,128)(2,1)S(1)} %collective-permute-done.2.k_ref), channel_id=1, source_target_pairs={{0,1},{2,3},{4,5},{6,7},{8,9},{10,11},{12,13},{14,15},{16,17},{18,... | collective-permute-start | bytes 3145736 | tf_op jit(solution)/shard_map/ppermute | solution.py:433
  47.0 19.1 %collective-permute-start.5 = (bf16[512,1024]{1,0:T(8,128)(2,1)}, bf16[512,1024]{1,0:T(8,128)(2,1)S(1)}, u32[]{:S(2)}, u32[]{:S(2)}) collective-permute-start(bf16[512,1024]{1,0:T(8,128)(2,1)} %collective-permute-done.4.v_ref), channel_id=1, source_target_pairs={{0,1},{2,3},{4,5},{6,7},{8,9},{10,11},{12,13},{14,15},{16,17},{18,... | collective-permute-start | bytes 3145736 | tf_op jit(solution)/shard_map/ppermute | solution.py:433

commit v5 on v4

--- a/solution.py
+++ b/solution.py
@@ -19,7 +19,7 @@
 RATE = math.log2(math.e) * 144.0 ** -0.5
 START = 2 * HQ
 PARTS = 3
-VMEM = 24 << 20
+VMEM = 16 << 20
 INTERPRET = False
 
 SLOT = 256
@@ -98,12 +98,13 @@
         write(cols, factors[:rows] * kept(cols) + factors[rows:] * taken(cols).astype(jnp.float32))
 
 
-def own_kernel(first_ref, len_ref, q_ref, k_ref, v_ref, acc_ref, state_ref, ends_ref):
+def own_kernel(first_ref, len_ref, q_ref, k_ref, v_ref, acc_ref, state_ref, spread_ref, out_ref, ends_ref):
     block = pl.program_id(0)
 
     @pl.when(block == 0)
     def _():
         ends_ref[...] = document_ends(len_ref[...])
+        spread_ref[...] = spreader()
 
     ends = ends_ref[...]
     keys = k_ref.shape[0]
@@ -117,7 +118,10 @@
 
     def emit(head, g, mixed, total, top):
         h = head * GROUPS + g
-        acc_ref[:, h * DH : (h + 1) * DH] = mixed * (1.0 / total)
+        cols = slice(h * DH, (h + 1) * DH)
+        mixed = mixed * (1.0 / total)
+        acc_ref[:, cols] = mixed
+        out_ref[:, cols] = mixed.astype(out_ref.dtype)
         state[0] = jnp.where(lane == HQ + h, total, jnp.where(lane == h, top, state[0]))
 
     attend(pairs_of(q_ref), heads_of(k_ref), heads_of(v_ref), bias, emit)
@@ -136,16 +140,16 @@
         edge = here + 2 * keys
         start = jnp.max(jnp.where(ends <= edge, ends, 0.0))
         right = jnp.min(jnp.where(ends > edge, ends, edge + edge)) - edge
-        by_keys = here + keys - start <= SLOT
-
-        @pl.when(by_keys)
+        reached = start < here + keys
+        by_keys = right > SLOT
+
+        @pl.when(reached & by_keys)
         def _():
             rows = pl.ds(keys - SLOT + block * BQ, BQ)
             slot_ref[:, :KV] = k_ref[rows, :]
             slot_ref[:, KV : 2 * KV] = v_ref[rows, :]
-            slot_ref[:, 2 * KV :] = jnp.zeros((BQ, 128), jnp.bfloat16)
-
-        @pl.when(jnp.logical_not(by_keys))
+
+        @pl.when(reached & jnp.logical_not(by_keys) & ((block * BQ).astype(jnp.float32) < right))
         def _():
             row = float_iota((BQ, 1), 0) + (block * BQ).astype(jnp.float32)
             col = float_iota((BQ, keys), 1)
@@ -192,45 +196,67 @@
     return before * scale, take * scale, top, total
 
 
+def rows_at(block):
+    return pl.ds(pl.multiple_of(block * BQ, BQ), BQ)
+
+
+def writer(done_ref, out_ref, sem):
+    def copy(block):
+        return pltpu.make_async_copy(done_ref.at[rows_at(block), :], out_ref.at[rows_at(block), :], sem.at[block])
+
+    return copy
+
+
 def next_kernel(
-    first_ref, q_ref, k_ref, v_ref, acc_ref, state_ref, out_ref, new_acc_ref, new_state_ref, fresh_ref, spread_ref
+    first_ref, q_ref, k_ref, v_ref, acc_ref, state_ref, spread_ref, prior_ref, out_ref, new_acc_ref, new_state_ref,
+    done_ref, fresh_ref, sem,
 ):
     keys = k_ref.shape[0]
     first = first_ref[0].astype(jnp.float32)
     base = first - keys
-    state = state_ref[...]
-    start = column(state, START)
-    lowest = jnp.min(start)
-
-    @pl.when(lowest >= first)
-    def _():
-        out_ref[...] = acc_ref[...].astype(out_ref.dtype)
-        new_state_ref[...] = state
-
-    @pl.when((lowest < first) & (pl.program_id(0) == 0))
-    def _():
-        spread_ref[...] = spreader()
-
-    @pl.when(lowest < first)
-    def _():
-        bias = jnp.where(float_iota((BQ, keys), 1) >= start - base, 0.0, HIDDEN)
-        emit, held = collect(fresh_ref)
-        attend(pairs_of(q_ref), heads_of(k_ref), heads_of(v_ref), bias, emit)
-        keep, take, top, total = joined(state, held[0])
-        lane = lax.broadcasted_iota(jnp.int32, (BQ, 128), 1)
-        totals = pltpu.roll(total, HQ, 1)
-        new_state_ref[...] = jnp.where(lane < HQ, top, jnp.where(lane < 2 * HQ, totals, state))
-
-        def write(cols, mixed):
-            new_acc_ref[:, cols] = mixed
-            out_ref[:, cols] = mixed.astype(out_ref.dtype)
-
-        mix(keep, lambda cols: acc_ref[:, cols], take, lambda cols: fresh_ref[:, cols], spread_ref, write)
+    blocks = q_ref.shape[0] // BQ
+    copy = writer(done_ref, out_ref, sem)
+
+    def earliest(block):
+        return jnp.min(state_ref[pl.ds(block * BQ, 8), START : START + 1])
+
+    def finishes(block):
+        return (earliest(block) < first) & (earliest(block) >= base)
+
+    @pl.loop(0, blocks)
+    def _(block):
+        @pl.when(earliest(block) < first)
+        def _():
+            rows = rows_at(block)
+            state = state_ref[rows, :]
+            bias = jnp.where(float_iota((BQ, keys), 1) >= column(state, START) - base, 0.0, HIDDEN)
+            emit, held = collect(fresh_ref)
+            attend(pairs_of(q_ref, rows), heads_of(k_ref), heads_of(v_ref), bias, emit)
+            keep, take, top, total = joined(state, held[0])
+            lane = lax.broadcasted_iota(jnp.int32, (BQ, 128), 1)
+            totals = pltpu.roll(total, HQ, 1)
+            new_state_ref[rows, :] = jnp.where(lane < HQ, top, jnp.where(lane < 2 * HQ, totals, state))
+
+            def write(cols, mixed):
+                new_acc_ref[rows, cols] = mixed
+                done_ref[rows, cols] = mixed.astype(done_ref.dtype)
+
+            mix(keep, lambda cols: acc_ref[rows, cols], take, lambda cols: fresh_ref[:, cols], spread_ref, write)
+
+        @pl.when(finishes(block))
+        def _():
+            copy(block).start()
+
+    @pl.loop(0, blocks)
+    def _(block):
+        @pl.when(finishes(block))
+        def _():
+            copy(block).wait()
 
 
 def last_kernel(
-    first_ref, q_ref, slot_ref, k_ref, v_ref, acc_ref, state_ref, prior_ref, out_ref, rows_ref, fresh_ref,
-    spread_ref, sem,
+    first_ref, q_ref, slot_ref, k_ref, v_ref, acc_ref, state_ref, starts_ref, spread_ref, prior_ref, out_ref,
+    done_ref, fresh_ref, sem,
 ):
     keys = k_ref.shape[0]
     first = first_ref[0].astype(jnp.float32)
@@ -238,32 +264,30 @@
     even = jnp.logical_not(odd)
     base = first - keys
     blocks = q_ref.shape[0] // BQ
-    by_keys = base - jnp.min(state_ref[:8, START : START + 1]) <= SLOT
+    by_keys = jnp.min(starts_ref[SLOT : SLOT + 8, START : START + 1]) < first
+    copy = writer(done_ref, out_ref, sem)
 
     def earliest(block):
-        return jnp.min(state_ref[pl.ds(block * BQ, 8), START : START + 1])
-
-    def copy(block):
-        rows = pl.ds(pl.multiple_of(block * BQ, BQ), BQ)
-        return pltpu.make_async_copy(rows_ref.at[rows, :], out_ref.at[rows, :], sem.at[block])
+        return jnp.min(starts_ref[pl.ds(block * BQ, 8), START : START + 1])
 
     def write(rows, keep, take, added):
         def put(cols, mixed):
-            rows_ref[rows, cols] = mixed.astype(rows_ref.dtype)
+            done_ref[rows, cols] = mixed.astype(done_ref.dtype)
 
         mix(keep, lambda cols: acc_ref[rows, cols], take, added, spread_ref, put)
 
-    def merge(block, get_keys, get_values, count, origin):
-        rows = pl.ds(pl.multiple_of(block * BQ, BQ), BQ)
+    def merge(block, ref_k, ref_v, at, skip, count, origin):
+        rows = rows_at(block)
         state = state_ref[rows, :]
+        part = slice(skip, skip + count)
         bias = jnp.where(float_iota((BQ, count), 1) >= column(state, START) - origin, 0.0, HIDDEN)
         emit, held = collect(fresh_ref)
-        attend(pairs_of(q_ref, rows), get_keys, get_values, bias, emit)
+        attend(pairs_of(q_ref, rows), heads_of(ref_k, part), heads_of(ref_v, part, at), bias, emit)
         keep, take, _, _ = joined(state, held[0])
         write(rows, keep, take, lambda cols: fresh_ref[:, cols])
 
     def combine(block):
-        rows = pl.ds(pl.multiple_of(block * BQ, BQ), BQ)
+        rows = rows_at(block)
         state = state_ref[rows, :]
         parts = slot_ref[rows, 2 * KV :].astype(jnp.float32)
         there = sum(heads_lanes(parts, part) for part in reversed(range(PARTS)))
@@ -274,28 +298,28 @@
         scale = 1.0 / (before + take)
         write(rows, before * scale, take * scale, lambda cols: slot_ref[rows, cols])
 
-    @pl.when(earliest(0) < base)
-    def _():
-        spread_ref[...] = spreader()
-
     @pl.loop(0, blocks)
     def _(block):
         start = earliest(block)
         needed = start < base
         far = start < base - SLOT
+        near = start >= base - BQ
 
         @pl.when(odd & far)
         def _():
-            merge(block, heads_of(k_ref), heads_of(v_ref), keys, base - keys)
+            merge(block, k_ref, v_ref, 0, 0, keys, base - keys)
 
         @pl.when(odd & needed & jnp.logical_not(far))
         def _():
-            near = slice(keys - SLOT, keys)
-            merge(block, heads_of(k_ref, near), heads_of(v_ref, near), SLOT, base - SLOT)
-
-        @pl.when(even & needed & by_keys)
-        def _():
-            merge(block, heads_of(slot_ref), heads_of(slot_ref, at=KV), SLOT, base - SLOT)
+            merge(block, k_ref, v_ref, 0, keys - SLOT, SLOT, base - SLOT)
+
+        @pl.when(even & needed & by_keys & near)
+        def _():
+            merge(block, slot_ref, slot_ref, KV, SLOT - BQ, BQ, base - BQ)
+
+        @pl.when(even & needed & by_keys & jnp.logical_not(near))
+        def _():
+            merge(block, slot_ref, slot_ref, KV, 0, SLOT, base - SLOT)
 
         @pl.when(even & needed & jnp.logical_not(by_keys) & (block * BQ < SLOT))
         def _():
@@ -318,6 +342,7 @@
 
 SMEM = pl.BlockSpec(memory_space=pltpu.SMEM)
 WHOLE = pl.BlockSpec(memory_space=pltpu.VMEM)
+ANY = pl.BlockSpec(memory_space=pl.ANY)
 WIDE = HQ * DH
 
 
@@ -344,8 +369,8 @@
         own_kernel,
         grid=(rows // BQ,),
         in_specs=[SMEM, WHOLE, rows_of(WIDE), WHOLE, WHOLE],
-        out_specs=[rows_of(WIDE), rows_of(128)],
-        out_shape=[f32(rows, WIDE), f32(rows, 128)],
+        out_specs=[rows_of(WIDE), rows_of(128), WHOLE, rows_of(WIDE)],
+        out_shape=[f32(rows, WIDE), f32(rows, 128), bf16(128, WIDE), bf16(rows, WIDE)],
         scratch_shapes=[pltpu.VMEM(lengths.shape, jnp.float32)],
         cost_estimate=cost(rows, keys.shape[0]),
         compiler_params=PARAMS,
@@ -386,41 +411,44 @@
     )(first, lengths, queries, keys, values)
 
 
-def next_stage(first, queries, keys, values, acc, state):
+def writing(rows):
+    return [
+        pltpu.VMEM((rows, WIDE), jnp.bfloat16),
+        pltpu.VMEM((BQ, WIDE), jnp.float32),
+        pltpu.SemaphoreType.DMA((rows // BQ,)),
+    ]
+
+
+def next_stage(first, queries, keys, values, acc, state, spread, prior):
     rows = queries.shape[0]
     return pl.pallas_call(
         next_kernel,
-        grid=(rows // BQ,),
-        in_specs=[SMEM, rows_of(WIDE), WHOLE, WHOLE, rows_of(WIDE), rows_of(128)],
-        out_specs=[rows_of(WIDE), rows_of(WIDE), rows_of(128)],
+        in_specs=[SMEM] + [WHOLE] * 6 + [ANY],
+        out_specs=[ANY, WHOLE, WHOLE],
         out_shape=[bf16(rows, WIDE), f32(rows, WIDE), f32(rows, 128)],
-        scratch_shapes=[pltpu.VMEM((BQ, WIDE), jnp.float32), pltpu.VMEM((128, WIDE), jnp.bfloat16)],
+        scratch_shapes=writing(rows),
+        input_output_aliases={7: 0},
         cost_estimate=cost(rows, keys.shape[0]),
         compiler_params=PARAMS,
         name="next_shard",
         interpret=INTERPRET,
-    )(first, queries, keys, values, acc, state)
-
-
-def last_stage(first, queries, slot, keys, values, acc, state, prior):
+    )(first, queries, keys, values, acc, state, spread, prior)
+
+
+def last_stage(first, queries, slot, keys, values, acc, state, starts, spread, prior):
     rows = queries.shape[0]
     return pl.pallas_call(
         last_kernel,
-        in_specs=[SMEM, WHOLE, WHOLE, WHOLE, WHOLE, WHOLE, WHOLE, pl.BlockSpec(memory_space=pl.ANY)],
-        out_specs=pl.BlockSpec(memory_space=pl.ANY),
+        in_specs=[SMEM] + [WHOLE] * 8 + [ANY],
+        out_specs=ANY,
         out_shape=bf16(rows, WIDE),
-        scratch_shapes=[
-            pltpu.VMEM((rows, WIDE), jnp.bfloat16),
-            pltpu.VMEM((BQ, WIDE), jnp.float32),
-            pltpu.VMEM((128, WIDE), jnp.bfloat16),
-            pltpu.SemaphoreType.DMA((rows // BQ,)),
-        ],
-        input_output_aliases={7: 0},
+        scratch_shapes=writing(rows),
+        input_output_aliases={9: 0},
         cost_estimate=cost(rows, SLOT),
         compiler_params=PARAMS,
         name="last_shard",
         interpret=INTERPRET,
-    )(first, queries, slot, keys, values, acc, state, prior)
+    )(first, queries, slot, keys, values, acc, state, starts, spread, prior)
 
 
 def on_device(queries, keys, values, doc_lengths):
@@ -436,14 +464,14 @@
     one_k = hop(keys, onward)
     one_v = hop(values, onward)
     guests = hop(leading_rows(queries, SLOT), [(i, i - 2) for i in evens if i])
-    acc, state = own_stage(first, lengths, queries, keys, values)
+    acc, state, spread, out = own_stage(first, lengths, queries, keys, values)
     slot = back_stage(first, lengths, guests, keys, values)
     slot = hop(slot, [(i, i + 2) for i in evens if i + 2 < count])
     across = [(i, i + 1) for i in evens]
     two_k = hop(one_k, across)
     two_v = hop(one_v, across)
-    out, acc, state_next = next_stage(first, queries, one_k, one_v, acc, state)
-    out = last_stage(first, queries, slot, two_k, two_v, acc, state_next, out)
+    out, acc, new_state = next_stage(first, queries, one_k, one_v, acc, state, spread, out)
+    out = last_stage(first, queries, slot, two_k, two_v, acc, new_state, state, spread, out)
     return out
 
 

time: 73.6 us -> 77.2 us (1.049)
  waiting for transfers between devices: 27.6 us -> 29.9 us
  Pallas kernels: 27.8 us -> 28.6 us
    ppermute x6, waiting for transfers between devices: 27.6 us -> 29.9 us  [hop(): return lax.ppermute(array, 'cp', pairs)]
    pallas_call x1, Pallas kernels: 1.79 us -> 0.53 us  [back_stage(): pl.pallas_call(back_kernel, grid=(SLOT // BQ,), in_specs=[SMEM, WHOLE, ro...]
    pallas_call x2, Pallas kernels: 18.3 us -> 19.5 us  [the longest x1 11.5 us: next_stage(): pl.pallas_call(next_kernel, in_specs=[SMEM] + [WHOLE] * 6 + [ANY], out_sp...]
    pallas_call x1, Pallas kernels: 6.59 us -> 7.6 us  [own_stage(): pl.pallas_call(own_kernel, grid=(rows // BQ,), in_specs=[SMEM, WHOLE, row...]
  transfers between devices with their start and end apart: 6 -> 6, of which waited for: 3 -> 3; matrix products, arithmetic and copies ran while one was open for 0% -> 0% of each run, Pallas kernels for 27% -> 25%
where the time goes in v5:
time: 77.2 us; the launch traced here: 77 us
  waiting for transfers between devices  29.9 us (39%)
  Pallas kernels  28.6 us (37%)
  starting transfers between devices  16.5 us (21%)
  local copies, waits for them, and re-layouts  1.61 us (2%)
    ppermute x6, waiting for transfers between devices, hop(): return lax.ppermute(array, 'cp', pairs)  29.9 us
    ppermute x6, starting transfers between devices, hop(): return lax.ppermute(array, 'cp', pairs)  16.5 us
    pallas_call x1, Pallas kernels, next_stage(): pl.pallas_call(next_kernel, in_specs=[SMEM] + [WHOLE] * 6 + [ANY], out_sp...  11.5 us
    pallas_call x1, Pallas kernels, last_stage(): pl.pallas_call(last_kernel, in_specs=[SMEM] + [WHOLE] * 8 + [ANY], out_sp...  7.98 us
    pallas_call x1, Pallas kernels, own_stage(): pl.pallas_call(own_kernel, grid=(rows // BQ,), in_specs=[SMEM, WHOLE, row...  7.6 us
    unnamed x10, local copies, waits for them, and re-layouts  1.61 us
  transfers between devices with their start and end apart: 6, of which 3 were waited for; matrix products, arithmetic and copies ran while one was open for 0% of the time, Pallas kernels for 25%

profile of v5, /device:TPU:20, one launch (start us, length us, event | category | flops | bytes accessed | tf_op | source)
XLA Modules:
  0.0 77.0 jit_solution(12026091302561122494)
XLA Ops:
  0.0 0.0 copy-start
  0.0 1.6 %copy-done = bf16[512,2048]{1,0:T(8,128)(2,1)S(1)} copy-done((bf16[512,2048]{1,0:T(8,128)(2,1)S(1)}, bf16[512,2048]{1,0:T(8,128)(2,1)}, u32[]{:S(2)}) %copy-start) | copy-done | bytes 2097176
  1.6 0.0 copy-start.2
  1.6 0.0 copy-start.3
  1.6 0.0 copy-start.4
  1.6 1.0 %leading_rows.1 = bf16[256,2048]{1,0:T(8,128)(2,1)} custom-call(bf16[512,2048]{1,0:T(8,128)(2,1)S(1)} %copy-done), custom_call_target="tpu_custom_call" | custom-call | tf_op jit(solution)/shard_map/leading_rows/pallas_call | solution.py:388
  2.6 7.7 %collective-permute-start = (bf16[256,2048]{1,0:T(8,128)(2,1)}, bf16[256,2048]{1,0:T(8,128)(2,1)S(1)}, u32[]{:S(2)}, u32[]{:S(2)}) collective-permute-start(bf16[256,2048]{1,0:T(8,128)(2,1)} %leading_rows.1), channel_id=1, source_target_pairs={{2,0},{4,2},{6,4},{8,6},{10,8},{12,10},{14,12},{16,14},{18,16},{20... | collective-permute-start | bytes 3145736 | tf_op jit(solution)/shard_map/ppermute | solution.py:461
  10.4 0.0 copy-done.2
  10.4 1.9 %collective-permute-start.2 = (bf16[512,1024]{1,0:T(8,128)(2,1)S(1)}, bf16[512,1024]{1,0:T(8,128)(2,1)}, u32[]{:S(2)}, u32[]{:S(2)}) collective-permute-start(bf16[512,1024]{1,0:T(8,128)(2,1)S(1)} %copy-done.2), channel_id=1, source_target_pairs={{0,1},{1,2},{2,3},{3,4},{4,5},{5,6},{6,7},{7,8},{8,9},{9,10},{10,1... | collective-permute-start | bytes 3145736 | tf_op jit(solution)/shard_map/ppermute | solution.py:461
  12.3 0.0 copy-done.3
  12.3 1.9 %collective-permute-start.4 = (bf16[512,1024]{1,0:T(8,128)(2,1)S(1)}, bf16[512,1024]{1,0:T(8,128)(2,1)}, u32[]{:S(2)}, u32[]{:S(2)}) collective-permute-start(bf16[512,1024]{1,0:T(8,128)(2,1)S(1)} %copy-done.3), channel_id=1, source_target_pairs={{0,1},{1,2},{2,3},{3,4},{4,5},{5,6},{6,7},{7,8},{8,9},{9,10},{10,1... | collective-permute-start | bytes 3145736 | tf_op jit(solution)/shard_map/ppermute | solution.py:461
  14.3 8.7 %collective-permute-done.q_ref = bf16[256,2048]{1,0:T(8,128)(2,1)S(1)} collective-permute-done((bf16[256,2048]{1,0:T(8,128)(2,1)}, bf16[256,2048]{1,0:T(8,128)(2,1)S(1)}, u32[]{:S(2)}, u32[]{:S(2)}) %collective-permute-start) | collective-permute-done | bytes 1048608 | tf_op jit(solution)/shard_map/ppermute | solution.py:461
  23.0 0.0 copy-done.4
  23.0 0.0 copy-start.1
  23.0 0.5 back_shard.1
  23.5 2.1 %collective-permute-start.1 = (bf16[256,2176]{1,0:T(8,128)(2,1)S(1)}, bf16[256,2176]{1,0:T(8,128)(2,1)S(1)}, u32[]{:S(2)}, u32[]{:S(2)}) collective-permute-start(bf16[256,2176]{1,0:T(8,128)(2,1)S(1)} %back_shard.1), channel_id=1, source_target_pairs={{0,2},{2,4},{4,6},{6,8},{8,10},{10,12},{12,14},{14,16},{16,18},{18... | collective-permute-start | bytes 3342344 | tf_op jit(solution)/shard_map/ppermute | solution.py:461
  25.6 3.1 %collective-permute-done.2.k_ref = bf16[512,1024]{1,0:T(8,128)(2,1)} collective-permute-done((bf16[512,1024]{1,0:T(8,128)(2,1)S(1)}, bf16[512,1024]{1,0:T(8,128)(2,1)}, u32[]{:S(2)}, u32[]{:S(2)}) %collective-permute-start.2) | collective-permute-done | bytes 1048608 | tf_op jit(solution)/shard_map/ppermute | solution.py:461
  28.7 1.3 %collective-permute-start.3 = (bf16[512,1024]{1,0:T(8,128)(2,1)}, bf16[512,1024]{1,0:T(8,128)(2,1)S(1)}, u32[]{:S(2)}, u32[]{:S(2)}) collective-permute-start(bf16[512,1024]{1,0:T(8,128)(2,1)} %collective-permute-done.2.k_ref), channel_id=1, source_target_pairs={{0,1},{2,3},{4,5},{6,7},{8,9},{10,11},{12,13},{14,15},{16,17},{18,... | collective-permute-start | bytes 3145736 | tf_op jit(solution)/shard_map/ppermute | solution.py:461
  30.1 18.1 %collective-permute-done.4.v_ref = bf16[512,1024]{1,0:T(8,128)(2,1)} collective-permute-done((bf16[512,1024]{1,0:T(8,128)(2,1)S(1)}, bf16[512,1024]{1,0:T(8,128)(2,1)}, u32[]{:S(2)}, u32[]{:S(2)}) %collective-permute-start.4) | collective-permute-done | bytes 1048608 | tf_op jit(solution)/shard_map/ppermute | solution.py:461
  48.1 1.5 %collective-permute-start.5 = (bf16[512,1024]{1,0:T(8,128)(2,1)}, bf16[512,1024]{1,0:T(8,128)(2,1)S(1)}, u32[]{:S(2)}, u32[]{:S(2)}) collective-permute-start(bf16[512,1024]{1,0:T(8,128)(2,1)} %collective-permute-done.4.v_ref), channel_id=1, source_target_pairs={{0,1},{2,3},{4,5},{6,7},{8,9},{10,11},{12,13},{14,15},{16,17},{18,... | collective-permute-start | bytes 3145736 | tf_op jit(solution)/shard_map/ppermute | solution.py:461
  49.7 0.0 copy-done.1
  49.7 7.6 %own_shard.1 = (f32[512,2048]{1,0:T(8,128)S(1)}, f32[512,128]{1,0:T(8,128)S(1)}, bf16[128,2048]{1,0:T(8,128)(2,1)S(1)}, bf16[512,2048]{1,0:T(8,128)(2,1)}) custom-call(s32[1]{0:T(128)} %bitcast.first_ref, s32[1,256]{1,0:T(1,128)S(1)} %bitcast.3, bf16[512,2048]{1,0:T(8,128)(2,1)S(1)} %copy-done.1, bf16[512,1024]{1,0:T(8,128)(2,1)S(1)} %copy-done.2, ...), custom_call_target="tpu_custom_call" | custom-call | flops 2147483648 | bytes 8388608 | tf_op jit(solution)/shard_map/own_shard/pallas_call | solution.py:368
  57.3 11.5 %next_shard.1 = (bf16[512,2048]{1,0:T(8,128)(2,1)}, f32[512,2048]{1,0:T(8,128)S(1)}, f32[512,128]{1,0:T(8,128)S(1)}) custom-call(s32[1]{0:T(128)} %bitcast.first_ref, bf16[512,2048]{1,0:T(8,128)(2,1)S(1)} %copy-done.1, bf16[512,1024]{1,0:T(8,128)(2,1)} %collective-permute-done.2.k_ref, ...), custom_call_target="tpu_custom_call", output_to_operand_aliasing={{0}: (7, {})} | custom-call | flops 2147483648 | bytes 8388608 | tf_op jit(solution)/shard_map/next_shard/pallas_call | solution.py:424
  68.8 0.0 collective-permute-done.3.k_ref
  68.8 0.0 collective-permute-done.5.v_ref
  68.8 0.0 collective-permute-done.1.slot_ref
  68.8 8.0 %last_shard.1 = bf16[512,2048]{1,0:T(8,128)(2,1)} custom-call(s32[1]{0:T(128)} %bitcast.first_ref, bf16[512,2048]{1,0:T(8,128)(2,1)S(1)} %copy-done.1, bf16[256,2176]{1,0:T(8,128)(2,1)S(1)} %collective-permute-done.1.slot_ref, bf16[512,1024]{1,0:T(8,128)(2,1)S(1)} %collective-permute-done.3.k_ref, ...), custom_call_target="tpu_custom_call", output_to_operand_aliasing={{}: (9, {})} | custom-call | flops 1073741824 | bytes 8388608 | tf_op jit(solution)/shard_map/last_shard/pallas_call | solution.py:440
Async XLA Ops:
  0.0 1.6 %copy-start = (bf16[512,2048]{1,0:T(8,128)(2,1)S(1)}, bf16[512,2048]{1,0:T(8,128)(2,1)}, u32[]{:S(2)}) copy-start(bf16[512,2048]{1,0:T(8,128)(2,1)} %q_ref.5) | copy-start | bytes 6291460
  1.6 8.8 %copy-start.2 = (bf16[512,1024]{1,0:T(8,128)(2,1)S(1)}, bf16[512,1024]{1,0:T(8,128)(2,1)}, u32[]{:S(2)}) copy-start(bf16[512,1024]{1,0:T(8,128)(2,1)} %k_ref.3) | copy-start | bytes 3145732
  1.6 10.7 %copy-start.3 = (bf16[512,1024]{1,0:T(8,128)(2,1)S(1)}, bf16[512,1024]{1,0:T(8,128)(2,1)}, u32[]{:S(2)}) copy-start(bf16[512,1024]{1,0:T(8,128)(2,1)} %v_ref.3) | copy-start | bytes 3145732
  1.6 21.4 %copy-start.4 = (s32[256]{0:T(256)S(1)}, s32[256]{0:T(256)}, u32[]{:S(2)}) copy-start(s32[256]{0:T(256)} %param.7) | copy-start | bytes 3076
  2.6 20.3 %collective-permute-start = (bf16[256,2048]{1,0:T(8,128)(2,1)}, bf16[256,2048]{1,0:T(8,128)(2,1)S(1)}, u32[]{:S(2)}, u32[]{:S(2)}) collective-permute-start(bf16[256,2048]{1,0:T(8,128)(2,1)} %leading_rows.1), channel_id=1, source_target_pairs={{2,0},{4,2},{6,4},{8,6},{10,8},{12,10},{14,12},{16,14},{18,16},{20... | collective-permute-start | bytes 3145736 | tf_op jit(solution)/shard_map/ppermute | solution.py:461
  10.4 18.3 %collective-permute-start.2 = (bf16[512,1024]{1,0:T(8,128)(2,1)S(1)}, bf16[512,1024]{1,0:T(8,128)(2,1)}, u32[]{:S(2)}, u32[]{:S(2)}) collective-permute-start(bf16[512,1024]{1,0:T(8,128)(2,1)S(1)} %copy-done.2), channel_id=1, source_target_pairs={{0,1},{1,2},{2,3},{3,4},{4,5},{5,6},{6,7},{7,8},{8,9},{9,10},{10,1... | collective-permute-start | bytes 3145736 | tf_op jit(solution)/shard_map/ppermute | solution.py:461
  12.3 35.8 %collective-permute-start.4 = (bf16[512,1024]{1,0:T(8,128)(2,1)S(1)}, bf16[512,1024]{1,0:T(8,128)(2,1)}, u32[]{:S(2)}, u32[]{:S(2)}) collective-permute-start(bf16[512,1024]{1,0:T(8,128)(2,1)S(1)} %copy-done.3), channel_id=1, source_target_pairs={{0,1},{1,2},{2,3},{3,4},{4,5},{5,6},{6,7},{7,8},{8,9},{9,10},{10,1... | collective-permute-start | bytes 3145736 | tf_op jit(solution)/shard_map/ppermute | solution.py:461
  23.0 26.7 %copy-start.1 = (bf16[512,2048]{1,0:T(8,128)(2,1)S(1)}, bf16[512,2048]{1,0:T(8,128)(2,1)}, u32[]{:S(2)}) copy-start(bf16[512,2048]{1,0:T(8,128)(2,1)} %q_ref.5) | copy-start | bytes 6291460
  23.5 45.3 %collective-permute-start.1 = (bf16[256,2176]{1,0:T(8,128)(2,1)S(1)}, bf16[256,2176]{1,0:T(8,128)(2,1)S(1)}, u32[]{:S(2)}, u32[]{:S(2)}) collective-permute-start(bf16[256,2176]{1,0:T(8,128)(2,1)S(1)} %back_shard.1), channel_id=1, source_target_pairs={{0,2},{2,4},{4,6},{6,8},{8,10},{10,12},{12,14},{14,16},{16,18},{18... | collective-permute-start | bytes 3342344 | tf_op jit(solution)/shard_map/ppermute | solution.py:461
  28.7 40.1 %collective-permute-start.3 = (bf16[512,1024]{1,0:T(8,128)(2,1)}, bf16[512,1024]{1,0:T(8,128)(2,1)S(1)}, u32[]{:S(2)}, u32[]{:S(2)}) collective-permute-start(bf16[512,1024]{1,0:T(8,128)(2,1)} %collective-permute-done.2.k_ref), channel_id=1, source_target_pairs={{0,1},{2,3},{4,5},{6,7},{8,9},{10,11},{12,13},{14,15},{16,17},{18,... | collective-permute-start | bytes 3145736 | tf_op jit(solution)/shard_map/ppermute | solution.py:461
  48.1 20.7 %collective-permute-start.5 = (bf16[512,1024]{1,0:T(8,128)(2,1)}, bf16[512,1024]{1,0:T(8,128)(2,1)S(1)}, u32[]{:S(2)}, u32[]{:S(2)}) collective-permute-start(bf16[512,1024]{1,0:T(8,128)(2,1)} %collective-permute-done.4.v_ref), channel_id=1, source_target_pairs={{0,1},{2,3},{4,5},{6,7},{8,9},{10,11},{12,13},{14,15},{16,17},{18,... | collective-permute-start | bytes 3145736 | tf_op jit(solution)/shard_map/ppermute | solution.py:461

commit v6 on v5

--- a/solution.py
+++ b/solution.py
@@ -1,3 +1,4 @@
+import functools
 import math
 
 import jax
@@ -98,7 +99,9 @@
         write(cols, factors[:rows] * kept(cols) + factors[rows:] * taken(cols).astype(jnp.float32))
 
 
-def own_kernel(first_ref, len_ref, q_ref, k_ref, v_ref, acc_ref, state_ref, spread_ref, out_ref, ends_ref):
+def own_kernel(
+    first_ref, len_ref, q_ref, k_ref, v_ref, acc_ref, state_ref, spread_ref, out_ref, mark_ref, ends_ref
+):
     block = pl.program_id(0)
 
     @pl.when(block == 0)
@@ -107,25 +110,31 @@
         spread_ref[...] = spreader()
 
     ends = ends_ref[...]
-    keys = k_ref.shape[0]
     first = first_ref[0].astype(jnp.float32)
     row = float_iota((BQ, 1), 0) + (block * BQ).astype(jnp.float32)
     start = jnp.max(jnp.where(ends <= row + first, ends, 0.0), axis=1, keepdims=True)
-    col = float_iota((BQ, keys), 1)
-    bias = jnp.where((col >= start - first) & (col <= row), 0.0, HIDDEN)
+    mark_ref[block] = jnp.min(start)
     lane = lax.broadcasted_iota(jnp.int32, (BQ, 128), 1)
-    state = [jnp.broadcast_to(start, (BQ, 128))]
-
-    def emit(head, g, mixed, total, top):
-        h = head * GROUPS + g
-        cols = slice(h * DH, (h + 1) * DH)
-        mixed = mixed * (1.0 / total)
-        acc_ref[:, cols] = mixed
-        out_ref[:, cols] = mixed.astype(out_ref.dtype)
-        state[0] = jnp.where(lane == HQ + h, total, jnp.where(lane == h, top, state[0]))
-
-    attend(pairs_of(q_ref), heads_of(k_ref), heads_of(v_ref), bias, emit)
-    state_ref[...] = state[0]
+
+    def over(count):
+        col = float_iota((BQ, count), 1)
+        bias = jnp.where((col >= start - first) & (col <= row), 0.0, HIDDEN)
+        state = [jnp.broadcast_to(start, (BQ, 128))]
+
+        def emit(head, g, mixed, total, top):
+            h = head * GROUPS + g
+            cols = slice(h * DH, (h + 1) * DH)
+            mixed = mixed * (1.0 / total)
+            acc_ref[:, cols] = mixed
+            out_ref[:, cols] = mixed.astype(out_ref.dtype)
+            state[0] = jnp.where(lane == HQ + h, total, jnp.where(lane == h, top, state[0]))
+
+        part = slice(0, count)
+        attend(pairs_of(q_ref), heads_of(k_ref, part), heads_of(v_ref, part), bias, emit)
+        state_ref[...] = state[0]
+
+    for step in range(k_ref.shape[0] // BQ):
+        pl.when(block == step)(functools.partial(over, (step + 1) * BQ))
 
 
 def back_kernel(first_ref, len_ref, q_ref, k_ref, v_ref, slot_ref):
@@ -149,11 +158,10 @@
             slot_ref[:, :KV] = k_ref[rows, :]
             slot_ref[:, KV : 2 * KV] = v_ref[rows, :]
 
-        @pl.when(reached & jnp.logical_not(by_keys) & ((block * BQ).astype(jnp.float32) < right))
-        def _():
+        def over(count):
             row = float_iota((BQ, 1), 0) + (block * BQ).astype(jnp.float32)
-            col = float_iota((BQ, keys), 1)
-            bias = jnp.where((col >= start - here) & (row < right), 0.0, HIDDEN)
+            col = float_iota((BQ, count), 1)
+            bias = jnp.where((col >= start - (here + keys - count)) & (row < right), 0.0, HIDDEN)
             lane = lax.broadcasted_iota(jnp.int32, (BQ, 128), 1)
             level = [jnp.zeros((BQ, 128), jnp.float32)]
 
@@ -162,8 +170,15 @@
                 slot_ref[:, h * DH : (h + 1) * DH] = (mixed * (1.0 / total)).astype(jnp.bfloat16)
                 level[0] = jnp.where(lane == h, top * RATE + jnp.log2(total), level[0])
 
-            attend(pairs_of(q_ref), heads_of(k_ref), heads_of(v_ref), bias, emit)
+            part = slice(keys - count, keys)
+            attend(pairs_of(q_ref), heads_of(k_ref, part), heads_of(v_ref, part), bias, emit)
             slot_ref[:, 2 * KV :] = in_parts(level[0])
+
+        working = reached & jnp.logical_not(by_keys) & ((block * BQ).astype(jnp.float32) < right)
+        length = here + keys - start
+        pl.when(working & (length <= 256))(functools.partial(over, 256))
+        pl.when(working & (length > 256) & (length <= 384))(functools.partial(over, 384))
+        pl.when(working & (length > 384))(functools.partial(over, keys))
 
 
 def column(state, lane):
@@ -174,14 +189,13 @@
     return pltpu.roll(state, 128 - group * HQ, 1) if group else state
 
 
-def collect(fresh_ref):
-    rows = fresh_ref.shape[0]
+def collect(fresh_ref, rows=BQ):
     lane = lax.broadcasted_iota(jnp.int32, (rows, 128), 1)
     held = [jnp.zeros((rows, 128), jnp.float32)]
 
     def emit(head, g, mixed, total, top):
         h = head * GROUPS + g
-        fresh_ref[:, h * DH : (h + 1) * DH] = mixed
+        fresh_ref[:rows, h * DH : (h + 1) * DH] = mixed
         held[0] = jnp.where(lane == HQ + h, total, jnp.where(lane == h, top, held[0]))
 
     return emit, held
@@ -208,7 +222,7 @@
 
 
 def next_kernel(
-    first_ref, q_ref, k_ref, v_ref, acc_ref, state_ref, spread_ref, prior_ref, out_ref, new_acc_ref, new_state_ref,
+    first_ref, mark_ref, q_ref, k_ref, v_ref, acc_ref, state_ref, spread_ref, prior_ref, out_ref, new_acc_ref, new_state_ref,
     done_ref, fresh_ref, sem,
 ):
     keys = k_ref.shape[0]
@@ -217,15 +231,12 @@
     blocks = q_ref.shape[0] // BQ
     copy = writer(done_ref, out_ref, sem)
 
-    def earliest(block):
-        return jnp.min(state_ref[pl.ds(block * BQ, 8), START : START + 1])
-
     def finishes(block):
-        return (earliest(block) < first) & (earliest(block) >= base)
+        return (mark_ref[block] < first) & (mark_ref[block] >= base)
 
     @pl.loop(0, blocks)
     def _(block):
-        @pl.when(earliest(block) < first)
+        @pl.when(mark_ref[block] < first)
         def _():
             rows = rows_at(block)
             state = state_ref[rows, :]
@@ -241,7 +252,7 @@
                 new_acc_ref[rows, cols] = mixed
                 done_ref[rows, cols] = mixed.astype(done_ref.dtype)
 
-            mix(keep, lambda cols: acc_ref[rows, cols], take, lambda cols: fresh_ref[:, cols], spread_ref, write)
+            mix(keep, lambda cols: acc_ref[rows, cols], take, lambda cols: fresh_ref[:BQ, cols], spread_ref, write)
 
         @pl.when(finishes(block))
         def _():
@@ -255,7 +266,7 @@
 
 
 def last_kernel(
-    first_ref, q_ref, slot_ref, k_ref, v_ref, acc_ref, state_ref, starts_ref, spread_ref, prior_ref, out_ref,
+    first_ref, mark_ref, q_ref, slot_ref, k_ref, v_ref, acc_ref, state_ref, spread_ref, prior_ref, out_ref,
     done_ref, fresh_ref, sem,
 ):
     keys = k_ref.shape[0]
@@ -264,11 +275,9 @@
     even = jnp.logical_not(odd)
     base = first - keys
     blocks = q_ref.shape[0] // BQ
-    by_keys = jnp.min(starts_ref[SLOT : SLOT + 8, START : START + 1]) < first
+    start = mark_ref[0]
+    by_keys = mark_ref[SLOT // BQ] < first
     copy = writer(done_ref, out_ref, sem)
-
-    def earliest(block):
-        return jnp.min(starts_ref[pl.ds(block * BQ, 8), START : START + 1])
 
     def write(rows, keep, take, added):
         def put(cols, mixed):
@@ -276,15 +285,16 @@
 
         mix(keep, lambda cols: acc_ref[rows, cols], take, added, spread_ref, put)
 
-    def merge(block, ref_k, ref_v, at, skip, count, origin):
-        rows = rows_at(block)
+    def merge(block, tall, ref_k, ref_v, at, count):
+        rows = pl.ds(pl.multiple_of(block * BQ, BQ), tall * BQ)
         state = state_ref[rows, :]
+        skip = ref_k.shape[0] - count
         part = slice(skip, skip + count)
-        bias = jnp.where(float_iota((BQ, count), 1) >= column(state, START) - origin, 0.0, HIDDEN)
-        emit, held = collect(fresh_ref)
+        bias = jnp.where(float_iota((tall * BQ, count), 1) >= column(state, START) - (base - count), 0.0, HIDDEN)
+        emit, held = collect(fresh_ref, tall * BQ)
         attend(pairs_of(q_ref, rows), heads_of(ref_k, part), heads_of(ref_v, part, at), bias, emit)
         keep, take, _, _ = joined(state, held[0])
-        write(rows, keep, take, lambda cols: fresh_ref[:, cols])
+        write(rows, keep, take, lambda cols: fresh_ref[: tall * BQ, cols])
 
     def combine(block):
         rows = rows_at(block)
@@ -298,42 +308,32 @@
         scale = 1.0 / (before + take)
         write(rows, before * scale, take * scale, lambda cols: slot_ref[rows, cols])
 
+    def sweep(condition, tall, work, end=blocks):
+        @pl.when(condition & (start < base))
+        def _():
+            @pl.loop(0, end // tall)
+            def _(step):
+                block = step * tall
+
+                @pl.when(mark_ref[block] < base)
+                def _():
+                    work(block)
+                    for i in range(tall):
+                        pl.when(mark_ref[block + i] < base)(copy(block + i).start)
+
+    near = start >= base - BQ
+    far = start < base - SLOT
+    some = jnp.logical_not(near | far)
+    sweep(odd & near, 2, lambda block: merge(block, 2, k_ref, v_ref, 0, BQ))
+    sweep(odd & some, 1, lambda block: merge(block, 1, k_ref, v_ref, 0, SLOT))
+    sweep(odd & far, 1, lambda block: merge(block, 1, k_ref, v_ref, 0, keys))
+    sweep(even & by_keys & near, 2, lambda block: merge(block, 2, slot_ref, slot_ref, KV, BQ))
+    sweep(even & by_keys & jnp.logical_not(near), 1, lambda block: merge(block, 1, slot_ref, slot_ref, KV, SLOT))
+    sweep(even & jnp.logical_not(by_keys), 1, combine, SLOT // BQ)
+
     @pl.loop(0, blocks)
     def _(block):
-        start = earliest(block)
-        needed = start < base
-        far = start < base - SLOT
-        near = start >= base - BQ
-
-        @pl.when(odd & far)
-        def _():
-            merge(block, k_ref, v_ref, 0, 0, keys, base - keys)
-
-        @pl.when(odd & needed & jnp.logical_not(far))
-        def _():
-            merge(block, k_ref, v_ref, 0, keys - SLOT, SLOT, base - SLOT)
-
-        @pl.when(even & needed & by_keys & near)
-        def _():
-            merge(block, slot_ref, slot_ref, KV, SLOT - BQ, BQ, base - BQ)
-
-        @pl.when(even & needed & by_keys & jnp.logical_not(near))
-        def _():
-            merge(block, slot_ref, slot_ref, KV, 0, SLOT, base - SLOT)
-
-        @pl.when(even & needed & jnp.logical_not(by_keys) & (block * BQ < SLOT))
-        def _():
-            combine(block)
-
-        @pl.when(needed)
-        def _():
-            copy(block).start()
-
-    @pl.loop(0, blocks)
-    def _(block):
-        @pl.when(earliest(block) < base)
-        def _():
-            copy(block).wait()
+        pl.when(mark_ref[block] < base)(lambda: copy(block).wait())
 
 
 def rows_of(width):
@@ -369,8 +369,8 @@
         own_kernel,
         grid=(rows // BQ,),
         in_specs=[SMEM, WHOLE, rows_of(WIDE), WHOLE, WHOLE],
-        out_specs=[rows_of(WIDE), rows_of(128), WHOLE, rows_of(WIDE)],
-        out_shape=[f32(rows, WIDE), f32(rows, 128), bf16(128, WIDE), bf16(rows, WIDE)],
+        out_specs=[rows_of(WIDE), rows_of(128), WHOLE, rows_of(WIDE), SMEM],
+        out_shape=[f32(rows, WIDE), f32(rows, 128), bf16(128, WIDE), bf16(rows, WIDE), f32(rows // BQ)],
         scratch_shapes=[pltpu.VMEM(lengths.shape, jnp.float32)],
         cost_estimate=cost(rows, keys.shape[0]),
         compiler_params=PARAMS,
@@ -379,22 +379,23 @@
     )(first, lengths, queries, keys, values)
 
 
-def copy_kernel(in_ref, out_ref):
-    out_ref[...] = in_ref[...]
+def copy_kernel(in_ref, out_ref, sem):
+    copy = pltpu.make_async_copy(in_ref.at[pl.ds(0, out_ref.shape[0]), :], out_ref, sem)
+    copy.start()
+    copy.wait()
 
 
 def leading_rows(array, rows):
-    block = pl.BlockSpec((rows, array.shape[1]), lambda i: (0, 0))
     return pl.pallas_call(
         copy_kernel,
-        grid=(1,),
-        in_specs=[block],
-        out_specs=block,
+        in_specs=[pl.BlockSpec(memory_space=pltpu.HBM)],
+        out_specs=WHOLE,
         out_shape=jax.ShapeDtypeStruct((rows, array.shape[1]), array.dtype),
+        scratch_shapes=[pltpu.SemaphoreType.DMA],
         compiler_params=PARAMS,
         name="leading_rows",
         interpret=INTERPRET,
-    )(array)
+    )(pltpu.with_memory_space_constraint(array, pltpu.HBM))
 
 
 def back_stage(first, lengths, queries, keys, values):
@@ -414,32 +415,32 @@
 def writing(rows):
     return [
         pltpu.VMEM((rows, WIDE), jnp.bfloat16),
-        pltpu.VMEM((BQ, WIDE), jnp.float32),
+        pltpu.VMEM((2 * BQ, WIDE), jnp.float32),
         pltpu.SemaphoreType.DMA((rows // BQ,)),
     ]
 
 
-def next_stage(first, queries, keys, values, acc, state, spread, prior):
+def next_stage(first, marks, queries, keys, values, acc, state, spread, prior):
     rows = queries.shape[0]
     return pl.pallas_call(
         next_kernel,
-        in_specs=[SMEM] + [WHOLE] * 6 + [ANY],
+        in_specs=[SMEM] * 2 + [WHOLE] * 6 + [ANY],
         out_specs=[ANY, WHOLE, WHOLE],
         out_shape=[bf16(rows, WIDE), f32(rows, WIDE), f32(rows, 128)],
         scratch_shapes=writing(rows),
-        input_output_aliases={7: 0},
+        input_output_aliases={8: 0},
         cost_estimate=cost(rows, keys.shape[0]),
         compiler_params=PARAMS,
         name="next_shard",
         interpret=INTERPRET,
-    )(first, queries, keys, values, acc, state, spread, prior)
-
-
-def last_stage(first, queries, slot, keys, values, acc, state, starts, spread, prior):
+    )(first, marks, queries, keys, values, acc, state, spread, prior)
+
+
+def last_stage(first, marks, queries, slot, keys, values, acc, state, spread, prior):
     rows = queries.shape[0]
     return pl.pallas_call(
         last_kernel,
-        in_specs=[SMEM] + [WHOLE] * 8 + [ANY],
+        in_specs=[SMEM] * 2 + [WHOLE] * 7 + [ANY],
         out_specs=ANY,
         out_shape=bf16(rows, WIDE),
         scratch_shapes=writing(rows),
@@ -448,7 +449,7 @@
         compiler_params=PARAMS,
         name="last_shard",
         interpret=INTERPRET,
-    )(first, queries, slot, keys, values, acc, state, starts, spread, prior)
+    )(first, marks, queries, slot, keys, values, acc, state, spread, prior)
 
 
 def on_device(queries, keys, values, doc_lengths):
@@ -464,14 +465,14 @@
     one_k = hop(keys, onward)
     one_v = hop(values, onward)
     guests = hop(leading_rows(queries, SLOT), [(i, i - 2) for i in evens if i])
-    acc, state, spread, out = own_stage(first, lengths, queries, keys, values)
+    acc, state, spread, out, marks = own_stage(first, lengths, queries, keys, values)
     slot = back_stage(first, lengths, guests, keys, values)
     slot = hop(slot, [(i, i + 2) for i in evens if i + 2 < count])
     across = [(i, i + 1) for i in evens]
     two_k = hop(one_k, across)
     two_v = hop(one_v, across)
-    out, acc, new_state = next_stage(first, queries, one_k, one_v, acc, state, spread, out)
-    out = last_stage(first, queries, slot, two_k, two_v, acc, new_state, state, spread, out)
+    out, acc, new_state = next_stage(first, marks, queries, one_k, one_v, acc, state, spread, out)
+    out = last_stage(first, marks, queries, slot, two_k, two_v, acc, new_state, spread, out)
     return out
 
 

time: 77.2 us -> 71.7 us (0.929)
  waiting for transfers between devices: 29.9 us -> 27.6 us
  local copies, waits for them, and re-layouts: 1.61 us -> 0.01 us
  Pallas kernels: 28.6 us -> 27.1 us
    ppermute x6, waiting for transfers between devices: 29.9 us -> 27.6 us  [hop(): return lax.ppermute(array, 'cp', pairs)]
    pallas_call x3, Pallas kernels: 20.5 us -> 18.5 us  [the longest x1 9.8 us: next_stage(): pl.pallas_call(next_kernel, in_specs=[SMEM] * 2 + [WHOLE] * 6 + [ANY], ou...]
    unnamed x10 -> x8, local copies, waits for them, and re-layouts: 1.61 us -> 0.01 us
    pallas_call x1, Pallas kernels: 0.53 us -> 1.76 us  [back_stage(): pl.pallas_call(back_kernel, grid=(SLOT // BQ,), in_specs=[SMEM, WHOLE, ro...]
  transfers between devices with their start and end apart: 6 -> 6, of which waited for: 3 -> 3; matrix products, arithmetic and copies ran while one was open for 0% -> 0% of each run, Pallas kernels for 25% -> 26%
where the time goes in v6:
time: 71.7 us; the launch traced here: 71.5 us
  waiting for transfers between devices  27.6 us (38%)
  Pallas kernels  27.1 us (38%)
  starting transfers between devices  16.4 us (23%)
    ppermute x6, waiting for transfers between devices, hop(): return lax.ppermute(array, 'cp', pairs)  27.6 us
    ppermute x6, starting transfers between devices, hop(): return lax.ppermute(array, 'cp', pairs)  16.4 us
    pallas_call x1, Pallas kernels, next_stage(): pl.pallas_call(next_kernel, in_specs=[SMEM] * 2 + [WHOLE] * 6 + [ANY], ou...  9.8 us
    pallas_call x1, Pallas kernels, own_stage(): pl.pallas_call(own_kernel, grid=(rows // BQ,), in_specs=[SMEM, WHOLE, row...  6.86 us
    pallas_call x1, Pallas kernels, last_stage(): pl.pallas_call(last_kernel, in_specs=[SMEM] * 2 + [WHOLE] * 7 + [ANY], ou...  6.38 us
    pallas_call x1, Pallas kernels, leading_rows(): pl.pallas_call(copy_kernel, in_specs=[pl.BlockSpec(memory_space=pltpu.HBM...  2.35 us
    pallas_call x1, Pallas kernels, back_stage(): pl.pallas_call(back_kernel, grid=(SLOT // BQ,), in_specs=[SMEM, WHOLE, ro...  1.76 us
  transfers between devices with their start and end apart: 6, of which 3 were waited for; matrix products, arithmetic and copies ran while one was open for 0% of the time, Pallas kernels for 26%

profile of v6, /device:TPU:20, one launch (start us, length us, event | category | flops | bytes accessed | tf_op | source)
XLA Modules:
  0.0 71.5 jit_solution(14080807242992974775)
XLA Ops:
  0.0 0.0 copy-start.1
  0.0 0.0 copy-start.2
  0.0 0.0 copy-start.3
  0.0 2.4 %leading_rows.1 = bf16[256,2048]{1,0:T(8,128)(2,1)} custom-call(bf16[512,2048]{1,0:T(8,128)(2,1)} %q_ref.5), custom_call_target="tpu_custom_call" | custom-call | tf_op jit(solution)/shard_map/leading_rows/pallas_call | solution.py:389
  2.4 7.7 %collective-permute-start = (bf16[256,2048]{1,0:T(8,128)(2,1)}, bf16[256,2048]{1,0:T(8,128)(2,1)}, u32[]{:S(2)}, u32[]{:S(2)}) collective-permute-start(bf16[256,2048]{1,0:T(8,128)(2,1)} %leading_rows.1), channel_id=1, source_target_pairs={{2,0},{4,2},{6,4},{8,6},{10,8},{12,10},{14,12},{16,14},{18,16},{20... | collective-permute-start | bytes 3145736 | tf_op jit(solution)/shard_map/ppermute | solution.py:462
  10.1 0.0 copy-done.1
  10.1 1.9 %collective-permute-start.2 = (bf16[512,1024]{1,0:T(8,128)(2,1)S(1)}, bf16[512,1024]{1,0:T(8,128)(2,1)S(1)}, u32[]{:S(2)}, u32[]{:S(2)}) collective-permute-start(bf16[512,1024]{1,0:T(8,128)(2,1)S(1)} %copy-done.1), channel_id=1, source_target_pairs={{0,1},{1,2},{2,3},{3,4},{4,5},{5,6},{6,7},{7,8},{8,9},{9,10},{10,1... | collective-permute-start | bytes 3145736 | tf_op jit(solution)/shard_map/ppermute | solution.py:462
  12.1 0.0 copy-done.2
  12.1 1.9 %collective-permute-start.4 = (bf16[512,1024]{1,0:T(8,128)(2,1)S(1)}, bf16[512,1024]{1,0:T(8,128)(2,1)}, u32[]{:S(2)}, u32[]{:S(2)}) collective-permute-start(bf16[512,1024]{1,0:T(8,128)(2,1)S(1)} %copy-done.2), channel_id=1, source_target_pairs={{0,1},{1,2},{2,3},{3,4},{4,5},{5,6},{6,7},{7,8},{8,9},{9,10},{10,1... | collective-permute-start | bytes 3145736 | tf_op jit(solution)/shard_map/ppermute | solution.py:462
  14.0 8.7 %collective-permute-done.q_ref = bf16[256,2048]{1,0:T(8,128)(2,1)} collective-permute-done((bf16[256,2048]{1,0:T(8,128)(2,1)}, bf16[256,2048]{1,0:T(8,128)(2,1)}, u32[]{:S(2)}, u32[]{:S(2)}) %collective-permute-start) | collective-permute-done | bytes 1048608 | tf_op jit(solution)/shard_map/ppermute | solution.py:462
  22.7 0.0 copy-done.3
  22.7 0.0 copy-start
  22.7 1.8 %back_shard.1 = bf16[256,2176]{1,0:T(8,128)(2,1)S(1)} custom-call(s32[1]{0:T(128)} %bitcast.first_ref, s32[1,256]{1,0:T(1,128)S(1)} %bitcast.2, bf16[256,2048]{1,0:T(8,128)(2,1)} %collective-permute-done.q_ref, bf16[512,1024]{1,0:T(8,128)(2,1)S(1)} %copy-done.1, bf16[512,1024]{1,0:T(8,128)(2,1)S(1)} %copy-done.2), custom_call_target="tpu_custom_call" | custom-call | flops 1073741824 | bytes 4194304 | tf_op jit(solution)/shard_map/back_shard/pallas_call | solution.py:402
  24.5 1.9 %collective-permute-start.1 = (bf16[256,2176]{1,0:T(8,128)(2,1)S(1)}, bf16[256,2176]{1,0:T(8,128)(2,1)S(1)}, u32[]{:S(2)}, u32[]{:S(2)}) collective-permute-start(bf16[256,2176]{1,0:T(8,128)(2,1)S(1)} %back_shard.1), channel_id=1, source_target_pairs={{0,2},{2,4},{4,6},{6,8},{8,10},{10,12},{12,14},{14,16},{16,18},{18... | collective-permute-start | bytes 3342344 | tf_op jit(solution)/shard_map/ppermute | solution.py:462
  26.4 1.9 %collective-permute-done.2.k_ref = bf16[512,1024]{1,0:T(8,128)(2,1)S(1)} collective-permute-done((bf16[512,1024]{1,0:T(8,128)(2,1)S(1)}, bf16[512,1024]{1,0:T(8,128)(2,1)S(1)}, u32[]{:S(2)}, u32[]{:S(2)}) %collective-permute-start.2) | collective-permute-done | bytes 1048608 | tf_op jit(solution)/shard_map/ppermute | solution.py:462
  28.4 1.3 %collective-permute-start.3 = (bf16[512,1024]{1,0:T(8,128)(2,1)S(1)}, bf16[512,1024]{1,0:T(8,128)(2,1)S(1)}, u32[]{:S(2)}, u32[]{:S(2)}) collective-permute-start(bf16[512,1024]{1,0:T(8,128)(2,1)S(1)} %collective-permute-done.2.k_ref), channel_id=1, source_target_pairs={{0,1},{2,3},{4,5},{6,7},{8,9},{10,11},{12,13},{14,15},{16,17},{18,... | collective-permute-start | bytes 3145736 | tf_op jit(solution)/shard_map/ppermute | solution.py:462
  29.7 17.0 %collective-permute-done.4.v_ref = bf16[512,1024]{1,0:T(8,128)(2,1)} collective-permute-done((bf16[512,1024]{1,0:T(8,128)(2,1)S(1)}, bf16[512,1024]{1,0:T(8,128)(2,1)}, u32[]{:S(2)}, u32[]{:S(2)}) %collective-permute-start.4) | collective-permute-done | bytes 1048608 | tf_op jit(solution)/shard_map/ppermute | solution.py:462
  46.7 1.5 %collective-permute-start.5 = (bf16[512,1024]{1,0:T(8,128)(2,1)}, bf16[512,1024]{1,0:T(8,128)(2,1)S(1)}, u32[]{:S(2)}, u32[]{:S(2)}) collective-permute-start(bf16[512,1024]{1,0:T(8,128)(2,1)} %collective-permute-done.4.v_ref), channel_id=1, source_target_pairs={{0,1},{2,3},{4,5},{6,7},{8,9},{10,11},{12,13},{14,15},{16,17},{18,... | collective-permute-start | bytes 3145736 | tf_op jit(solution)/shard_map/ppermute | solution.py:462
  48.2 0.0 copy-done
  48.2 6.9 %own_shard.1 = (f32[512,2048]{1,0:T(8,128)S(1)}, f32[512,128]{1,0:T(8,128)S(1)}, bf16[128,2048]{1,0:T(8,128)(2,1)S(1)}, bf16[512,2048]{1,0:T(8,128)(2,1)}, f32[4]{0:T(128)S(1)}) custom-call(s32[1]{0:T(128)} %bitcast.first_ref, s32[1,256]{1,0:T(1,128)S(1)} %bitcast.3, bf16[512,2048]{1,0:T(8,128)(2,1)S(1)} %copy-done, bf16[512,1024]{1,0:T(8,128)(2,1)S(1)} %copy-done.1, ...), custom_call_target="tpu_custom_call" | custom-call | flops 2147483648 | bytes 8388608 | tf_op jit(solution)/shard_map/own_shard/pallas_call | solution.py:368
  55.1 9.8 %next_shard.1 = (bf16[512,2048]{1,0:T(8,128)(2,1)}, f32[512,2048]{1,0:T(8,128)S(1)}, f32[512,128]{1,0:T(8,128)S(1)}) custom-call(s32[1]{0:T(128)} %bitcast.first_ref, f32[4]{0:T(128)S(1)} %get-tuple-element.13.mark_ref, bf16[512,2048]{1,0:T(8,128)(2,1)S(1)} %copy-done, ...), custom_call_target="tpu_custom_call", output_to_operand_aliasing={{0}: (8, {})} | custom-call | flops 2147483648 | bytes 8388608 | tf_op jit(solution)/shard_map/next_shard/pallas_call | solution.py:425
  64.9 0.0 collective-permute-done.3.k_ref
  64.9 0.0 collective-permute-done.5.v_ref
  64.9 0.0 collective-permute-done.1.slot_ref
  64.9 6.4 %last_shard.1 = bf16[512,2048]{1,0:T(8,128)(2,1)} custom-call(s32[1]{0:T(128)} %bitcast.first_ref, f32[4]{0:T(128)S(1)} %get-tuple-element.13.mark_ref, bf16[512,2048]{1,0:T(8,128)(2,1)S(1)} %copy-done, bf16[256,2176]{1,0:T(8,128)(2,1)S(1)} %collective-permute-done.1.slot_ref, ...), custom_call_target="tpu_custom_call", output_to_operand_aliasing={{}: (9, {})} | custom-call | flops 1073741824 | bytes 8388608 | tf_op jit(solution)/shard_map/last_shard/pallas_call | solution.py:441
Async XLA Ops:
  0.0 10.1 %copy-start.1 = (bf16[512,1024]{1,0:T(8,128)(2,1)S(1)}, bf16[512,1024]{1,0:T(8,128)(2,1)}, u32[]{:S(2)}) copy-start(bf16[512,1024]{1,0:T(8,128)(2,1)} %k_ref.3) | copy-start | bytes 3145732
  0.0 12.1 %copy-start.2 = (bf16[512,1024]{1,0:T(8,128)(2,1)S(1)}, bf16[512,1024]{1,0:T(8,128)(2,1)}, u32[]{:S(2)}) copy-start(bf16[512,1024]{1,0:T(8,128)(2,1)} %v_ref.3) | copy-start | bytes 3145732
  0.0 22.7 %copy-start.3 = (s32[256]{0:T(256)S(1)}, s32[256]{0:T(256)}, u32[]{:S(2)}) copy-start(s32[256]{0:T(256)} %param.7) | copy-start | bytes 3076
  2.4 20.4 %collective-permute-start = (bf16[256,2048]{1,0:T(8,128)(2,1)}, bf16[256,2048]{1,0:T(8,128)(2,1)}, u32[]{:S(2)}, u32[]{:S(2)}) collective-permute-start(bf16[256,2048]{1,0:T(8,128)(2,1)} %leading_rows.1), channel_id=1, source_target_pairs={{2,0},{4,2},{6,4},{8,6},{10,8},{12,10},{14,12},{16,14},{18,16},{20... | collective-permute-start | bytes 3145736 | tf_op jit(solution)/shard_map/ppermute | solution.py:462
  10.1 18.2 %collective-permute-start.2 = (bf16[512,1024]{1,0:T(8,128)(2,1)S(1)}, bf16[512,1024]{1,0:T(8,128)(2,1)S(1)}, u32[]{:S(2)}, u32[]{:S(2)}) collective-permute-start(bf16[512,1024]{1,0:T(8,128)(2,1)S(1)} %copy-done.1), channel_id=1, source_target_pairs={{0,1},{1,2},{2,3},{3,4},{4,5},{5,6},{6,7},{7,8},{8,9},{9,10},{10,1... | collective-permute-start | bytes 3145736 | tf_op jit(solution)/shard_map/ppermute | solution.py:462
  12.1 34.6 %collective-permute-start.4 = (bf16[512,1024]{1,0:T(8,128)(2,1)S(1)}, bf16[512,1024]{1,0:T(8,128)(2,1)}, u32[]{:S(2)}, u32[]{:S(2)}) collective-permute-start(bf16[512,1024]{1,0:T(8,128)(2,1)S(1)} %copy-done.2), channel_id=1, source_target_pairs={{0,1},{1,2},{2,3},{3,4},{4,5},{5,6},{6,7},{7,8},{8,9},{9,10},{10,1... | collective-permute-start | bytes 3145736 | tf_op jit(solution)/shard_map/ppermute | solution.py:462
  22.7 25.5 %copy-start = (bf16[512,2048]{1,0:T(8,128)(2,1)S(1)}, bf16[512,2048]{1,0:T(8,128)(2,1)}, u32[]{:S(2)}) copy-start(bf16[512,2048]{1,0:T(8,128)(2,1)} %q_ref.5) | copy-start | bytes 6291460
  24.5 40.4 %collective-permute-start.1 = (bf16[256,2176]{1,0:T(8,128)(2,1)S(1)}, bf16[256,2176]{1,0:T(8,128)(2,1)S(1)}, u32[]{:S(2)}, u32[]{:S(2)}) collective-permute-start(bf16[256,2176]{1,0:T(8,128)(2,1)S(1)} %back_shard.1), channel_id=1, source_target_pairs={{0,2},{2,4},{4,6},{6,8},{8,10},{10,12},{12,14},{14,16},{16,18},{18... | collective-permute-start | bytes 3342344 | tf_op jit(solution)/shard_map/ppermute | solution.py:462
  28.4 36.5 %collective-permute-start.3 = (bf16[512,1024]{1,0:T(8,128)(2,1)S(1)}, bf16[512,1024]{1,0:T(8,128)(2,1)S(1)}, u32[]{:S(2)}, u32[]{:S(2)}) collective-permute-start(bf16[512,1024]{1,0:T(8,128)(2,1)S(1)} %collective-permute-done.2.k_ref), channel_id=1, source_target_pairs={{0,1},{2,3},{4,5},{6,7},{8,9},{10,11},{12,13},{14,15},{16,17},{18,... | collective-permute-start | bytes 3145736 | tf_op jit(solution)/shard_map/ppermute | solution.py:462
  46.7 18.2 %collective-permute-start.5 = (bf16[512,1024]{1,0:T(8,128)(2,1)}, bf16[512,1024]{1,0:T(8,128)(2,1)S(1)}, u32[]{:S(2)}, u32[]{:S(2)}) collective-permute-start(bf16[512,1024]{1,0:T(8,128)(2,1)} %collective-permute-done.4.v_ref), channel_id=1, source_target_pairs={{0,1},{2,3},{4,5},{6,7},{8,9},{10,11},{12,13},{14,15},{16,17},{18,... | collective-permute-start | bytes 3145736 | tf_op jit(solution)/shard_map/ppermute | solution.py:462

commit v7 on v6

--- a/solution.py
+++ b/solution.py
@@ -21,6 +21,7 @@
 START = 2 * HQ
 PARTS = 3
 VMEM = 16 << 20
+FEW = 128
 INTERPRET = False
 
 SLOT = 256
@@ -55,11 +56,14 @@
         weights = jnp.exp2((scores - top) * RATE)
         rounded = weights.astype(jnp.bfloat16).reshape(GROUPS * rows, -1)
         value = values(head)
-        value = jnp.concatenate([value, jnp.ones_like(value)], axis=1)
+        few = value.shape[0] <= FEW
+        if not few:
+            value = jnp.concatenate([value, jnp.ones_like(value)], axis=1)
         mixed = lax.dot_general(rounded, value, (((1,), (0,)), ((), ())), preferred_element_type=jnp.float32)
-        mixed = mixed.reshape(GROUPS, rows, 2 * DH)
+        mixed = mixed.reshape(GROUPS, rows, -1)
+        totals = jnp.sum(weights, axis=-1, keepdims=True) if few else mixed[:, :, DH:]
         for g in range(GROUPS):
-            emit(head, g, mixed[g, :, :DH], mixed[g, :, DH:], top[g])
+            emit(head, g, mixed[g, :, :DH], totals[g], top[g])
 
 
 def heads_of(ref, rows=slice(None), at=0):
@@ -223,13 +227,14 @@
 
 def next_kernel(
     first_ref, mark_ref, q_ref, k_ref, v_ref, acc_ref, state_ref, spread_ref, prior_ref, out_ref, new_acc_ref, new_state_ref,
-    done_ref, fresh_ref, sem,
+    done_ref, fresh_all_ref, sem,
 ):
     keys = k_ref.shape[0]
     first = first_ref[0].astype(jnp.float32)
     base = first - keys
     blocks = q_ref.shape[0] // BQ
     copy = writer(done_ref, out_ref, sem)
+    fresh_ref = fresh_all_ref.at[0]
 
     def finishes(block):
         return (mark_ref[block] < first) & (mark_ref[block] >= base)
@@ -285,16 +290,22 @@
 
         mix(keep, lambda cols: acc_ref[rows, cols], take, added, spread_ref, put)
 
-    def merge(block, tall, ref_k, ref_v, at, count):
+    def merge(block, tall, ref_k, ref_v, at, count, fresh):
         rows = pl.ds(pl.multiple_of(block * BQ, BQ), tall * BQ)
         state = state_ref[rows, :]
         skip = ref_k.shape[0] - count
         part = slice(skip, skip + count)
         bias = jnp.where(float_iota((tall * BQ, count), 1) >= column(state, START) - (base - count), 0.0, HIDDEN)
-        emit, held = collect(fresh_ref, tall * BQ)
+        emit, held = collect(fresh, tall * BQ)
         attend(pairs_of(q_ref, rows), heads_of(ref_k, part), heads_of(ref_v, part, at), bias, emit)
-        keep, take, _, _ = joined(state, held[0])
-        write(rows, keep, take, lambda cols: fresh_ref[: tall * BQ, cols])
+
+        def finish():
+            keep, take, _, _ = joined(state, held[0])
+            write(rows, keep, take, lambda cols: fresh[: tall * BQ, cols])
+            for i in range(tall):
+                pl.when(mark_ref[block + i] < base)(copy(block + i).start)
+
+        return finish
 
     def combine(block):
         rows = rows_at(block)
@@ -318,18 +329,36 @@
                 @pl.when(mark_ref[block] < base)
                 def _():
                     work(block)
-                    for i in range(tall):
-                        pl.when(mark_ref[block + i] < base)(copy(block + i).start)
 
     near = start >= base - BQ
     far = start < base - SLOT
     some = jnp.logical_not(near | far)
-    sweep(odd & near, 2, lambda block: merge(block, 2, k_ref, v_ref, 0, BQ))
-    sweep(odd & some, 1, lambda block: merge(block, 1, k_ref, v_ref, 0, SLOT))
-    sweep(odd & far, 1, lambda block: merge(block, 1, k_ref, v_ref, 0, keys))
-    sweep(even & by_keys & near, 2, lambda block: merge(block, 2, slot_ref, slot_ref, KV, BQ))
-    sweep(even & by_keys & jnp.logical_not(near), 1, lambda block: merge(block, 1, slot_ref, slot_ref, KV, SLOT))
-    sweep(even & jnp.logical_not(by_keys), 1, combine, SLOT // BQ)
+    sweep(odd & near, 2, lambda block: merge(block, 2, k_ref, v_ref, 0, BQ, fresh_ref.at[0])())
+    sweep(odd & some, 1, lambda block: merge(block, 1, k_ref, v_ref, 0, SLOT, fresh_ref.at[0])())
+    sweep(odd & far, 1, lambda block: merge(block, 1, k_ref, v_ref, 0, keys, fresh_ref.at[0])())
+
+    def with_slot(count):
+        pending = None
+        for block in range(SLOT // BQ + 1):
+            finish = merge(block, 1, slot_ref, slot_ref, KV, count, fresh_ref.at[block % 2])
+            if pending is not None:
+                pending()
+            pending = finish
+        pending()
+        if count == BQ:
+            pl.when(mark_ref[blocks - 1] < base)(
+                lambda: merge(blocks - 1, 1, slot_ref, slot_ref, KV, count, fresh_ref.at[1])()
+            )
+
+    travelled = even & by_keys & (start < base)
+    pl.when(travelled & near)(functools.partial(with_slot, BQ))
+    pl.when(travelled & jnp.logical_not(near))(functools.partial(with_slot, SLOT))
+
+    def combined(block):
+        combine(block)
+        copy(block).start()
+
+    sweep(even & jnp.logical_not(by_keys), 1, combined, SLOT // BQ)
 
     @pl.loop(0, blocks)
     def _(block):
@@ -415,7 +444,7 @@
 def writing(rows):
     return [
         pltpu.VMEM((rows, WIDE), jnp.bfloat16),
-        pltpu.VMEM((2 * BQ, WIDE), jnp.float32),
+        pltpu.VMEM((2, 2 * BQ, WIDE), jnp.float32),
         pltpu.SemaphoreType.DMA((rows // BQ,)),
     ]
 

time: 71.7 us -> 71.8 us (level)
  transfers between devices with their start and end apart: 6 -> 6, of which waited for: 3 -> 3; matrix products, arithmetic and copies ran while one was open for 0% -> 0% of each run, Pallas kernels for 26% -> 25%
where the time goes in v7:
time: 71.8 us; the launch traced here: 71.5 us
  waiting for transfers between devices  27.6 us (38%)
  Pallas kernels  27.2 us (38%)
  starting transfers between devices  16.4 us (23%)
    ppermute x6, waiting for transfers between devices, hop(): return lax.ppermute(array, 'cp', pairs)  27.6 us
    ppermute x6, starting transfers between devices, hop(): return lax.ppermute(array, 'cp', pairs)  16.4 us
    pallas_call x1, Pallas kernels, next_stage(): pl.pallas_call(next_kernel, in_specs=[SMEM] * 2 + [WHOLE] * 6 + [ANY], ou...  9.79 us
    pallas_call x1, Pallas kernels, last_stage(): pl.pallas_call(last_kernel, in_specs=[SMEM] * 2 + [WHOLE] * 7 + [ANY], ou...  6.68 us
    pallas_call x1, Pallas kernels, own_stage(): pl.pallas_call(own_kernel, grid=(rows // BQ,), in_specs=[SMEM, WHOLE, row...  6.62 us
    pallas_call x1, Pallas kernels, leading_rows(): pl.pallas_call(copy_kernel, in_specs=[pl.BlockSpec(memory_space=pltpu.HBM...  2.35 us
    pallas_call x1, Pallas kernels, back_stage(): pl.pallas_call(back_kernel, grid=(SLOT // BQ,), in_specs=[SMEM, WHOLE, ro...  1.76 us
  transfers between devices with their start and end apart: 6, of which 3 were waited for; matrix products, arithmetic and copies ran while one was open for 0% of the time, Pallas kernels for 25%

profile of v7, /device:TPU:20, one launch (start us, length us, event | category | flops | bytes accessed | tf_op | source)
XLA Modules:
  0.0 71.5 jit_solution(9614843186743189288)
XLA Ops:
  0.0 0.0 copy-start.1
  0.0 0.0 copy-start.2
  0.0 0.0 copy-start.3
  0.0 2.4 %leading_rows.1 = bf16[256,2048]{1,0:T(8,128)(2,1)} custom-call(bf16[512,2048]{1,0:T(8,128)(2,1)} %q_ref.5), custom_call_target="tpu_custom_call" | custom-call | tf_op jit(solution)/shard_map/leading_rows/pallas_call | solution.py:418
  2.4 7.7 %collective-permute-start = (bf16[256,2048]{1,0:T(8,128)(2,1)}, bf16[256,2048]{1,0:T(8,128)(2,1)}, u32[]{:S(2)}, u32[]{:S(2)}) collective-permute-start(bf16[256,2048]{1,0:T(8,128)(2,1)} %leading_rows.1), channel_id=1, source_target_pairs={{2,0},{4,2},{6,4},{8,6},{10,8},{12,10},{14,12},{16,14},{18,16},{20... | collective-permute-start | bytes 3145736 | tf_op jit(solution)/shard_map/ppermute | solution.py:491
  10.1 0.0 copy-done.1
  10.1 1.9 %collective-permute-start.2 = (bf16[512,1024]{1,0:T(8,128)(2,1)S(1)}, bf16[512,1024]{1,0:T(8,128)(2,1)S(1)}, u32[]{:S(2)}, u32[]{:S(2)}) collective-permute-start(bf16[512,1024]{1,0:T(8,128)(2,1)S(1)} %copy-done.1), channel_id=1, source_target_pairs={{0,1},{1,2},{2,3},{3,4},{4,5},{5,6},{6,7},{7,8},{8,9},{9,10},{10,1... | collective-permute-start | bytes 3145736 | tf_op jit(solution)/shard_map/ppermute | solution.py:491
  12.1 0.0 copy-done.2
  12.1 1.9 %collective-permute-start.4 = (bf16[512,1024]{1,0:T(8,128)(2,1)S(1)}, bf16[512,1024]{1,0:T(8,128)(2,1)}, u32[]{:S(2)}, u32[]{:S(2)}) collective-permute-start(bf16[512,1024]{1,0:T(8,128)(2,1)S(1)} %copy-done.2), channel_id=1, source_target_pairs={{0,1},{1,2},{2,3},{3,4},{4,5},{5,6},{6,7},{7,8},{8,9},{9,10},{10,1... | collective-permute-start | bytes 3145736 | tf_op jit(solution)/shard_map/ppermute | solution.py:491
  14.0 8.7 %collective-permute-done.q_ref = bf16[256,2048]{1,0:T(8,128)(2,1)} collective-permute-done((bf16[256,2048]{1,0:T(8,128)(2,1)}, bf16[256,2048]{1,0:T(8,128)(2,1)}, u32[]{:S(2)}, u32[]{:S(2)}) %collective-permute-start) | collective-permute-done | bytes 1048608 | tf_op jit(solution)/shard_map/ppermute | solution.py:491
  22.7 0.0 copy-done.3
  22.7 0.0 copy-start
  22.7 1.8 %back_shard.1 = bf16[256,2176]{1,0:T(8,128)(2,1)S(1)} custom-call(s32[1]{0:T(128)} %bitcast.first_ref, s32[1,256]{1,0:T(1,128)S(1)} %bitcast.2, bf16[256,2048]{1,0:T(8,128)(2,1)} %collective-permute-done.q_ref, bf16[512,1024]{1,0:T(8,128)(2,1)S(1)} %copy-done.1, bf16[512,1024]{1,0:T(8,128)(2,1)S(1)} %copy-done.2), custom_call_target="tpu_custom_call" | custom-call | flops 1073741824 | bytes 4194304 | tf_op jit(solution)/shard_map/back_shard/pallas_call | solution.py:431
  24.5 1.9 %collective-permute-start.1 = (bf16[256,2176]{1,0:T(8,128)(2,1)S(1)}, bf16[256,2176]{1,0:T(8,128)(2,1)S(1)}, u32[]{:S(2)}, u32[]{:S(2)}) collective-permute-start(bf16[256,2176]{1,0:T(8,128)(2,1)S(1)} %back_shard.1), channel_id=1, source_target_pairs={{0,2},{2,4},{4,6},{6,8},{8,10},{10,12},{12,14},{14,16},{16,18},{18... | collective-permute-start | bytes 3342344 | tf_op jit(solution)/shard_map/ppermute | solution.py:491
  26.4 1.9 %collective-permute-done.2.k_ref = bf16[512,1024]{1,0:T(8,128)(2,1)S(1)} collective-permute-done((bf16[512,1024]{1,0:T(8,128)(2,1)S(1)}, bf16[512,1024]{1,0:T(8,128)(2,1)S(1)}, u32[]{:S(2)}, u32[]{:S(2)}) %collective-permute-start.2) | collective-permute-done | bytes 1048608 | tf_op jit(solution)/shard_map/ppermute | solution.py:491
  28.4 1.3 %collective-permute-start.3 = (bf16[512,1024]{1,0:T(8,128)(2,1)S(1)}, bf16[512,1024]{1,0:T(8,128)(2,1)S(1)}, u32[]{:S(2)}, u32[]{:S(2)}) collective-permute-start(bf16[512,1024]{1,0:T(8,128)(2,1)S(1)} %collective-permute-done.2.k_ref), channel_id=1, source_target_pairs={{0,1},{2,3},{4,5},{6,7},{8,9},{10,11},{12,13},{14,15},{16,17},{18,... | collective-permute-start | bytes 3145736 | tf_op jit(solution)/shard_map/ppermute | solution.py:491
  29.7 17.0 %collective-permute-done.4.v_ref = bf16[512,1024]{1,0:T(8,128)(2,1)} collective-permute-done((bf16[512,1024]{1,0:T(8,128)(2,1)S(1)}, bf16[512,1024]{1,0:T(8,128)(2,1)}, u32[]{:S(2)}, u32[]{:S(2)}) %collective-permute-start.4) | collective-permute-done | bytes 1048608 | tf_op jit(solution)/shard_map/ppermute | solution.py:491
  46.7 1.5 %collective-permute-start.5 = (bf16[512,1024]{1,0:T(8,128)(2,1)}, bf16[512,1024]{1,0:T(8,128)(2,1)S(1)}, u32[]{:S(2)}, u32[]{:S(2)}) collective-permute-start(bf16[512,1024]{1,0:T(8,128)(2,1)} %collective-permute-done.4.v_ref), channel_id=1, source_target_pairs={{0,1},{2,3},{4,5},{6,7},{8,9},{10,11},{12,13},{14,15},{16,17},{18,... | collective-permute-start | bytes 3145736 | tf_op jit(solution)/shard_map/ppermute | solution.py:491
  48.2 0.0 copy-done
  48.2 6.6 %own_shard.1 = (f32[512,2048]{1,0:T(8,128)S(1)}, f32[512,128]{1,0:T(8,128)S(1)}, bf16[128,2048]{1,0:T(8,128)(2,1)S(1)}, bf16[512,2048]{1,0:T(8,128)(2,1)}, f32[4]{0:T(128)S(1)}) custom-call(s32[1]{0:T(128)} %bitcast.first_ref, s32[1,256]{1,0:T(1,128)S(1)} %bitcast.3, bf16[512,2048]{1,0:T(8,128)(2,1)S(1)} %copy-done, bf16[512,1024]{1,0:T(8,128)(2,1)S(1)} %copy-done.1, ...), custom_call_target="tpu_custom_call" | custom-call | flops 2147483648 | bytes 8388608 | tf_op jit(solution)/shard_map/own_shard/pallas_call | solution.py:397
  54.8 9.8 %next_shard.1 = (bf16[512,2048]{1,0:T(8,128)(2,1)}, f32[512,2048]{1,0:T(8,128)S(1)}, f32[512,128]{1,0:T(8,128)S(1)}) custom-call(s32[1]{0:T(128)} %bitcast.first_ref, f32[4]{0:T(128)S(1)} %get-tuple-element.13.mark_ref, bf16[512,2048]{1,0:T(8,128)(2,1)S(1)} %copy-done, ...), custom_call_target="tpu_custom_call", output_to_operand_aliasing={{0}: (8, {})} | custom-call | flops 2147483648 | bytes 8388608 | tf_op jit(solution)/shard_map/next_shard/pallas_call | solution.py:454
  64.7 0.0 collective-permute-done.3.k_ref
  64.7 0.0 collective-permute-done.5.v_ref
  64.7 0.0 collective-permute-done.1.slot_ref
  64.7 6.7 %last_shard.1 = bf16[512,2048]{1,0:T(8,128)(2,1)} custom-call(s32[1]{0:T(128)} %bitcast.first_ref, f32[4]{0:T(128)S(1)} %get-tuple-element.13.mark_ref, bf16[512,2048]{1,0:T(8,128)(2,1)S(1)} %copy-done, bf16[256,2176]{1,0:T(8,128)(2,1)S(1)} %collective-permute-done.1.slot_ref, ...), custom_call_target="tpu_custom_call", output_to_operand_aliasing={{}: (9, {})} | custom-call | flops 1073741824 | bytes 8388608 | tf_op jit(solution)/shard_map/last_shard/pallas_call | solution.py:470
Async XLA Ops:
  0.0 10.1 %copy-start.1 = (bf16[512,1024]{1,0:T(8,128)(2,1)S(1)}, bf16[512,1024]{1,0:T(8,128)(2,1)}, u32[]{:S(2)}) copy-start(bf16[512,1024]{1,0:T(8,128)(2,1)} %k_ref.3) | copy-start | bytes 3145732
  0.0 12.1 %copy-start.2 = (bf16[512,1024]{1,0:T(8,128)(2,1)S(1)}, bf16[512,1024]{1,0:T(8,128)(2,1)}, u32[]{:S(2)}) copy-start(bf16[512,1024]{1,0:T(8,128)(2,1)} %v_ref.3) | copy-start | bytes 3145732
  0.0 22.7 %copy-start.3 = (s32[256]{0:T(256)S(1)}, s32[256]{0:T(256)}, u32[]{:S(2)}) copy-start(s32[256]{0:T(256)} %param.7) | copy-start | bytes 3076
  2.4 20.4 %collective-permute-start = (bf16[256,2048]{1,0:T(8,128)(2,1)}, bf16[256,2048]{1,0:T(8,128)(2,1)}, u32[]{:S(2)}, u32[]{:S(2)}) collective-permute-start(bf16[256,2048]{1,0:T(8,128)(2,1)} %leading_rows.1), channel_id=1, source_target_pairs={{2,0},{4,2},{6,4},{8,6},{10,8},{12,10},{14,12},{16,14},{18,16},{20... | collective-permute-start | bytes 3145736 | tf_op jit(solution)/shard_map/ppermute | solution.py:491
  10.1 18.2 %collective-permute-start.2 = (bf16[512,1024]{1,0:T(8,128)(2,1)S(1)}, bf16[512,1024]{1,0:T(8,128)(2,1)S(1)}, u32[]{:S(2)}, u32[]{:S(2)}) collective-permute-start(bf16[512,1024]{1,0:T(8,128)(2,1)S(1)} %copy-done.1), channel_id=1, source_target_pairs={{0,1},{1,2},{2,3},{3,4},{4,5},{5,6},{6,7},{7,8},{8,9},{9,10},{10,1... | collective-permute-start | bytes 3145736 | tf_op jit(solution)/shard_map/ppermute | solution.py:491
  12.1 34.6 %collective-permute-start.4 = (bf16[512,1024]{1,0:T(8,128)(2,1)S(1)}, bf16[512,1024]{1,0:T(8,128)(2,1)}, u32[]{:S(2)}, u32[]{:S(2)}) collective-permute-start(bf16[512,1024]{1,0:T(8,128)(2,1)S(1)} %copy-done.2), channel_id=1, source_target_pairs={{0,1},{1,2},{2,3},{3,4},{4,5},{5,6},{6,7},{7,8},{8,9},{9,10},{10,1... | collective-permute-start | bytes 3145736 | tf_op jit(solution)/shard_map/ppermute | solution.py:491
  22.7 25.5 %copy-start = (bf16[512,2048]{1,0:T(8,128)(2,1)S(1)}, bf16[512,2048]{1,0:T(8,128)(2,1)}, u32[]{:S(2)}) copy-start(bf16[512,2048]{1,0:T(8,128)(2,1)} %q_ref.5) | copy-start | bytes 6291460
  24.5 40.2 %collective-permute-start.1 = (bf16[256,2176]{1,0:T(8,128)(2,1)S(1)}, bf16[256,2176]{1,0:T(8,128)(2,1)S(1)}, u32[]{:S(2)}, u32[]{:S(2)}) collective-permute-start(bf16[256,2176]{1,0:T(8,128)(2,1)S(1)} %back_shard.1), channel_id=1, source_target_pairs={{0,2},{2,4},{4,6},{6,8},{8,10},{10,12},{12,14},{14,16},{16,18},{18... | collective-permute-start | bytes 3342344 | tf_op jit(solution)/shard_map/ppermute | solution.py:491
  28.4 36.3 %collective-permute-start.3 = (bf16[512,1024]{1,0:T(8,128)(2,1)S(1)}, bf16[512,1024]{1,0:T(8,128)(2,1)S(1)}, u32[]{:S(2)}, u32[]{:S(2)}) collective-permute-start(bf16[512,1024]{1,0:T(8,128)(2,1)S(1)} %collective-permute-done.2.k_ref), channel_id=1, source_target_pairs={{0,1},{2,3},{4,5},{6,7},{8,9},{10,11},{12,13},{14,15},{16,17},{18,... | collective-permute-start | bytes 3145736 | tf_op jit(solution)/shard_map/ppermute | solution.py:491
  46.7 18.0 %collective-permute-start.5 = (bf16[512,1024]{1,0:T(8,128)(2,1)}, bf16[512,1024]{1,0:T(8,128)(2,1)S(1)}, u32[]{:S(2)}, u32[]{:S(2)}) collective-permute-start(bf16[512,1024]{1,0:T(8,128)(2,1)} %collective-permute-done.4.v_ref), channel_id=1, source_target_pairs={{0,1},{2,3},{4,5},{6,7},{8,9},{10,11},{12,13},{14,15},{16,17},{18,... | collective-permute-start | bytes 3145736 | tf_op jit(solution)/shard_map/ppermute | solution.py:491

commit v8 on v6

v8 whole, which is shorter than its diff:
```python
import functools
import math

import jax
import jax.numpy as jnp
from jax import lax
from jax.experimental import pallas as pl
from jax.experimental.pallas import tpu as pltpu
from jax.sharding import PartitionSpec as P


HQ = 16
HK = 8
DH = 128
GROUPS = HQ // HK
WIDTH = GROUPS * DH
KV = HK * DH
BQ = 128
HIDDEN = -1e30
RATE = math.log2(math.e) * 144.0 ** -0.5
PARTS = 3
VMEM = 16 << 20
FEW = 128
INTERPRET = False

SLOT = 256


def document_ends(lengths):
    docs = lengths.shape[1]
    sub = lax.broadcasted_iota(jnp.int32, (docs, docs), 0)
    lane = lax.broadcasted_iota(jnp.int32, (docs, docs), 1)
    rows = jnp.broadcast_to(lengths.astype(jnp.float32), (docs, docs))
    column = jnp.sum(jnp.where(sub == lane, rows, 0.0), axis=1, keepdims=True)
    return jnp.sum(jnp.where(sub <= lane, column, 0.0), axis=0, keepdims=True)


def float_iota(shape, axis):
    return lax.broadcasted_iota(jnp.int32, shape, axis).astype(jnp.float32)


def attend(pair, keys, values, bias, emit, before=None):
    rows = bias.shape[0]

    def score(head):
        return lax.dot_general(pair(head), keys(head), (((1,), (1,)), ((), ())), preferred_element_type=jnp.float32)

    ahead = score(0)
    for head in range(HK):
        scores = ahead
        if head + 1 < HK:
            ahead = score(head + 1)
        scores = scores.reshape(GROUPS, rows, -1) + bias[None]
        top = jnp.max(scores, axis=-1, keepdims=True)
        if before is not None:
            top = jnp.maximum(top, jnp.stack([before(head * GROUPS + g) for g in range(GROUPS)]))
        wide = top if before is None else jnp.concatenate([top] * (scores.shape[-1] // DH), axis=-1)
        weights = jnp.exp2((scores - wide) * RATE)
        rounded = weights.astype(jnp.bfloat16).reshape(GROUPS * rows, -1)
        value = values(head)
        few = value.shape[0] <= FEW
        if not few:
            value = jnp.concatenate([value, jnp.ones_like(value)], axis=1)
        mixed = lax.dot_general(rounded, value, (((1,), (0,)), ((), ())), preferred_element_type=jnp.float32)
        mixed = mixed.reshape(GROUPS, rows, -1)
        totals = jnp.sum(weights, axis=-1, keepdims=True) if few else mixed[:, :, DH:]
        for g in range(GROUPS):
            emit(head * GROUPS + g, mixed[g, :, :DH], totals[g], top[g])


def columns(h):
    return slice(h * DH, (h + 1) * DH)


def heads_of(ref, rows=slice(None), at=0):
    return lambda head: ref[rows, at + head * DH : at + (head + 1) * DH]


def pairs_of(ref, rows=slice(None)):
    def pair(head):
        both = ref[rows, head * WIDTH : (head + 1) * WIDTH]
        return jnp.concatenate([both[:, :DH], both[:, DH:]], axis=0)

    return pair


def in_parts(table):
    rest = jnp.where(lax.broadcasted_iota(jnp.int32, table.shape, 1) < HQ, table, 0.0)
    parts = jnp.zeros_like(table)
    for part in range(PARTS):
        piece = rest.astype(jnp.bfloat16).astype(jnp.float32)
        parts = parts + (pltpu.roll(piece, part * HQ, 1) if part else piece)
        rest = rest - piece
    return parts.astype(jnp.bfloat16)


def own_kernel(
    first_ref, len_ref, q_ref, k_ref, v_ref, acc_ref, level_ref, start_ref, out_ref, mark_ref, ends_ref
):
    block = pl.program_id(0)

    @pl.when(block == 0)
    def _():
        ends_ref[...] = document_ends(len_ref[...])

    ends = ends_ref[...]
    first = first_ref[0].astype(jnp.float32)
    row = float_iota((BQ, 1), 0) + (block * BQ).astype(jnp.float32)
    start = jnp.max(jnp.where(ends <= row + first, ends, 0.0), axis=1, keepdims=True)
    mark_ref[block] = jnp.min(start)
    start_ref[...] = jnp.broadcast_to(start, start_ref.shape)

    def over(count):
        col = float_iota((BQ, count), 1)
        bias = jnp.where((col >= start - first) & (col <= row), 0.0, HIDDEN)

        def emit(h, mixed, total, top):
            mixed = mixed * (1.0 / total)
            acc_ref[:, columns(h)] = mixed
            out_ref[:, columns(h)] = mixed.astype(out_ref.dtype)
            level_ref[:, columns(h)] = jnp.broadcast_to(top + jnp.log2(total) * (1.0 / RATE), (BQ, DH))

        part = slice(0, count)
        attend(pairs_of(q_ref), heads_of(k_ref, part), heads_of(v_ref, part), bias, emit)

    for step in range(k_ref.shape[0] // BQ):
        pl.when(block == step)(functools.partial(over, (step + 1) * BQ))


def back_kernel(first_ref, len_ref, q_ref, k_ref, v_ref, slot_ref):
    first = first_ref[0]
    here = first.astype(jnp.float32)
    keys = k_ref.shape[0]
    block = pl.program_id(0)

    @pl.when((first // keys) % 2 == 0)
    def _():
        ends = document_ends(len_ref[...])
        edge = here + 2 * keys
        start = jnp.max(jnp.where(ends <= edge, ends, 0.0))
        right = jnp.min(jnp.where(ends > edge, ends, edge + edge)) - edge
        reached = start < here + keys
        by_keys = right > SLOT

        @pl.when(reached & by_keys)
        def _():
            rows = pl.ds(keys - SLOT + block * BQ, BQ)
            slot_ref[:, :KV] = k_ref[rows, :]
            slot_ref[:, KV : 2 * KV] = v_ref[rows, :]

        def over(count):
            row = float_iota((BQ, 1), 0) + (block * BQ).astype(jnp.float32)
            col = float_iota((BQ, count), 1)
            bias = jnp.where((col >= start - (here + keys - count)) & (row < right), 0.0, HIDDEN)
            lane = lax.broadcasted_iota(jnp.int32, (BQ, 128), 1)
            level = [jnp.zeros((BQ, 128), jnp.float32)]

            def emit(h, mixed, total, top):
                slot_ref[:, columns(h)] = (mixed * (1.0 / total)).astype(jnp.bfloat16)
                level[0] = jnp.where(lane == h, top * RATE + jnp.log2(total), level[0])

            part = slice(keys - count, keys)
            attend(pairs_of(q_ref), heads_of(k_ref, part), heads_of(v_ref, part), bias, emit)
            slot_ref[:, 2 * KV :] = in_parts(level[0])

        working = reached & jnp.logical_not(by_keys) & ((block * BQ).astype(jnp.float32) < right)
        length = here + keys - start
        pl.when(working & (length <= 256))(functools.partial(over, 256))
        pl.when(working & (length > 256) & (length <= 384))(functools.partial(over, 384))
        pl.when(working & (length > 384))(functools.partial(over, keys))


def rows_at(block):
    return pl.ds(pl.multiple_of(block * BQ, BQ), BQ)


def writer(done_ref, out_ref, sem):
    def copy(block):
        return pltpu.make_async_copy(done_ref.at[rows_at(block), :], out_ref.at[rows_at(block), :], sem.at[block])

    return copy


def added(rows, acc_ref, level_ref, write):
    def emit(h, mixed, total, top):
        keep = jnp.exp2((level_ref[rows, columns(h)] - top) * RATE)
        total = total + keep
        mixed = (mixed + keep * acc_ref[rows, columns(h)]) * (1.0 / total)
        write(h, mixed, lambda: top + jnp.log2(total) * (1.0 / RATE))

    return emit


def levels_of(level_ref, rows):
    return lambda h: level_ref[rows, columns(h)]


def next_kernel(
    first_ref, mark_ref, q_ref, k_ref, v_ref, acc_ref, level_ref, start_ref, prior_ref, out_ref, new_acc_ref,
    new_level_ref, done_ref, sem,
):
    keys = k_ref.shape[0]
    first = first_ref[0].astype(jnp.float32)
    base = first - keys
    blocks = q_ref.shape[0] // BQ
    copy = writer(done_ref, out_ref, sem)

    def finishes(block):
        return (mark_ref[block] < first) & (mark_ref[block] >= base)

    @pl.loop(0, blocks)
    def _(block):
        @pl.when(mark_ref[block] < first)
        def _():
            rows = rows_at(block)
            bias = jnp.where(float_iota((BQ, keys), 1) >= start_ref[rows, :1] - base, 0.0, HIDDEN)

            def write(h, mixed, level):
                new_acc_ref[rows, columns(h)] = mixed
                done_ref[rows, columns(h)] = mixed.astype(done_ref.dtype)
                new_level_ref[rows, columns(h)] = level()

            emit = added(rows, acc_ref, level_ref, write)
            attend(
                pairs_of(q_ref, rows), heads_of(k_ref), heads_of(v_ref), bias, emit, levels_of(level_ref, rows)
            )

        pl.when(finishes(block))(lambda: copy(block).start())

    @pl.loop(0, blocks)
    def _(block):
        pl.when(finishes(block))(lambda: copy(block).wait())


def last_kernel(
    first_ref, mark_ref, q_ref, slot_ref, k_ref, v_ref, acc_ref, level_ref, start_ref, prior_ref, out_ref,
    done_ref, sem,
):
    keys = k_ref.shape[0]
    first = first_ref[0].astype(jnp.float32)
    odd = (first_ref[0] // keys) % 2 == 1
    even = jnp.logical_not(odd)
    base = first - keys
    blocks = q_ref.shape[0] // BQ
    start = mark_ref[0]
    by_keys = mark_ref[SLOT // BQ] < first
    copy = writer(done_ref, out_ref, sem)

    def merge(block, ref_k, ref_v, at, count):
        rows = rows_at(block)
        skip = ref_k.shape[0] - count
        part = slice(skip, skip + count)
        bias = jnp.where(float_iota((BQ, count), 1) >= start_ref[rows, :1] - (base - count), 0.0, HIDDEN)

        def write(h, mixed, level):
            done_ref[rows, columns(h)] = mixed.astype(done_ref.dtype)

        emit = added(rows, acc_ref, level_ref, write)
        attend(
            pairs_of(q_ref, rows), heads_of(ref_k, part), heads_of(ref_v, part, at), bias, emit,
            levels_of(level_ref, rows),
        )

    def combine(block):
        rows = rows_at(block)
        parts = slot_ref[rows, 2 * KV :].astype(jnp.float32)
        there = parts
        for part in range(1, PARTS):
            there = there + pltpu.roll(parts, 128 - part * HQ, 1)
        for h in range(HQ):
            here = level_ref[rows, columns(h)] * RATE
            other = jnp.broadcast_to(there[:, h : h + 1], here.shape)
            top = jnp.maximum(here, other)
            keep, take = jnp.exp2(here - top), jnp.exp2(other - top)
            mixed = keep * acc_ref[rows, columns(h)] + take * slot_ref[rows, columns(h)].astype(jnp.float32)
            done_ref[rows, columns(h)] = (mixed * (1.0 / (keep + take))).astype(done_ref.dtype)

    def sweep(condition, work, end=blocks):
        @pl.when(condition & (start < base))
        def _():
            @pl.loop(0, end)
            def _(block):
                @pl.when(mark_ref[block] < base)
                def _():
                    work(block)
                    copy(block).start()

    near = start >= base - BQ
    far = start < base - SLOT
    some = jnp.logical_not(near | far)
    sweep(odd & near, lambda block: merge(block, k_ref, v_ref, 0, BQ))
    sweep(odd & some, lambda block: merge(block, k_ref, v_ref, 0, SLOT))
    sweep(odd & far, lambda block: merge(block, k_ref, v_ref, 0, keys))
    sweep(even & by_keys & near, lambda block: merge(block, slot_ref, slot_ref, KV, BQ))
    sweep(even & by_keys & jnp.logical_not(near), lambda block: merge(block, slot_ref, slot_ref, KV, SLOT))
    sweep(even & jnp.logical_not(by_keys), combine, SLOT // BQ)

    @pl.loop(0, blocks)
    def _(block):
        pl.when(mark_ref[block] < base)(lambda: copy(block).wait())


def rows_of(width):
    return pl.BlockSpec((BQ, width), lambda i: (i, 0))


SMEM = pl.BlockSpec(memory_space=pltpu.SMEM)
WHOLE = pl.BlockSpec(memory_space=pltpu.VMEM)
ANY = pl.BlockSpec(memory_space=pl.ANY)
WIDE = HQ * DH


def cost(rows, keys):
    return pl.CostEstimate(
        flops=4 * rows * keys * WIDE, bytes_accessed=rows * WIDE * 8, transcendentals=rows * keys * HQ
    )


PARAMS = pltpu.CompilerParams(vmem_limit_bytes=VMEM)


def f32(*shape):
    return jax.ShapeDtypeStruct(shape, jnp.float32)


def bf16(*shape):
    return jax.ShapeDtypeStruct(shape, jnp.bfloat16)


def own_stage(first, lengths, queries, keys, values):
    rows = queries.shape[0]
    return pl.pallas_call(
        own_kernel,
        grid=(rows // BQ,),
        in_specs=[SMEM, WHOLE, rows_of(WIDE), WHOLE, WHOLE],
        out_specs=[rows_of(WIDE), rows_of(WIDE), rows_of(128), rows_of(WIDE), SMEM],
        out_shape=[f32(rows, WIDE), f32(rows, WIDE), f32(rows, 128), bf16(rows, WIDE), f32(rows // BQ)],
        scratch_shapes=[pltpu.VMEM(lengths.shape, jnp.float32)],
        cost_estimate=cost(rows, keys.shape[0]),
        compiler_params=PARAMS,
        name="own_shard",
        interpret=INTERPRET,
    )(first, lengths, queries, keys, values)


def copy_kernel(in_ref, out_ref, sem):
    copy = pltpu.make_async_copy(in_ref.at[pl.ds(0, out_ref.shape[0]), :], out_ref, sem)
    copy.start()
    copy.wait()


def leading_rows(array, rows):
    return pl.pallas_call(
        copy_kernel,
        in_specs=[pl.BlockSpec(memory_space=pltpu.HBM)],
        out_specs=WHOLE,
        out_shape=jax.ShapeDtypeStruct((rows, array.shape[1]), array.dtype),
        scratch_shapes=[pltpu.SemaphoreType.DMA],
        compiler_params=PARAMS,
        name="leading_rows",
        interpret=INTERPRET,
    )(pltpu.with_memory_space_constraint(array, pltpu.HBM))


def back_stage(first, lengths, queries, keys, values):
    return pl.pallas_call(
        back_kernel,
        grid=(SLOT // BQ,),
        in_specs=[SMEM, WHOLE, rows_of(WIDE), WHOLE, WHOLE],
        out_specs=rows_of(2 * KV + 128),
        out_shape=bf16(SLOT, 2 * KV + 128),
        cost_estimate=cost(SLOT, keys.shape[0]),
        compiler_params=PARAMS,
        name="back_shard",
        interpret=INTERPRET,
    )(first, lengths, queries, keys, values)


def writing(rows):
    return [
        pltpu.VMEM((rows, WIDE), jnp.bfloat16),
        pltpu.SemaphoreType.DMA((rows // BQ,)),
    ]


def next_stage(first, marks, queries, keys, values, acc, levels, starts, prior):
    rows = queries.shape[0]
    return pl.pallas_call(
        next_kernel,
        in_specs=[SMEM] * 2 + [WHOLE] * 6 + [ANY],
        out_specs=[ANY, WHOLE, WHOLE],
        out_shape=[bf16(rows, WIDE), f32(rows, WIDE), f32(rows, WIDE)],
        scratch_shapes=writing(rows),
        input_output_aliases={8: 0},
        cost_estimate=cost(rows, keys.shape[0]),
        compiler_params=PARAMS,
        name="next_shard",
        interpret=INTERPRET,
    )(first, marks, queries, keys, values, acc, levels, starts, prior)


def last_stage(first, marks, queries, slot, keys, values, acc, levels, starts, prior):
    rows = queries.shape[0]
    return pl.pallas_call(
        last_kernel,
        in_specs=[SMEM] * 2 + [WHOLE] * 7 + [ANY],
        out_specs=ANY,
        out_shape=bf16(rows, WIDE),
        scratch_shapes=writing(rows),
        input_output_aliases={9: 0},
        cost_estimate=cost(rows, SLOT),
        compiler_params=PARAMS,
        name="last_shard",
        interpret=INTERPRET,
    )(first, marks, queries, slot, keys, values, acc, levels, starts, prior)


def on_device(queries, keys, values, doc_lengths):
    count = lax.axis_size("cp")
    first = (lax.axis_index("cp").astype(jnp.int32) * queries.shape[0]).reshape(1)
    lengths = doc_lengths.reshape(1, -1)
    evens = range(0, count, 2)

    def hop(array, pairs):
        return lax.ppermute(array, "cp", pairs)

    onward = [(i, i + 1) for i in range(count - 1)]
    one_k = hop(keys, onward)
    one_v = hop(values, onward)
    guests = hop(leading_rows(queries, SLOT), [(i, i - 2) for i in evens if i])
    acc, levels, starts, out, marks = own_stage(first, lengths, queries, keys, values)
    slot = back_stage(first, lengths, guests, keys, values)
    slot = hop(slot, [(i, i + 2) for i in evens if i + 2 < count])
    across = [(i, i + 1) for i in evens]
    two_k = hop(one_k, across)
    two_v = hop(one_v, across)
    out, acc, levels = next_stage(first, marks, queries, one_k, one_v, acc, levels, starts, out)
    out = last_stage(first, marks, queries, slot, two_k, two_v, acc, levels, starts, out)
    return out


def solution(mesh):
    return jax.shard_map(
        on_device,
        mesh=mesh,
        in_specs=(P(("grp", "cp"), None), P(("grp", "cp"), None), P(("grp", "cp"), None), P("grp")),
        out_specs=P(("grp", "cp"), None),
        check_vma=False,
    )
```

time: 71.7 us -> 69.3 us (0.967)
  Pallas kernels: 27.1 us -> 24.8 us
    pallas_call x1, Pallas kernels: 6.38 us -> 5.11 us  [last_stage(): pl.pallas_call(last_kernel, in_specs=[SMEM] * 2 + [WHOLE] * 7 + [ANY], ou...]
    pallas_call x1, Pallas kernels: 9.8 us -> 8.73 us  [next_stage(): pl.pallas_call(next_kernel, in_specs=[SMEM] * 2 + [WHOLE] * 6 + [ANY], ou...]
  transfers between devices with their start and end apart: 6 -> 6, of which waited for: 3 -> 3; matrix products, arithmetic and copies ran while one was open for 0% -> 0% of each run, Pallas kernels for 26% -> 25%
where the time goes in v8:
time: 69.3 us; the launch traced here: 69.1 us
  waiting for transfers between devices  27.6 us (40%)
  Pallas kernels  24.8 us (36%)
  starting transfers between devices  16.4 us (24%)
    ppermute x6, waiting for transfers between devices, hop(): return lax.ppermute(array, 'cp', pairs)  27.6 us
    ppermute x6, starting transfers between devices, hop(): return lax.ppermute(array, 'cp', pairs)  16.4 us
    pallas_call x1, Pallas kernels, next_stage(): pl.pallas_call(next_kernel, in_specs=[SMEM] * 2 + [WHOLE] * 6 + [ANY], ou...  8.73 us
    pallas_call x1, Pallas kernels, own_stage(): pl.pallas_call(own_kernel, grid=(rows // BQ,), in_specs=[SMEM, WHOLE, row...  6.82 us
    pallas_call x1, Pallas kernels, last_stage(): pl.pallas_call(last_kernel, in_specs=[SMEM] * 2 + [WHOLE] * 7 + [ANY], ou...  5.11 us
    pallas_call x1, Pallas kernels, leading_rows(): pl.pallas_call(copy_kernel, in_specs=[pl.BlockSpec(memory_space=pltpu.HBM...  2.35 us
    pallas_call x1, Pallas kernels, back_stage(): pl.pallas_call(back_kernel, grid=(SLOT // BQ,), in_specs=[SMEM, WHOLE, ro...  1.76 us
  transfers between devices with their start and end apart: 6, of which 3 were waited for; matrix products, arithmetic and copies ran while one was open for 0% of the time, Pallas kernels for 25%

profile of v8, /device:TPU:20, one launch (start us, length us, event | category | flops | bytes accessed | tf_op | source)
XLA Modules:
  0.0 69.1 jit_solution(11690687804974915272)
XLA Ops:
  0.0 0.0 copy-start.1
  0.0 0.0 copy-start.2
  0.0 0.0 copy-start.3
  0.0 2.4 %leading_rows.1 = bf16[256,2048]{1,0:T(8,128)(2,1)} custom-call(bf16[512,2048]{1,0:T(8,128)(2,1)} %q_ref.5), custom_call_target="tpu_custom_call" | custom-call | tf_op jit(solution)/shard_map/leading_rows/pallas_call | solution.py:353
  2.4 7.7 %collective-permute-start = (bf16[256,2048]{1,0:T(8,128)(2,1)}, bf16[256,2048]{1,0:T(8,128)(2,1)}, u32[]{:S(2)}, u32[]{:S(2)}) collective-permute-start(bf16[256,2048]{1,0:T(8,128)(2,1)} %leading_rows.1), channel_id=1, source_target_pairs={{2,0},{4,2},{6,4},{8,6},{10,8},{12,10},{14,12},{16,14},{18,16},{20... | collective-permute-start | bytes 3145736 | tf_op jit(solution)/shard_map/ppermute | solution.py:425
  10.1 0.0 copy-done.1
  10.1 1.9 %collective-permute-start.2 = (bf16[512,1024]{1,0:T(8,128)(2,1)S(1)}, bf16[512,1024]{1,0:T(8,128)(2,1)S(1)}, u32[]{:S(2)}, u32[]{:S(2)}) collective-permute-start(bf16[512,1024]{1,0:T(8,128)(2,1)S(1)} %copy-done.1), channel_id=1, source_target_pairs={{0,1},{1,2},{2,3},{3,4},{4,5},{5,6},{6,7},{7,8},{8,9},{9,10},{10,1... | collective-permute-start | bytes 3145736 | tf_op jit(solution)/shard_map/ppermute | solution.py:425
  12.1 0.0 copy-done.2
  12.1 1.9 %collective-permute-start.4 = (bf16[512,1024]{1,0:T(8,128)(2,1)S(1)}, bf16[512,1024]{1,0:T(8,128)(2,1)}, u32[]{:S(2)}, u32[]{:S(2)}) collective-permute-start(bf16[512,1024]{1,0:T(8,128)(2,1)S(1)} %copy-done.2), channel_id=1, source_target_pairs={{0,1},{1,2},{2,3},{3,4},{4,5},{5,6},{6,7},{7,8},{8,9},{9,10},{10,1... | collective-permute-start | bytes 3145736 | tf_op jit(solution)/shard_map/ppermute | solution.py:425
  14.0 8.7 %collective-permute-done.q_ref = bf16[256,2048]{1,0:T(8,128)(2,1)} collective-permute-done((bf16[256,2048]{1,0:T(8,128)(2,1)}, bf16[256,2048]{1,0:T(8,128)(2,1)}, u32[]{:S(2)}, u32[]{:S(2)}) %collective-permute-start) | collective-permute-done | bytes 1048608 | tf_op jit(solution)/shard_map/ppermute | solution.py:425
  22.7 0.0 copy-done.3
  22.7 0.0 copy-start
  22.7 1.8 %back_shard.1 = bf16[256,2176]{1,0:T(8,128)(2,1)S(1)} custom-call(s32[1]{0:T(128)} %bitcast.first_ref, s32[1,256]{1,0:T(1,128)S(1)} %bitcast.2, bf16[256,2048]{1,0:T(8,128)(2,1)} %collective-permute-done.q_ref, bf16[512,1024]{1,0:T(8,128)(2,1)S(1)} %copy-done.1, bf16[512,1024]{1,0:T(8,128)(2,1)S(1)} %copy-done.2), custom_call_target="tpu_custom_call" | custom-call | flops 1073741824 | bytes 4194304 | tf_op jit(solution)/shard_map/back_shard/pallas_call | solution.py:366
  24.5 1.9 %collective-permute-start.1 = (bf16[256,2176]{1,0:T(8,128)(2,1)S(1)}, bf16[256,2176]{1,0:T(8,128)(2,1)S(1)}, u32[]{:S(2)}, u32[]{:S(2)}) collective-permute-start(bf16[256,2176]{1,0:T(8,128)(2,1)S(1)} %back_shard.1), channel_id=1, source_target_pairs={{0,2},{2,4},{4,6},{6,8},{8,10},{10,12},{12,14},{14,16},{16,18},{18... | collective-permute-start | bytes 3342344 | tf_op jit(solution)/shard_map/ppermute | solution.py:425
  26.4 1.9 %collective-permute-done.2.k_ref = bf16[512,1024]{1,0:T(8,128)(2,1)S(1)} collective-permute-done((bf16[512,1024]{1,0:T(8,128)(2,1)S(1)}, bf16[512,1024]{1,0:T(8,128)(2,1)S(1)}, u32[]{:S(2)}, u32[]{:S(2)}) %collective-permute-start.2) | collective-permute-done | bytes 1048608 | tf_op jit(solution)/shard_map/ppermute | solution.py:425
  28.4 1.3 %collective-permute-start.3 = (bf16[512,1024]{1,0:T(8,128)(2,1)S(1)}, bf16[512,1024]{1,0:T(8,128)(2,1)S(1)}, u32[]{:S(2)}, u32[]{:S(2)}) collective-permute-start(bf16[512,1024]{1,0:T(8,128)(2,1)S(1)} %collective-permute-done.2.k_ref), channel_id=1, source_target_pairs={{0,1},{2,3},{4,5},{6,7},{8,9},{10,11},{12,13},{14,15},{16,17},{18,... | collective-permute-start | bytes 3145736 | tf_op jit(solution)/shard_map/ppermute | solution.py:425
  29.7 17.0 %collective-permute-done.4.v_ref = bf16[512,1024]{1,0:T(8,128)(2,1)} collective-permute-done((bf16[512,1024]{1,0:T(8,128)(2,1)S(1)}, bf16[512,1024]{1,0:T(8,128)(2,1)}, u32[]{:S(2)}, u32[]{:S(2)}) %collective-permute-start.4) | collective-permute-done | bytes 1048608 | tf_op jit(solution)/shard_map/ppermute | solution.py:425
  46.7 1.5 %collective-permute-start.5 = (bf16[512,1024]{1,0:T(8,128)(2,1)}, bf16[512,1024]{1,0:T(8,128)(2,1)S(1)}, u32[]{:S(2)}, u32[]{:S(2)}) collective-permute-start(bf16[512,1024]{1,0:T(8,128)(2,1)} %collective-permute-done.4.v_ref), channel_id=1, source_target_pairs={{0,1},{2,3},{4,5},{6,7},{8,9},{10,11},{12,13},{14,15},{16,17},{18,... | collective-permute-start | bytes 3145736 | tf_op jit(solution)/shard_map/ppermute | solution.py:425
  48.2 0.0 copy-done
  48.2 6.8 %own_shard.1 = (f32[512,2048]{1,0:T(8,128)S(1)}, f32[512,2048]{1,0:T(8,128)S(1)}, f32[512,128]{1,0:T(8,128)S(1)}, bf16[512,2048]{1,0:T(8,128)(2,1)}, f32[4]{0:T(128)S(1)}) custom-call(s32[1]{0:T(128)} %bitcast.first_ref, s32[1,256]{1,0:T(1,128)S(1)} %bitcast.3, bf16[512,2048]{1,0:T(8,128)(2,1)S(1)} %copy-done, bf16[512,1024]{1,0:T(8,128)(2,1)S(1)} %copy-done.1, ...), custom_call_target="tpu_custom_call" | custom-call | flops 2147483648 | bytes 8388608 | tf_op jit(solution)/shard_map/own_shard/pallas_call | solution.py:332
  55.0 8.7 %next_shard.1 = (bf16[512,2048]{1,0:T(8,128)(2,1)}, f32[512,2048]{1,0:T(8,128)S(1)}, f32[512,2048]{1,0:T(8,128)S(1)}) custom-call(s32[1]{0:T(128)} %bitcast.first_ref, f32[4]{0:T(128)S(1)} %get-tuple-element.13.mark_ref, bf16[512,2048]{1,0:T(8,128)(2,1)S(1)} %copy-done, ...), custom_call_target="tpu_custom_call", output_to_operand_aliasing={{0}: (8, {})} | custom-call | flops 2147483648 | bytes 8388608 | tf_op jit(solution)/shard_map/next_shard/pallas_call | solution.py:388
  63.8 0.0 collective-permute-done.3.k_ref
  63.8 0.0 collective-permute-done.5.v_ref
  63.8 0.0 collective-permute-done.1.slot_ref
  63.8 5.1 %last_shard.1 = bf16[512,2048]{1,0:T(8,128)(2,1)} custom-call(s32[1]{0:T(128)} %bitcast.first_ref, f32[4]{0:T(128)S(1)} %get-tuple-element.13.mark_ref, bf16[512,2048]{1,0:T(8,128)(2,1)S(1)} %copy-done, bf16[256,2176]{1,0:T(8,128)(2,1)S(1)} %collective-permute-done.1.slot_ref, ...), custom_call_target="tpu_custom_call", output_to_operand_aliasing={{}: (9, {})} | custom-call | flops 1073741824 | bytes 8388608 | tf_op jit(solution)/shard_map/last_shard/pallas_call | solution.py:404
Async XLA Ops:
  0.0 10.1 %copy-start.1 = (bf16[512,1024]{1,0:T(8,128)(2,1)S(1)}, bf16[512,1024]{1,0:T(8,128)(2,1)}, u32[]{:S(2)}) copy-start(bf16[512,1024]{1,0:T(8,128)(2,1)} %k_ref.3) | copy-start | bytes 3145732
  0.0 12.1 %copy-start.2 = (bf16[512,1024]{1,0:T(8,128)(2,1)S(1)}, bf16[512,1024]{1,0:T(8,128)(2,1)}, u32[]{:S(2)}) copy-start(bf16[512,1024]{1,0:T(8,128)(2,1)} %v_ref.3) | copy-start | bytes 3145732
  0.0 22.7 %copy-start.3 = (s32[256]{0:T(256)S(1)}, s32[256]{0:T(256)}, u32[]{:S(2)}) copy-start(s32[256]{0:T(256)} %param.7) | copy-start | bytes 3076
  2.4 20.4 %collective-permute-start = (bf16[256,2048]{1,0:T(8,128)(2,1)}, bf16[256,2048]{1,0:T(8,128)(2,1)}, u32[]{:S(2)}, u32[]{:S(2)}) collective-permute-start(bf16[256,2048]{1,0:T(8,128)(2,1)} %leading_rows.1), channel_id=1, source_target_pairs={{2,0},{4,2},{6,4},{8,6},{10,8},{12,10},{14,12},{16,14},{18,16},{20... | collective-permute-start | bytes 3145736 | tf_op jit(solution)/shard_map/ppermute | solution.py:425
  10.1 18.2 %collective-permute-start.2 = (bf16[512,1024]{1,0:T(8,128)(2,1)S(1)}, bf16[512,1024]{1,0:T(8,128)(2,1)S(1)}, u32[]{:S(2)}, u32[]{:S(2)}) collective-permute-start(bf16[512,1024]{1,0:T(8,128)(2,1)S(1)} %copy-done.1), channel_id=1, source_target_pairs={{0,1},{1,2},{2,3},{3,4},{4,5},{5,6},{6,7},{7,8},{8,9},{9,10},{10,1... | collective-permute-start | bytes 3145736 | tf_op jit(solution)/shard_map/ppermute | solution.py:425
  12.1 34.6 %collective-permute-start.4 = (bf16[512,1024]{1,0:T(8,128)(2,1)S(1)}, bf16[512,1024]{1,0:T(8,128)(2,1)}, u32[]{:S(2)}, u32[]{:S(2)}) collective-permute-start(bf16[512,1024]{1,0:T(8,128)(2,1)S(1)} %copy-done.2), channel_id=1, source_target_pairs={{0,1},{1,2},{2,3},{3,4},{4,5},{5,6},{6,7},{7,8},{8,9},{9,10},{10,1... | collective-permute-start | bytes 3145736 | tf_op jit(solution)/shard_map/ppermute | solution.py:425
  22.7 25.5 %copy-start = (bf16[512,2048]{1,0:T(8,128)(2,1)S(1)}, bf16[512,2048]{1,0:T(8,128)(2,1)}, u32[]{:S(2)}) copy-start(bf16[512,2048]{1,0:T(8,128)(2,1)} %q_ref.5) | copy-start | bytes 6291460
  24.5 39.3 %collective-permute-start.1 = (bf16[256,2176]{1,0:T(8,128)(2,1)S(1)}, bf16[256,2176]{1,0:T(8,128)(2,1)S(1)}, u32[]{:S(2)}, u32[]{:S(2)}) collective-permute-start(bf16[256,2176]{1,0:T(8,128)(2,1)S(1)} %back_shard.1), channel_id=1, source_target_pairs={{0,2},{2,4},{4,6},{6,8},{8,10},{10,12},{12,14},{14,16},{16,18},{18... | collective-permute-start | bytes 3342344 | tf_op jit(solution)/shard_map/ppermute | solution.py:425
  28.4 35.4 %collective-permute-start.3 = (bf16[512,1024]{1,0:T(8,128)(2,1)S(1)}, bf16[512,1024]{1,0:T(8,128)(2,1)S(1)}, u32[]{:S(2)}, u32[]{:S(2)}) collective-permute-start(bf16[512,1024]{1,0:T(8,128)(2,1)S(1)} %collective-permute-done.2.k_ref), channel_id=1, source_target_pairs={{0,1},{2,3},{4,5},{6,7},{8,9},{10,11},{12,13},{14,15},{16,17},{18,... | collective-permute-start | bytes 3145736 | tf_op jit(solution)/shard_map/ppermute | solution.py:425
  46.7 17.1 %collective-permute-start.5 = (bf16[512,1024]{1,0:T(8,128)(2,1)}, bf16[512,1024]{1,0:T(8,128)(2,1)S(1)}, u32[]{:S(2)}, u32[]{:S(2)}) collective-permute-start(bf16[512,1024]{1,0:T(8,128)(2,1)} %collective-permute-done.4.v_ref), channel_id=1, source_target_pairs={{0,1},{2,3},{4,5},{6,7},{8,9},{10,11},{12,13},{14,15},{16,17},{18,... | collective-permute-start | bytes 3145736 | tf_op jit(solution)/shard_map/ppermute | solution.py:425

commit v9 on v8

--- a/solution.py
+++ b/solution.py
@@ -140,7 +140,7 @@
         start = jnp.max(jnp.where(ends <= edge, ends, 0.0))
         right = jnp.min(jnp.where(ends > edge, ends, edge + edge)) - edge
         reached = start < here + keys
-        by_keys = right > SLOT
+        by_keys = here + keys - start <= SLOT
 
         @pl.when(reached & by_keys)
         def _():
@@ -165,8 +165,7 @@
 
         working = reached & jnp.logical_not(by_keys) & ((block * BQ).astype(jnp.float32) < right)
         length = here + keys - start
-        pl.when(working & (length <= 256))(functools.partial(over, 256))
-        pl.when(working & (length > 256) & (length <= 384))(functools.partial(over, 384))
+        pl.when(working & (length <= 384))(functools.partial(over, 384))
         pl.when(working & (length > 384))(functools.partial(over, keys))
 
 
@@ -243,7 +242,7 @@
     base = first - keys
     blocks = q_ref.shape[0] // BQ
     start = mark_ref[0]
-    by_keys = mark_ref[SLOT // BQ] < first
+    by_keys = base - start <= SLOT
     copy = writer(done_ref, out_ref, sem)
 
     def merge(block, ref_k, ref_v, at, count):

time: 69.3 us -> 69.4 us (level)
  no operation moved by 1% of the time
where the time goes in v9:
time: 69.4 us; the launch traced here: 69.1 us
  waiting for transfers between devices  27.7 us (40%)
  Pallas kernels  24.9 us (36%)
  starting transfers between devices  16.2 us (23%)
    ppermute x6, waiting for transfers between devices, hop(): return lax.ppermute(array, 'cp', pairs)  27.7 us
    ppermute x6, starting transfers between devices, hop(): return lax.ppermute(array, 'cp', pairs)  16.2 us
    pallas_call x1, Pallas kernels, next_stage(): pl.pallas_call(next_kernel, in_specs=[SMEM] * 2 + [WHOLE] * 6 + [ANY], ou...  8.73 us
    pallas_call x1, Pallas kernels, own_stage(): pl.pallas_call(own_kernel, grid=(rows // BQ,), in_specs=[SMEM, WHOLE, row...  6.82 us
    pallas_call x1, Pallas kernels, last_stage(): pl.pallas_call(last_kernel, in_specs=[SMEM] * 2 + [WHOLE] * 7 + [ANY], ou...  5.3 us
    pallas_call x1, Pallas kernels, leading_rows(): pl.pallas_call(copy_kernel, in_specs=[pl.BlockSpec(memory_space=pltpu.HBM...  2.35 us
    pallas_call x1, Pallas kernels, back_stage(): pl.pallas_call(back_kernel, grid=(SLOT // BQ,), in_specs=[SMEM, WHOLE, ro...  1.74 us
  transfers between devices with their start and end apart: 6, of which 3 were waited for; matrix products, arithmetic and copies ran while one was open for 0% of the time, Pallas kernels for 25%

profile of v9, /device:TPU:20, one launch (start us, length us, event | category | flops | bytes accessed | tf_op | source)
XLA Modules:
  0.0 69.1 jit_solution(129855028817074072)
XLA Ops:
  0.0 0.0 copy-start.1
  0.0 0.0 copy-start.2
  0.0 0.0 copy-start.3
  0.0 2.4 %leading_rows.1 = bf16[256,2048]{1,0:T(8,128)(2,1)} custom-call(bf16[512,2048]{1,0:T(8,128)(2,1)} %q_ref.5), custom_call_target="tpu_custom_call" | custom-call | tf_op jit(solution)/shard_map/leading_rows/pallas_call | solution.py:352
  2.4 7.7 %collective-permute-start = (bf16[256,2048]{1,0:T(8,128)(2,1)}, bf16[256,2048]{1,0:T(8,128)(2,1)}, u32[]{:S(2)}, u32[]{:S(2)}) collective-permute-start(bf16[256,2048]{1,0:T(8,128)(2,1)} %leading_rows.1), channel_id=1, source_target_pairs={{2,0},{4,2},{6,4},{8,6},{10,8},{12,10},{14,12},{16,14},{18,16},{20... | collective-permute-start | bytes 3145736 | tf_op jit(solution)/shard_map/ppermute | solution.py:424
  10.1 0.0 copy-done.1
  10.1 1.9 %collective-permute-start.2 = (bf16[512,1024]{1,0:T(8,128)(2,1)S(1)}, bf16[512,1024]{1,0:T(8,128)(2,1)S(1)}, u32[]{:S(2)}, u32[]{:S(2)}) collective-permute-start(bf16[512,1024]{1,0:T(8,128)(2,1)S(1)} %copy-done.1), channel_id=1, source_target_pairs={{0,1},{1,2},{2,3},{3,4},{4,5},{5,6},{6,7},{7,8},{8,9},{9,10},{10,1... | collective-permute-start | bytes 3145736 | tf_op jit(solution)/shard_map/ppermute | solution.py:424
  12.1 0.0 copy-done.2
  12.1 1.9 %collective-permute-start.4 = (bf16[512,1024]{1,0:T(8,128)(2,1)S(1)}, bf16[512,1024]{1,0:T(8,128)(2,1)}, u32[]{:S(2)}, u32[]{:S(2)}) collective-permute-start(bf16[512,1024]{1,0:T(8,128)(2,1)S(1)} %copy-done.2), channel_id=1, source_target_pairs={{0,1},{1,2},{2,3},{3,4},{4,5},{5,6},{6,7},{7,8},{8,9},{9,10},{10,1... | collective-permute-start | bytes 3145736 | tf_op jit(solution)/shard_map/ppermute | solution.py:424
  14.0 8.7 %collective-permute-done.q_ref = bf16[256,2048]{1,0:T(8,128)(2,1)} collective-permute-done((bf16[256,2048]{1,0:T(8,128)(2,1)}, bf16[256,2048]{1,0:T(8,128)(2,1)}, u32[]{:S(2)}, u32[]{:S(2)}) %collective-permute-start) | collective-permute-done | bytes 1048608 | tf_op jit(solution)/shard_map/ppermute | solution.py:424
  22.7 0.0 copy-done.3
  22.7 0.0 copy-start
  22.7 1.7 %back_shard.1 = bf16[256,2176]{1,0:T(8,128)(2,1)S(1)} custom-call(s32[1]{0:T(128)} %bitcast.first_ref, s32[1,256]{1,0:T(1,128)S(1)} %bitcast.2, bf16[256,2048]{1,0:T(8,128)(2,1)} %collective-permute-done.q_ref, bf16[512,1024]{1,0:T(8,128)(2,1)S(1)} %copy-done.1, bf16[512,1024]{1,0:T(8,128)(2,1)S(1)} %copy-done.2), custom_call_target="tpu_custom_call" | custom-call | flops 1073741824 | bytes 4194304 | tf_op jit(solution)/shard_map/back_shard/pallas_call | solution.py:365
  24.5 1.9 %collective-permute-start.1 = (bf16[256,2176]{1,0:T(8,128)(2,1)S(1)}, bf16[256,2176]{1,0:T(8,128)(2,1)S(1)}, u32[]{:S(2)}, u32[]{:S(2)}) collective-permute-start(bf16[256,2176]{1,0:T(8,128)(2,1)S(1)} %back_shard.1), channel_id=1, source_target_pairs={{0,2},{2,4},{4,6},{6,8},{8,10},{10,12},{12,14},{14,16},{16,18},{18... | collective-permute-start | bytes 3342344 | tf_op jit(solution)/shard_map/ppermute | solution.py:424
  26.4 1.9 %collective-permute-done.2.k_ref = bf16[512,1024]{1,0:T(8,128)(2,1)S(1)} collective-permute-done((bf16[512,1024]{1,0:T(8,128)(2,1)S(1)}, bf16[512,1024]{1,0:T(8,128)(2,1)S(1)}, u32[]{:S(2)}, u32[]{:S(2)}) %collective-permute-start.2) | collective-permute-done | bytes 1048608 | tf_op jit(solution)/shard_map/ppermute | solution.py:424
  28.4 1.3 %collective-permute-start.3 = (bf16[512,1024]{1,0:T(8,128)(2,1)S(1)}, bf16[512,1024]{1,0:T(8,128)(2,1)S(1)}, u32[]{:S(2)}, u32[]{:S(2)}) collective-permute-start(bf16[512,1024]{1,0:T(8,128)(2,1)S(1)} %collective-permute-done.2.k_ref), channel_id=1, source_target_pairs={{0,1},{2,3},{4,5},{6,7},{8,9},{10,11},{12,13},{14,15},{16,17},{18,... | collective-permute-start | bytes 3145736 | tf_op jit(solution)/shard_map/ppermute | solution.py:424
  29.7 17.0 %collective-permute-done.4.v_ref = bf16[512,1024]{1,0:T(8,128)(2,1)} collective-permute-done((bf16[512,1024]{1,0:T(8,128)(2,1)S(1)}, bf16[512,1024]{1,0:T(8,128)(2,1)}, u32[]{:S(2)}, u32[]{:S(2)}) %collective-permute-start.4) | collective-permute-done | bytes 1048608 | tf_op jit(solution)/shard_map/ppermute | solution.py:424
  46.7 1.3 %collective-permute-start.5 = (bf16[512,1024]{1,0:T(8,128)(2,1)}, bf16[512,1024]{1,0:T(8,128)(2,1)S(1)}, u32[]{:S(2)}, u32[]{:S(2)}) collective-permute-start(bf16[512,1024]{1,0:T(8,128)(2,1)} %collective-permute-done.4.v_ref), channel_id=1, source_target_pairs={{0,1},{2,3},{4,5},{6,7},{8,9},{10,11},{12,13},{14,15},{16,17},{18,... | collective-permute-start | bytes 3145736 | tf_op jit(solution)/shard_map/ppermute | solution.py:424
  48.0 0.0 copy-done
  48.1 6.8 %own_shard.1 = (f32[512,2048]{1,0:T(8,128)S(1)}, f32[512,2048]{1,0:T(8,128)S(1)}, f32[512,128]{1,0:T(8,128)S(1)}, bf16[512,2048]{1,0:T(8,128)(2,1)}, f32[4]{0:T(128)S(1)}) custom-call(s32[1]{0:T(128)} %bitcast.first_ref, s32[1,256]{1,0:T(1,128)S(1)} %bitcast.3, bf16[512,2048]{1,0:T(8,128)(2,1)S(1)} %copy-done, bf16[512,1024]{1,0:T(8,128)(2,1)S(1)} %copy-done.1, ...), custom_call_target="tpu_custom_call" | custom-call | flops 2147483648 | bytes 8388608 | tf_op jit(solution)/shard_map/own_shard/pallas_call | solution.py:331
  54.9 8.7 %next_shard.1 = (bf16[512,2048]{1,0:T(8,128)(2,1)}, f32[512,2048]{1,0:T(8,128)S(1)}, f32[512,2048]{1,0:T(8,128)S(1)}) custom-call(s32[1]{0:T(128)} %bitcast.first_ref, f32[4]{0:T(128)S(1)} %get-tuple-element.13.mark_ref, bf16[512,2048]{1,0:T(8,128)(2,1)S(1)} %copy-done, ...), custom_call_target="tpu_custom_call", output_to_operand_aliasing={{0}: (8, {})} | custom-call | flops 2147483648 | bytes 8388608 | tf_op jit(solution)/shard_map/next_shard/pallas_call | solution.py:387
  63.6 0.0 collective-permute-done.3.k_ref
  63.6 0.0 collective-permute-done.5.v_ref
  63.6 0.0 collective-permute-done.1.slot_ref
  63.7 5.3 %last_shard.1 = bf16[512,2048]{1,0:T(8,128)(2,1)} custom-call(s32[1]{0:T(128)} %bitcast.first_ref, f32[4]{0:T(128)S(1)} %get-tuple-element.13.mark_ref, bf16[512,2048]{1,0:T(8,128)(2,1)S(1)} %copy-done, bf16[256,2176]{1,0:T(8,128)(2,1)S(1)} %collective-permute-done.1.slot_ref, ...), custom_call_target="tpu_custom_call", output_to_operand_aliasing={{}: (9, {})} | custom-call | flops 1073741824 | bytes 8388608 | tf_op jit(solution)/shard_map/last_shard/pallas_call | solution.py:403
Async XLA Ops:
  0.0 10.1 %copy-start.1 = (bf16[512,1024]{1,0:T(8,128)(2,1)S(1)}, bf16[512,1024]{1,0:T(8,128)(2,1)}, u32[]{:S(2)}) copy-start(bf16[512,1024]{1,0:T(8,128)(2,1)} %k_ref.3) | copy-start | bytes 3145732
  0.0 12.1 %copy-start.2 = (bf16[512,1024]{1,0:T(8,128)(2,1)S(1)}, bf16[512,1024]{1,0:T(8,128)(2,1)}, u32[]{:S(2)}) copy-start(bf16[512,1024]{1,0:T(8,128)(2,1)} %v_ref.3) | copy-start | bytes 3145732
  0.0 22.7 %copy-start.3 = (s32[256]{0:T(256)S(1)}, s32[256]{0:T(256)}, u32[]{:S(2)}) copy-start(s32[256]{0:T(256)} %param.7) | copy-start | bytes 3076
  2.4 20.4 %collective-permute-start = (bf16[256,2048]{1,0:T(8,128)(2,1)}, bf16[256,2048]{1,0:T(8,128)(2,1)}, u32[]{:S(2)}, u32[]{:S(2)}) collective-permute-start(bf16[256,2048]{1,0:T(8,128)(2,1)} %leading_rows.1), channel_id=1, source_target_pairs={{2,0},{4,2},{6,4},{8,6},{10,8},{12,10},{14,12},{16,14},{18,16},{20... | collective-permute-start | bytes 3145736 | tf_op jit(solution)/shard_map/ppermute | solution.py:424
  10.1 18.2 %collective-permute-start.2 = (bf16[512,1024]{1,0:T(8,128)(2,1)S(1)}, bf16[512,1024]{1,0:T(8,128)(2,1)S(1)}, u32[]{:S(2)}, u32[]{:S(2)}) collective-permute-start(bf16[512,1024]{1,0:T(8,128)(2,1)S(1)} %copy-done.1), channel_id=1, source_target_pairs={{0,1},{1,2},{2,3},{3,4},{4,5},{5,6},{6,7},{7,8},{8,9},{9,10},{10,1... | collective-permute-start | bytes 3145736 | tf_op jit(solution)/shard_map/ppermute | solution.py:424
  12.1 34.6 %collective-permute-start.4 = (bf16[512,1024]{1,0:T(8,128)(2,1)S(1)}, bf16[512,1024]{1,0:T(8,128)(2,1)}, u32[]{:S(2)}, u32[]{:S(2)}) collective-permute-start(bf16[512,1024]{1,0:T(8,128)(2,1)S(1)} %copy-done.2), channel_id=1, source_target_pairs={{0,1},{1,2},{2,3},{3,4},{4,5},{5,6},{6,7},{7,8},{8,9},{9,10},{10,1... | collective-permute-start | bytes 3145736 | tf_op jit(solution)/shard_map/ppermute | solution.py:424
  22.7 25.3 %copy-start = (bf16[512,2048]{1,0:T(8,128)(2,1)S(1)}, bf16[512,2048]{1,0:T(8,128)(2,1)}, u32[]{:S(2)}) copy-start(bf16[512,2048]{1,0:T(8,128)(2,1)} %q_ref.5) | copy-start | bytes 6291460
  24.5 39.2 %collective-permute-start.1 = (bf16[256,2176]{1,0:T(8,128)(2,1)S(1)}, bf16[256,2176]{1,0:T(8,128)(2,1)S(1)}, u32[]{:S(2)}, u32[]{:S(2)}) collective-permute-start(bf16[256,2176]{1,0:T(8,128)(2,1)S(1)} %back_shard.1), channel_id=1, source_target_pairs={{0,2},{2,4},{4,6},{6,8},{8,10},{10,12},{12,14},{14,16},{16,18},{18... | collective-permute-start | bytes 3342344 | tf_op jit(solution)/shard_map/ppermute | solution.py:424
  28.4 35.3 %collective-permute-start.3 = (bf16[512,1024]{1,0:T(8,128)(2,1)S(1)}, bf16[512,1024]{1,0:T(8,128)(2,1)S(1)}, u32[]{:S(2)}, u32[]{:S(2)}) collective-permute-start(bf16[512,1024]{1,0:T(8,128)(2,1)S(1)} %collective-permute-done.2.k_ref), channel_id=1, source_target_pairs={{0,1},{2,3},{4,5},{6,7},{8,9},{10,11},{12,13},{14,15},{16,17},{18,... | collective-permute-start | bytes 3145736 | tf_op jit(solution)/shard_map/ppermute | solution.py:424
  46.7 16.9 %collective-permute-start.5 = (bf16[512,1024]{1,0:T(8,128)(2,1)}, bf16[512,1024]{1,0:T(8,128)(2,1)S(1)}, u32[]{:S(2)}, u32[]{:S(2)}) collective-permute-start(bf16[512,1024]{1,0:T(8,128)(2,1)} %collective-permute-done.4.v_ref), channel_id=1, source_target_pairs={{0,1},{2,3},{4,5},{6,7},{8,9},{10,11},{12,13},{14,15},{16,17},{18,... | collective-permute-start | bytes 3145736 | tf_op jit(solution)/shard_map/ppermute | solution.py:424
